TPU v7x, 32 devices: a whole 2x2x4 slice. The times are simulated.
32 devices in a mesh: dp: 2 (over core), seq: 16 (over z, y, x).
Axes of the slice: x: 2, y: 2, z: 4, core: 2. Of those that a mesh axis runs over, the one named last changes fastest.
Arguments:
- tokens: bfloat16 [16, 1024, 768], P('dp', 'seq'), may hold values from -6 to 6
- lengths: int32 [16], P('dp'), may hold values from 256 to 1024, as said below
- w_qkv: bfloat16 [768, 2304], P('seq', 'dp'), may hold values from -0.21875 to 0.21875
- w_out: bfloat16 [768, 768], P('seq', 'dp'), may hold values from -6 to 6
- w_gate: bfloat16 [768, 3072], P('seq', 'dp'), may hold values from -0.21875 to 0.21875
- w_up: bfloat16 [768, 3072], P('seq', 'dp'), may hold values from -0.21875 to 0.21875
- w_down: bfloat16 [3072, 768], P('seq', 'dp'), may hold values from -0.109375 to 0.109375
- ln_params: bfloat16 [4, 768], P(None, ('dp', 'seq')), may hold values from -2 to 2, as said below
- cotangent: bfloat16 [16, 1024, 768], P('dp', 'seq'), may hold values from -6 to 6
Outputs:
- output: bfloat16 [16, 1024, 768], P('dp', 'seq')
- grad_tokens: bfloat16 [16, 1024, 768], P('dp', 'seq')
- grad_w_qkv: float32 [768, 2304], P('seq', 'dp')
- grad_w_out: float32 [768, 768], P('seq', 'dp')
- grad_w_gate: float32 [768, 3072], P('seq', 'dp')
- grad_w_up: float32 [768, 3072], P('seq', 'dp')
- grad_w_down: float32 [3072, 768], P('seq', 'dp')
- grad_ln_params: float32 [4, 768], P(None, ('dp', 'seq'))
Inputs may be any that keep to these rules, and one draw needn't show every extreme that they name: Slot s holds valid tokens at positions below lengths[s]; in every draw one slot has 1024 and one 1024 / 4. `ln_params`: rows 0 and 2 are gains, rows 1 and 3 biases.
All inputs are finite; a program needn't handle non-finite values.
Results may differ from a plain program's by a relative error of at most 0.025.
Values may be sent and summed in bfloat16 or wider, within the bound.
A program may use at most 192 MiB of HBM per device.

v0:
```python
import jax
import jax.numpy as jnp
from jax import lax
from jax.sharding import PartitionSpec as P

HEADS = 12
HEAD_DIM = 64


norm_epsilon = 1e-12
score_scale = 0.125
masked_score = -1e30


def shifted(shard, axis, by):
    count = lax.axis_size(axis)
    return lax.ppermute(shard, axis, [(i, (i + by) % count) for i in range(count)])


def rotary_tables(positions):
    pair_index = jnp.arange(HEAD_DIM // 2, dtype=jnp.float32)
    inverse = jnp.power(jnp.float32(1000.0), -2.0 * pair_index / HEAD_DIM)
    angles = positions.astype(jnp.float32)[:, None] * inverse[None, :]
    cos_tab = jnp.concatenate([jnp.cos(angles), jnp.cos(angles)], axis=-1)
    sin_tab = jnp.concatenate([jnp.sin(angles), jnp.sin(angles)], axis=-1)
    return (cos_tab, sin_tab)


def rotate(values, cos_tab, sin_tab):
    half_dim = values.shape[-1] // 2
    turned = jnp.concatenate([-values[..., half_dim:], values[..., :half_dim]], axis=-1)
    return values * cos_tab + turned * sin_tab


def norm_parts(values, gain_vec, bias_vec):
    center = values - jnp.mean(values, axis=-1, keepdims=True)
    inv_std = lax.rsqrt(jnp.mean(center * center, axis=-1, keepdims=True) + norm_epsilon)
    normed = center * inv_std
    return (normed * gain_vec + bias_vec, normed, inv_std)


def norm_back(grad_in, normed, inv_std, gain_vec):
    scaled = grad_in * gain_vec
    return inv_std * (
        scaled
        - jnp.mean(scaled, axis=-1, keepdims=True)
        - normed * jnp.mean(scaled * normed, axis=-1, keepdims=True)
    )


def heads_view(flat_rows):
    return flat_rows.reshape(flat_rows.shape[0], flat_rows.shape[1], HEADS, HEAD_DIM)


def attend_block(run_state, queries, key_blk, value_blk, key_start, lengths):
    run_max, run_sum, run_acc = run_state
    scores = (
        jnp.einsum(
            "sqhd,skhd->shqk",
            heads_view(queries),
            heads_view(key_blk),
            preferred_element_type=jnp.float32,
        )
        * score_scale
    )
    key_pos = key_start + jnp.arange(key_blk.shape[1], dtype=jnp.int32)
    key_mask = (key_pos[None, :] < lengths[:, None])[:, None, None, :]
    scores = jnp.where(key_mask, scores, masked_score)
    new_max = jnp.maximum(run_max, jnp.max(scores, axis=-1))
    exp_scores = jnp.where(key_mask, jnp.exp(scores - new_max[..., None]), 0.0)
    factor = jnp.exp(run_max - new_max)
    run_sum = run_sum * factor + jnp.sum(exp_scores, axis=-1)
    run_acc = run_acc * factor[..., None] + jnp.einsum(
        "shqk,skhd->shqd",
        exp_scores.astype(jnp.bfloat16),
        heads_view(value_blk),
        preferred_element_type=jnp.float32,
    )
    return (new_max, run_sum, run_acc)


def block_grads(queries, grad_att, log_total, delta_rows, key_blk, value_blk, key_ok):
    query_h = heads_view(queries)
    grad_h = heads_view(grad_att)
    key_h = heads_view(key_blk)
    scores = (
        jnp.einsum("sqhd,skhd->shqk", query_h, key_h, preferred_element_type=jnp.float32)
        * score_scale
    )
    key_mask = key_ok[:, None, None, :]
    soft_probs = jnp.where(key_mask, jnp.exp(scores - log_total[..., None]), 0.0)
    grad_probs = jnp.einsum(
        "sqhd,skhd->shqk", grad_h, heads_view(value_blk), preferred_element_type=jnp.float32
    )
    grad_scores = (soft_probs * (grad_probs - delta_rows[..., None])).astype(jnp.bfloat16)
    part_q = (
        jnp.einsum("shqk,skhd->sqhd", grad_scores, key_h, preferred_element_type=jnp.float32)
        * score_scale
    )
    part_k = (
        jnp.einsum("shqk,sqhd->skhd", grad_scores, query_h, preferred_element_type=jnp.float32)
        * score_scale
    )
    part_v = jnp.einsum(
        "shqk,sqhd->skhd",
        soft_probs.astype(jnp.bfloat16),
        grad_h,
        preferred_element_type=jnp.float32,
    )
    shape_out = queries.shape
    return (part_q.reshape(shape_out), part_k.reshape(key_blk.shape), part_v.reshape(key_blk.shape))


def local(tokens, lengths, w_qkv, w_out, w_gate, w_up, w_down, ln_params, cotangent):
    slot_count, span_len, width = tokens.shape
    row_count = slot_count * span_len
    cycle_size = lax.axis_size("seq")
    my_index = lax.axis_index("seq")
    row_qkv, row_out, row_gate, row_up, row_down, row_norm = (
        lax.all_gather(w_qkv, "seq", axis=0, tiled=True),
        lax.all_gather(w_out, "seq", axis=0, tiled=True),
        lax.all_gather(w_gate, "seq", axis=0, tiled=True),
        lax.all_gather(w_up, "seq", axis=0, tiled=True),
        lax.all_gather(w_down, "seq", axis=0, tiled=True),
        lax.all_gather(ln_params, "seq", axis=1, tiled=True),
    )
    wide_qkv, wide_out, wide_gate, wide_up, wide_down, wide_norm = (
        lax.all_gather(row_qkv, "dp", axis=1, tiled=True),
        lax.all_gather(row_out, "dp", axis=1, tiled=True),
        lax.all_gather(row_gate, "dp", axis=1, tiled=True),
        lax.all_gather(row_up, "dp", axis=1, tiled=True),
        lax.all_gather(row_down, "dp", axis=1, tiled=True),
        lax.all_gather(row_norm, "dp", axis=1, tiled=True),
    )
    norm_full = wide_norm.astype(jnp.float32)
    flat_tokens = tokens.reshape(row_count, width)
    token_f32 = flat_tokens.astype(jnp.float32)
    positions = my_index * span_len + jnp.arange(span_len, dtype=jnp.int32)
    row_valid = (positions[None, :] < lengths[:, None]).astype(jnp.float32).reshape(row_count, 1)
    cos_tab, sin_tab = rotary_tables(positions)
    cos_four = cos_tab[None, :, None, :]
    sin_four = sin_tab[None, :, None, :]
    qkv_pre = jnp.dot(flat_tokens, wide_qkv, preferred_element_type=jnp.float32)
    split_qkv = qkv_pre.reshape(slot_count, span_len, 3, HEADS, HEAD_DIM)
    queries = (
        rotate(split_qkv[:, :, 0], cos_four, sin_four)
        .astype(jnp.bfloat16)
        .reshape(slot_count, span_len, width)
    )
    keys_rot = (
        rotate(split_qkv[:, :, 1], cos_four, sin_four)
        .astype(jnp.bfloat16)
        .reshape(slot_count, span_len, width)
    )
    values = split_qkv[:, :, 2].astype(jnp.bfloat16).reshape(slot_count, span_len, width)
    start_state = (
        jnp.full((slot_count, HEADS, span_len), masked_score, jnp.float32),
        jnp.zeros((slot_count, HEADS, span_len), jnp.float32),
        jnp.zeros((slot_count, HEADS, span_len, HEAD_DIM), jnp.float32),
    )
    key_piece = lax.all_gather(keys_rot, "seq", axis=1, tiled=True)
    value_piece = lax.all_gather(values, "seq", axis=1, tiled=True)
    block_count = key_piece.shape[1] // span_len

    def one_block(block_id, inner_state):
        offset = block_id * span_len
        key_blk = lax.dynamic_slice_in_dim(key_piece, offset, span_len, axis=1)
        value_blk = lax.dynamic_slice_in_dim(value_piece, offset, span_len, axis=1)
        return attend_block(inner_state, queries, key_blk, value_blk, offset, lengths)

    run_max, run_sum, run_acc = lax.fori_loop(0, block_count, one_block, start_state)
    attended = run_acc / run_sum[..., None]
    log_total = run_max + jnp.log(run_sum)
    attn_low = attended.transpose(0, 2, 1, 3).reshape(row_count, width).astype(jnp.bfloat16)
    branch = jnp.dot(attn_low, wide_out, preferred_element_type=jnp.float32)
    hidden, normed_one, inv_one = norm_parts(token_f32 + branch, norm_full[0], norm_full[1])
    hidden_low = hidden.astype(jnp.bfloat16)
    gate_pre = jnp.dot(hidden_low, wide_gate, preferred_element_type=jnp.float32)
    up_proj = jnp.dot(hidden_low, wide_up, preferred_element_type=jnp.float32)
    activated = jax.nn.silu(gate_pre)
    inner_low = (activated * up_proj).astype(jnp.bfloat16)
    branch_two = jnp.dot(inner_low, wide_down, preferred_element_type=jnp.float32)
    result, normed_two, inv_two = norm_parts(hidden + branch_two, norm_full[2], norm_full[3])
    output = (result * row_valid).astype(jnp.bfloat16).reshape(slot_count, span_len, width)
    back_qkv, back_out, back_gate, back_up, back_down, back_norm = (
        lax.all_gather(w_qkv, "seq", axis=0, tiled=True),
        lax.all_gather(w_out, "seq", axis=0, tiled=True),
        lax.all_gather(w_gate, "seq", axis=0, tiled=True),
        lax.all_gather(w_up, "seq", axis=0, tiled=True),
        lax.all_gather(w_down, "seq", axis=0, tiled=True),
        lax.all_gather(ln_params, "seq", axis=1, tiled=True),
    )
    wide_qkv, wide_out, wide_gate, wide_up, wide_down, wide_norm = (
        lax.all_gather(back_qkv, "dp", axis=1, tiled=True),
        lax.all_gather(back_out, "dp", axis=1, tiled=True),
        lax.all_gather(back_gate, "dp", axis=1, tiled=True),
        lax.all_gather(back_up, "dp", axis=1, tiled=True),
        lax.all_gather(back_down, "dp", axis=1, tiled=True),
        lax.all_gather(back_norm, "dp", axis=1, tiled=True),
    )
    norm_full = wide_norm.astype(jnp.float32)
    grad_out = cotangent.reshape(row_count, width).astype(jnp.float32) * row_valid
    gain_two_grad = jnp.sum(grad_out * normed_two, axis=0)
    bias_two_grad = jnp.sum(grad_out, axis=0)
    grad_res2 = norm_back(grad_out, normed_two, inv_two, norm_full[2])
    grad_branch2 = grad_res2.astype(jnp.bfloat16)
    grad_wdown = jnp.einsum(
        "rf,rd->fd", inner_low, grad_branch2, preferred_element_type=jnp.float32
    )
    grad_inner = jnp.einsum(
        "rd,fd->rf", grad_branch2, wide_down, preferred_element_type=jnp.float32
    )
    sigma = jax.nn.sigmoid(gate_pre)
    grad_gate = (grad_inner * up_proj * sigma * (1.0 + gate_pre * (1.0 - sigma))).astype(
        jnp.bfloat16
    )
    grad_up = (grad_inner * activated).astype(jnp.bfloat16)
    grad_wgate = jnp.einsum("rd,rf->df", hidden_low, grad_gate, preferred_element_type=jnp.float32)
    grad_wup = jnp.einsum("rd,rf->df", hidden_low, grad_up, preferred_element_type=jnp.float32)
    grad_hidden = (
        grad_res2
        + jnp.einsum("rf,df->rd", grad_gate, wide_gate, preferred_element_type=jnp.float32)
        + jnp.einsum("rf,df->rd", grad_up, wide_up, preferred_element_type=jnp.float32)
    )
    gain_one_grad = jnp.sum(grad_hidden * normed_one, axis=0)
    bias_one_grad = jnp.sum(grad_hidden, axis=0)
    grad_res1 = norm_back(grad_hidden, normed_one, inv_one, norm_full[0])
    grad_branch1 = grad_res1.astype(jnp.bfloat16)
    grad_wout = jnp.einsum("ri,rd->id", attn_low, grad_branch1, preferred_element_type=jnp.float32)
    grad_att = (
        jnp.einsum("rd,id->ri", grad_branch1, wide_out, preferred_element_type=jnp.float32)
        .astype(jnp.bfloat16)
        .reshape(slot_count, span_len, width)
    )
    zero_rows = jnp.zeros((slot_count, span_len, width), jnp.float32)
    delta_rows = jnp.einsum("sqhd,shqd->shq", heads_view(grad_att).astype(jnp.float32), attended)

    def key_turn(turn_id, run_state):
        key_cur, value_cur, grad_keys, grad_values, grad_query = run_state
        key_start = (my_index - turn_id) % cycle_size * span_len
        key_ok = (key_start + jnp.arange(span_len, dtype=jnp.int32))[None, :] < lengths[:, None]
        part_q, part_k, part_v = block_grads(
            queries, grad_att, log_total, delta_rows, key_cur, value_cur, key_ok
        )
        key_cur, value_cur = shifted((key_cur, value_cur), "seq", 1)
        grad_keys, grad_values = (
            shifted((grad_keys + part_k).astype(jnp.bfloat16), "seq", 1).astype(jnp.float32),
            shifted((grad_values + part_v).astype(jnp.bfloat16), "seq", 1).astype(jnp.float32),
        )
        return (key_cur, value_cur, grad_keys, grad_values, grad_query + part_q)

    key_cur, value_cur, grad_keys, grad_values, grad_query = lax.fori_loop(
        0, cycle_size - 1, key_turn, (keys_rot, values, zero_rows, zero_rows, zero_rows)
    )
    key_start = (my_index - (cycle_size - 1)) % cycle_size * span_len
    key_ok = (key_start + jnp.arange(span_len, dtype=jnp.int32))[None, :] < lengths[:, None]
    part_q, part_k, part_v = block_grads(
        queries, grad_att, log_total, delta_rows, key_cur, value_cur, key_ok
    )
    grad_query = grad_query + part_q
    grad_keys, grad_values = (
        shifted((grad_keys + part_k).astype(jnp.bfloat16), "seq", 1).astype(jnp.float32),
        shifted((grad_values + part_v).astype(jnp.bfloat16), "seq", 1).astype(jnp.float32),
    )
    query_back = rotate(heads_view(grad_query), cos_four, -sin_four)
    key_back = rotate(heads_view(grad_keys), cos_four, -sin_four)
    grad_qkv = jnp.stack([query_back, key_back, heads_view(grad_values)], axis=2)
    grad_qkv = grad_qkv.reshape(row_count, 3 * width).astype(jnp.bfloat16)
    grad_wqkv = jnp.einsum("rd,re->de", flat_tokens, grad_qkv, preferred_element_type=jnp.float32)
    grad_tokens = grad_res1 + jnp.einsum(
        "re,de->rd", grad_qkv, wide_qkv, preferred_element_type=jnp.float32
    )
    grad_tokens = grad_tokens.astype(jnp.bfloat16).reshape(slot_count, span_len, width)
    grad_norm = jnp.stack([gain_one_grad, bias_one_grad, gain_two_grad, bias_two_grad], axis=0)
    col_qkv, col_out, col_gate, col_up, col_down, col_norm = (
        lax.psum_scatter(
            grad_wqkv.astype(jnp.bfloat16), "dp", scatter_dimension=1, tiled=True
        ).astype(jnp.float32),
        lax.psum_scatter(
            grad_wout.astype(jnp.bfloat16), "dp", scatter_dimension=1, tiled=True
        ).astype(jnp.float32),
        lax.psum_scatter(
            grad_wgate.astype(jnp.bfloat16), "dp", scatter_dimension=1, tiled=True
        ).astype(jnp.float32),
        lax.psum_scatter(
            grad_wup.astype(jnp.bfloat16), "dp", scatter_dimension=1, tiled=True
        ).astype(jnp.float32),
        lax.psum_scatter(
            grad_wdown.astype(jnp.bfloat16), "dp", scatter_dimension=1, tiled=True
        ).astype(jnp.float32),
        lax.psum_scatter(
            grad_norm.astype(jnp.bfloat16), "dp", scatter_dimension=1, tiled=True
        ).astype(jnp.float32),
    )
    own_qkv, own_out, own_gate, own_up, own_down, own_norm = (
        lax.psum_scatter(
            col_qkv.astype(jnp.bfloat16), "seq", scatter_dimension=0, tiled=True
        ).astype(jnp.float32),
        lax.psum_scatter(
            col_out.astype(jnp.bfloat16), "seq", scatter_dimension=0, tiled=True
        ).astype(jnp.float32),
        lax.psum_scatter(
            col_gate.astype(jnp.bfloat16), "seq", scatter_dimension=0, tiled=True
        ).astype(jnp.float32),
        lax.psum_scatter(
            col_up.astype(jnp.bfloat16), "seq", scatter_dimension=0, tiled=True
        ).astype(jnp.float32),
        lax.psum_scatter(
            col_down.astype(jnp.bfloat16), "seq", scatter_dimension=0, tiled=True
        ).astype(jnp.float32),
        lax.psum_scatter(
            col_norm.astype(jnp.bfloat16), "seq", scatter_dimension=1, tiled=True
        ).astype(jnp.float32),
    )
    return (output, grad_tokens, own_qkv, own_out, own_gate, own_up, own_down, own_norm)


def solution(mesh):
    placed = (
        P("dp", "seq", None),
        P("dp"),
        P("seq", "dp"),
        P("seq", "dp"),
        P("seq", "dp"),
        P("seq", "dp"),
        P("seq", "dp"),
        P(None, ("dp", "seq")),
        P("dp", "seq", None),
    )
    return jax.shard_map(
        local,
        mesh=mesh,
        in_specs=placed,
        out_specs=(
            P("dp", "seq", None),
            P("dp", "seq", None),
            P("seq", "dp"),
            P("seq", "dp"),
            P("seq", "dp"),
            P("seq", "dp"),
            P("seq", "dp"),
            P(None, ("dp", "seq")),
        ),
        check_vma=False,
    )
```

profile of v0, /device:TPU:0, one launch (start us, length us, event | category | flops | bytes accessed | tf_op | source)
XLA Modules:
  0.0 3373.3 jit_solution(6626745041927650767)
XLA Ops:
  7.9 64.3 %all-gather.13.cloned.1.call-done = bf16[768,1152]{1,0:T(8,128)(2,1)} async-done(((bf16[48,1152]{1,0:T(8,128)(2,1)}), bf16[768,1152]{1,0:T(8,128)(2,1)}) %all-gather.13.cloned.1.call-update) | async-done | bytes 1769488 | tf_op jit(solution)/shard_map/all_gather | solution.py:120
  111.9 48.7 %all_gather.58 = bf16[768,384]{1,0:T(8,128)(2,1)} all-gather(bf16[48,384]{1,0:T(8,128)(2,1)S(1)} %copy-done.47), channel_id=1, replica_groups=mesh['dp'=2,'seq'=16] {'seq'}, dimensions={0}, use_global_device_ids=true | all-gather | bytes 626688 | tf_op jit(solution)/shard_map/all_gather | solution.py:121
  161.4 58.8 %all-gather.27.cloned.1.call-done = bf16[768,1536]{1,0:T(8,128)(2,1)} async-done(((bf16[48,1536]{1,0:T(8,128)(2,1)}), bf16[768,1536]{1,0:T(8,128)(2,1)}) %all-gather.27.cloned.1.call-update) | async-done | bytes 2359312 | tf_op jit(solution)/shard_map/all_gather | solution.py:123
  220.5 38.3 %all-gather = bf16[16,24,4]{1,2,0:T(4,128)(2,1)S(1)} all-gather(bf16[1,24,4]{1,2,0:T(4,128)(2,1)S(1)} %bitcast.189), channel_id=1, replica_groups=mesh['dp'=2,'seq'=16] {'seq'}, dimensions={0}, use_global_device_ids=true | all-gather | bytes 3264 | tf_op jit(solution)/shard_map/all_gather | solution.py:125
  262.5 21.0 all-gather.31.cloned.1.call-done
  288.5 147.3 %all-gather.17.cloned.1.call-done = bf16[8,1024,768]{2,1,0:T(8,128)(2,1)} async-done(((bf16[8,64,768]{2,1,0:T(8,128)(2,1)}), bf16[8,1024,768]{2,1,0:T(8,128)(2,1)}) %all-gather.17.cloned.1.call-update) | async-done | bytes 12582928 | tf_op jit(solution)/shard_map/all_gather | solution.py:161
  435.8 152.3 %all-gather.19.cloned.1.call-done = bf16[8,1024,768]{2,1,0:T(8,128)(2,1)} async-done(((bf16[8,64,768]{2,1,0:T(8,128)(2,1)}), bf16[8,1024,768]{2,1,0:T(8,128)(2,1)}) %all-gather.19.cloned.1.call-update) | async-done | bytes 12582928 | tf_op jit(solution)/shard_map/all_gather | solution.py:162
  588.2 287.8 %while.42 = (s32[]{:T(128)}, f32[8,12,64]{2,1,0:T(8,128)S(1)}, f32[8,12,64]{2,1,0:T(8,128)S(1)}, f32[8,12,64,64]{3,2,1,0:T(8,128)}, s32[8]{0:T(128)S(1)}, /*inde...) while((s32[]{:T(128)}, f32[8,12,64]{2,1,0:T(8,128)S(1)}, ...), condition=%wide.region_3.4_spmd.clone, body=%wide.region_0.3_spmd.clone.sunk | while | flops 106986048 | bytes 16911072 | solution.py:171
  941.7 1573.5 %while.43 = (s32[]{:T(128)}, bf16[8,64,768]{2,1,0:T(8,128)(2,1)}, bf16[8,64,768]{2,1,0:T(8,128)(2,1)}, f32[8,64,768]{2,1,0:T(8,128)}, f32[8,64,768]{2,1,0:T(8,12...) while((s32[]{:T(128)}, bf16[8,64,768]{2,1,0:T(8,128)(2,1)}, ...), condition=%wide.region_13.14_spmd.clone, body=%wide.region_12.13_spmd.clone.sunk | while | flops 260309568 | bytes 100739736 | solution.py:252
  1018.5 14.4 collective-permute-done
  1032.9 15.0 collective-permute-done.1
  1125.0 14.4 collective-permute-done
  1230.1 14.4 collective-permute-done
  1334.7 14.4 collective-permute-done
  1439.4 14.4 collective-permute-done
  1544.1 14.4 collective-permute-done
  1648.8 14.4 collective-permute-done
  1753.5 14.4 collective-permute-done
  1858.2 14.4 collective-permute-done
  1962.9 14.4 collective-permute-done
  2067.6 14.4 collective-permute-done
  2172.3 14.4 collective-permute-done
  2277.0 14.4 collective-permute-done
  2381.7 14.4 collective-permute-done
  2486.3 14.4 collective-permute-done
  2676.1 15.9 reduce-scatter.39.cloned.1.call-done
  2704.7 41.9 %all-reduce = bf16[4,384]{1,0:T(4,128)(2,1)S(1)} all-reduce(bf16[4,384]{1,0:T(4,128)(2,1)S(1)} %copy.185), channel_id=13, replica_groups=mesh['dp'=2,'seq'=16] {'seq'}, use_global_device_ids=true, to_apply=%region_29.30.clone | all-reduce | flops 1536 | bytes 6144
  2752.9 80.1 %reduce-scatter.23.cloned.1.call-done = bf16[48,384]{1,0:T(8,128)(2,1)} async-done(((bf16[768,384]{1,0:T(8,128)(2,1)}), bf16[48,384]{1,0:T(8,128)(2,1)}) %reduce-scatter.23.cloned.1.call-update) | async-done | bytes 36880 | tf_op jit(solution)/shard_map/reduce_scatter | solution.py:299
  2834.4 130.0 %reduce-scatter.35.cloned.1.call-done = bf16[48,1152]{1,0:T(8,128)(2,1)} async-done(((bf16[768,1152]{1,0:T(8,128)(2,1)}), bf16[48,1152]{1,0:T(8,128)(2,1)}) %reduce-scatter.35.cloned.1.call-update) | async-done | bytes 110608
  2966.4 131.2 %reduce-scatter.27.cloned.1.call-done = bf16[48,1536]{1,0:T(8,128)(2,1)} async-done(((bf16[768,1536]{1,0:T(8,128)(2,1)}), bf16[48,1536]{1,0:T(8,128)(2,1)}) %reduce-scatter.27.cloned.1.call-update) | async-done | bytes 147472 | tf_op jit(solution)/shard_map/reduce_scatter | solution.py:302
  3099.2 131.8 %reduce-scatter.31.cloned.1.call-done = bf16[48,1536]{1,0:T(8,128)(2,1)} async-done(((bf16[768,1536]{1,0:T(8,128)(2,1)}), bf16[48,1536]{1,0:T(8,128)(2,1)}) %reduce-scatter.31.cloned.1.call-update) | async-done | bytes 147472 | tf_op jit(solution)/shard_map/reduce_scatter | solution.py:305
  3232.6 131.9 %reduce-scatter.33.cloned.1.call-done = bf16[192,384]{1,0:T(8,128)(2,1)} async-done(((bf16[3072,384]{1,0:T(8,128)(2,1)}), bf16[192,384]{1,0:T(8,128)(2,1)}) %reduce-scatter.33.cloned.1.call-update) | async-done | bytes 147472 | tf_op jit(solution)/shard_map/reduce_scatter | solution.py:308
  (1120 shorter events, 1929.3 us)
Async XLA Ops:
  7.2 65.1 %all-gather.13.cloned.1.call-start = ((), (), s32[]{:S(2)}) async-start(), calls=%async_computation.11 | async-start | bytes 1880064 | tf_op jit(solution)/shard_map/all_gather | solution.py:120
  7.9 77.3 %all-gather.15.cloned.1.call-start = ((), (), s32[]{:S(2)}) async-start(), calls=%async_computation.12 | async-start | bytes 5308416 | tf_op jit(solution)/shard_map/all_gather | solution.py:128
  72.2 88.5 %all-gather.23.cloned.1.call-start = ((), (), s32[]{:S(2)}) async-start(), calls=%async_computation.16 | async-start | bytes 2506752 | tf_op jit(solution)/shard_map/all_gather | solution.py:122
  73.0 147.2 %all-gather.27.cloned.1.call-start = ((), (), s32[]{:S(2)}) async-start(), calls=%async_computation.18 | async-start | bytes 2506752 | tf_op jit(solution)/shard_map/all_gather | solution.py:123
  73.6 209.9 %all-gather.31.cloned.1.call-start = ((), (), s32[]{:S(2)}) async-start(), calls=%async_computation.20 | async-start | bytes 2506752 | tf_op jit(solution)/shard_map/all_gather | solution.py:124
  74.1 361.7 %all-gather.17.cloned.1.call-start = ((), (), s32[]{:S(2)}) async-start(), calls=%async_computation.13 | async-start | bytes 13369344 | tf_op jit(solution)/shard_map/all_gather | solution.py:161
  108.1 480.0 %all-gather.19.cloned.1.call-start = ((), (), s32[]{:S(2)}) async-start(), calls=%async_computation.14 | async-start | bytes 13369344 | tf_op jit(solution)/shard_map/all_gather | solution.py:162
  111.9 768.6 %all-gather.21.cloned.1.call-start = ((), (), s32[]{:S(2)}) async-start(), calls=%async_computation.15 | async-start | bytes 1769472 | tf_op jit(solution)/shard_map/all_gather | solution.py:129
  160.6 722.9 %all-gather.25.cloned.1.call-start = ((), (), s32[]{:S(2)}) async-start(), calls=%async_computation.17 | async-start | bytes 7077888 | tf_op jit(solution)/shard_map/all_gather | solution.py:130
  161.4 729.3 %all-gather.29.cloned.1.call-start = ((), (), s32[]{:S(2)}) async-start(), calls=%async_computation.19 | async-start | bytes 7077888 | tf_op jit(solution)/shard_map/all_gather | solution.py:131
  220.2 679.9 %all-gather.33.cloned.1.call-start = ((), (), s32[]{:S(2)}) async-start(), calls=%async_computation.21 | async-start | bytes 7077888 | tf_op jit(solution)/shard_map/all_gather | solution.py:132
  283.5 2378.4 %reduce-scatter.37.cloned.1.call-start = ((), (), s32[]{:S(2)}) async-start(), calls=%async_computation.30 | async-start | bytes 1769472
  1095.9 57.8 %collective-permute-start.1 = (bf16[8,64,768]{2,1,0:T(8,128)(2,1)}, bf16[8,64,768]{2,1,0:T(8,128)(2,1)}, u32[]{:S(2)}, u32[]{:S(2)}) collective-permute-start(bf16[8,64,768]{2,1,0:T(8,128)(2,1)} %copy.265), channel_id=1, source_target_pairs={{0,1},{1,2},{2,3},{3,4},{4,5},{5,6},{6,7},{7,8},{8,9},{9,10},{10,1... | collective-permute-start | bytes 2359304 | tf_op jit(solution)/shard_map/while/body/eval_jaxpr/ppermute | solution.py:17
  1201.2 57.3 %collective-permute-start.1 = (bf16[8,64,768]{2,1,0:T(8,128)(2,1)}, bf16[8,64,768]{2,1,0:T(8,128)(2,1)}, u32[]{:S(2)}, u32[]{:S(2)}) collective-permute-start(bf16[8,64,768]{2,1,0:T(8,128)(2,1)} %copy.265), channel_id=1, source_target_pairs={{0,1},{1,2},{2,3},{3,4},{4,5},{5,6},{6,7},{7,8},{8,9},{9,10},{10,1... | collective-permute-start | bytes 2359304 | tf_op jit(solution)/shard_map/while/body/eval_jaxpr/ppermute | solution.py:17
  1306.0 57.2 %collective-permute-start.1 = (bf16[8,64,768]{2,1,0:T(8,128)(2,1)}, bf16[8,64,768]{2,1,0:T(8,128)(2,1)}, u32[]{:S(2)}, u32[]{:S(2)}) collective-permute-start(bf16[8,64,768]{2,1,0:T(8,128)(2,1)} %copy.265), channel_id=1, source_target_pairs={{0,1},{1,2},{2,3},{3,4},{4,5},{5,6},{6,7},{7,8},{8,9},{9,10},{10,1... | collective-permute-start | bytes 2359304 | tf_op jit(solution)/shard_map/while/body/eval_jaxpr/ppermute | solution.py:17
  1410.7 57.2 %collective-permute-start.1 = (bf16[8,64,768]{2,1,0:T(8,128)(2,1)}, bf16[8,64,768]{2,1,0:T(8,128)(2,1)}, u32[]{:S(2)}, u32[]{:S(2)}) collective-permute-start(bf16[8,64,768]{2,1,0:T(8,128)(2,1)} %copy.265), channel_id=1, source_target_pairs={{0,1},{1,2},{2,3},{3,4},{4,5},{5,6},{6,7},{7,8},{8,9},{9,10},{10,1... | collective-permute-start | bytes 2359304 | tf_op jit(solution)/shard_map/while/body/eval_jaxpr/ppermute | solution.py:17
  1515.4 57.2 %collective-permute-start.1 = (bf16[8,64,768]{2,1,0:T(8,128)(2,1)}, bf16[8,64,768]{2,1,0:T(8,128)(2,1)}, u32[]{:S(2)}, u32[]{:S(2)}) collective-permute-start(bf16[8,64,768]{2,1,0:T(8,128)(2,1)} %copy.265), channel_id=1, source_target_pairs={{0,1},{1,2},{2,3},{3,4},{4,5},{5,6},{6,7},{7,8},{8,9},{9,10},{10,1... | collective-permute-start | bytes 2359304 | tf_op jit(solution)/shard_map/while/body/eval_jaxpr/ppermute | solution.py:17
  1620.1 57.2 %collective-permute-start.1 = (bf16[8,64,768]{2,1,0:T(8,128)(2,1)}, bf16[8,64,768]{2,1,0:T(8,128)(2,1)}, u32[]{:S(2)}, u32[]{:S(2)}) collective-permute-start(bf16[8,64,768]{2,1,0:T(8,128)(2,1)} %copy.265), channel_id=1, source_target_pairs={{0,1},{1,2},{2,3},{3,4},{4,5},{5,6},{6,7},{7,8},{8,9},{9,10},{10,1... | collective-permute-start | bytes 2359304 | tf_op jit(solution)/shard_map/while/body/eval_jaxpr/ppermute | solution.py:17
  1724.8 57.2 %collective-permute-start.1 = (bf16[8,64,768]{2,1,0:T(8,128)(2,1)}, bf16[8,64,768]{2,1,0:T(8,128)(2,1)}, u32[]{:S(2)}, u32[]{:S(2)}) collective-permute-start(bf16[8,64,768]{2,1,0:T(8,128)(2,1)} %copy.265), channel_id=1, source_target_pairs={{0,1},{1,2},{2,3},{3,4},{4,5},{5,6},{6,7},{7,8},{8,9},{9,10},{10,1... | collective-permute-start | bytes 2359304 | tf_op jit(solution)/shard_map/while/body/eval_jaxpr/ppermute | solution.py:17
  1829.5 57.2 %collective-permute-start.1 = (bf16[8,64,768]{2,1,0:T(8,128)(2,1)}, bf16[8,64,768]{2,1,0:T(8,128)(2,1)}, u32[]{:S(2)}, u32[]{:S(2)}) collective-permute-start(bf16[8,64,768]{2,1,0:T(8,128)(2,1)} %copy.265), channel_id=1, source_target_pairs={{0,1},{1,2},{2,3},{3,4},{4,5},{5,6},{6,7},{7,8},{8,9},{9,10},{10,1... | collective-permute-start | bytes 2359304 | tf_op jit(solution)/shard_map/while/body/eval_jaxpr/ppermute | solution.py:17
  1934.2 57.2 %collective-permute-start.1 = (bf16[8,64,768]{2,1,0:T(8,128)(2,1)}, bf16[8,64,768]{2,1,0:T(8,128)(2,1)}, u32[]{:S(2)}, u32[]{:S(2)}) collective-permute-start(bf16[8,64,768]{2,1,0:T(8,128)(2,1)} %copy.265), channel_id=1, source_target_pairs={{0,1},{1,2},{2,3},{3,4},{4,5},{5,6},{6,7},{7,8},{8,9},{9,10},{10,1... | collective-permute-start | bytes 2359304 | tf_op jit(solution)/shard_map/while/body/eval_jaxpr/ppermute | solution.py:17
  2038.9 57.2 %collective-permute-start.1 = (bf16[8,64,768]{2,1,0:T(8,128)(2,1)}, bf16[8,64,768]{2,1,0:T(8,128)(2,1)}, u32[]{:S(2)}, u32[]{:S(2)}) collective-permute-start(bf16[8,64,768]{2,1,0:T(8,128)(2,1)} %copy.265), channel_id=1, source_target_pairs={{0,1},{1,2},{2,3},{3,4},{4,5},{5,6},{6,7},{7,8},{8,9},{9,10},{10,1... | collective-permute-start | bytes 2359304 | tf_op jit(solution)/shard_map/while/body/eval_jaxpr/ppermute | solution.py:17
  2143.6 57.2 %collective-permute-start.1 = (bf16[8,64,768]{2,1,0:T(8,128)(2,1)}, bf16[8,64,768]{2,1,0:T(8,128)(2,1)}, u32[]{:S(2)}, u32[]{:S(2)}) collective-permute-start(bf16[8,64,768]{2,1,0:T(8,128)(2,1)} %copy.265), channel_id=1, source_target_pairs={{0,1},{1,2},{2,3},{3,4},{4,5},{5,6},{6,7},{7,8},{8,9},{9,10},{10,1... | collective-permute-start | bytes 2359304 | tf_op jit(solution)/shard_map/while/body/eval_jaxpr/ppermute | solution.py:17
  2248.2 57.2 %collective-permute-start.1 = (bf16[8,64,768]{2,1,0:T(8,128)(2,1)}, bf16[8,64,768]{2,1,0:T(8,128)(2,1)}, u32[]{:S(2)}, u32[]{:S(2)}) collective-permute-start(bf16[8,64,768]{2,1,0:T(8,128)(2,1)} %copy.265), channel_id=1, source_target_pairs={{0,1},{1,2},{2,3},{3,4},{4,5},{5,6},{6,7},{7,8},{8,9},{9,10},{10,1... | collective-permute-start | bytes 2359304 | tf_op jit(solution)/shard_map/while/body/eval_jaxpr/ppermute | solution.py:17
  2352.9 57.2 %collective-permute-start.1 = (bf16[8,64,768]{2,1,0:T(8,128)(2,1)}, bf16[8,64,768]{2,1,0:T(8,128)(2,1)}, u32[]{:S(2)}, u32[]{:S(2)}) collective-permute-start(bf16[8,64,768]{2,1,0:T(8,128)(2,1)} %copy.265), channel_id=1, source_target_pairs={{0,1},{1,2},{2,3},{3,4},{4,5},{5,6},{6,7},{7,8},{8,9},{9,10},{10,1... | collective-permute-start | bytes 2359304 | tf_op jit(solution)/shard_map/while/body/eval_jaxpr/ppermute | solution.py:17
  2457.6 57.2 %collective-permute-start.1 = (bf16[8,64,768]{2,1,0:T(8,128)(2,1)}, bf16[8,64,768]{2,1,0:T(8,128)(2,1)}, u32[]{:S(2)}, u32[]{:S(2)}) collective-permute-start(bf16[8,64,768]{2,1,0:T(8,128)(2,1)} %copy.265), channel_id=1, source_target_pairs={{0,1},{1,2},{2,3},{3,4},{4,5},{5,6},{6,7},{7,8},{8,9},{9,10},{10,1... | collective-permute-start | bytes 2359304 | tf_op jit(solution)/shard_map/while/body/eval_jaxpr/ppermute | solution.py:17
  2558.3 105.8 %reduce-scatter.21.cloned.1.call-start = ((), (), s32[]{:S(2)}) async-start(), calls=%async_computation.22 | async-start | bytes 5308416 | tf_op jit(solution)/shard_map/reduce_scatter | solution.py:276
  2661.8 171.2 %reduce-scatter.23.cloned.1.call-start = ((), (), s32[]{:S(2)}) async-start(), calls=%async_computation.23 | async-start | bytes 626688 | tf_op jit(solution)/shard_map/reduce_scatter | solution.py:299
  2664.0 300.3 %reduce-scatter.35.cloned.1.call-start = ((), (), s32[]{:S(2)}) async-start(), calls=%async_computation.29 | async-start | bytes 1880064
  2668.0 429.6 %reduce-scatter.27.cloned.1.call-start = ((), (), s32[]{:S(2)}) async-start(), calls=%async_computation.25 | async-start | bytes 2506752 | tf_op jit(solution)/shard_map/reduce_scatter | solution.py:302
  2668.6 562.4 %reduce-scatter.31.cloned.1.call-start = ((), (), s32[]{:S(2)}) async-start(), calls=%async_computation.27 | async-start | bytes 2506752 | tf_op jit(solution)/shard_map/reduce_scatter | solution.py:305
  2676.1 688.5 %reduce-scatter.33.cloned.1.call-start = ((), (), s32[]{:S(2)}) async-start(), calls=%async_computation.28 | async-start | bytes 2506752 | tf_op jit(solution)/shard_map/reduce_scatter | solution.py:308
  (199 other events, 2951.8 us)
Sparse Core Ops, SparseCore 0:
  10.8 61.4 all-gather.12
  73.8 11.3 all-gather.14
  88.0 66.7 all-gather.22
  157.5 62.6 all-gather.26
  222.8 60.6 all-gather.30
  286.0 149.7 all-gather.16
  438.5 149.6 all-gather.18
  589.7 7.3 all-gather.20
  598.7 15.6 all-gather.24
  615.7 15.6 all-gather.28
  632.9 15.4 all-gather.32
  2558.5 10.4 reduce-scatter.36
  2630.7 13.6 reduce-scatter.20
  2646.5 13.6 reduce-scatter.24
  2662.4 13.6 reduce-scatter.28
  2678.2 13.7 reduce-scatter.38
  2694.7 8.9 reduce-scatter.40
  2708.2 124.7 reduce-scatter.22
  2837.8 126.4 reduce-scatter.34
  2969.1 128.4 reduce-scatter.26
  3102.5 128.4 reduce-scatter.30
  3235.9 128.5 reduce-scatter.32
where the time goes:
time: 3390 us; the launch traced here: 3370 us
  waiting for transfers between devices  1690 us (50%)
  local copies, waits for them, and re-layouts  868 us (26%)
  matrix products  377 us (11%)
  other arithmetic  281 us (8%)
  blocking collectives  131 us (4%)
    ppermute x62, waiting for transfers between devices, shifted(): lax.ppermute(shard, axis, [(i, (i + by) % count) for i in range(count)])  599 us
    reshape x68, local copies, waits for them, and re-layouts, heads_view(): flat_rows.reshape(flat_rows.shape[0], flat_rows.shape[1], HEADS, HEAD_DIM)  227 us
    unnamed x26, waiting for transfers between devices  155 us
    all_gather x1, waiting for transfers between devices, local(): value_piece = lax.all_gather(values, 'seq', axis=1, tiled=True)  152 us
    all_gather x1, waiting for transfers between devices, local(): key_piece = lax.all_gather(keys_rot, 'seq', axis=1, tiled=True)  147 us
    reduce_scatter x1, waiting for transfers between devices, local(): lax.psum_scatter(col_down.astype(jnp.bfloat16), 'seq', scatter_dimension=...  132 us
    reduce_scatter x1, waiting for transfers between devices, local(): lax.psum_scatter(col_up.astype(jnp.bfloat16), 'seq', scatter_dimension=0,...  132 us
    reduce_scatter x1, waiting for transfers between devices, local(): lax.psum_scatter(col_gate.astype(jnp.bfloat16), 'seq', scatter_dimension=...  131 us
  transfers between devices with their start and end apart: 84, of which 59 were waited for; matrix products, arithmetic and copies ran while one was open for 28% of the time, Pallas kernels for 0%

commit v1 on v0

--- a/solution.py
+++ b/solution.py
@@ -1,6 +1,10 @@
+import functools
+
 import jax
 import jax.numpy as jnp
 from jax import lax
+from jax.experimental import pallas as pl
+from jax.experimental.pallas import tpu as pltpu
 from jax.sharding import PartitionSpec as P
 
 HEADS = 12
@@ -315,6 +319,761 @@
     return (output, grad_tokens, own_qkv, own_out, own_gate, own_up, own_down, own_norm)
 
 
+MESH = pl.DeviceIdType.MESH
+CHIPS, ZS = 16, 4
+OFFSETS = sorted(((dx, dy, dz) for dx in (0, 1) for dy in (0, 1) for dz in range(-3, 4)),
+                 key=lambda o: (o[0] + o[1], abs(o[2]), o))
+ORDERS = ("zxy", "zxy", "xzy", "yzx", "zyx", "zxy")
+
+
+def pick(index, values):
+    out = jnp.int32(0)
+    for place, value in enumerate(values):
+        if value:
+            out = out + jnp.where(index == place, jnp.int32(value), 0)
+    return out
+
+
+def place():
+    core, chip = lax.axis_index("dp"), lax.axis_index("seq")
+    return core, chip, chip % 2, (chip // 2) % 2, chip // 4
+
+
+def chip_at(x, y, z):
+    return (z * 2 + y) * 2 + x
+
+
+def meet_all(core, chip):
+    barrier = pltpu.get_barrier_semaphore()
+    me = core * CHIPS + chip
+
+    def greet(step, carry):
+        other = (me + step) % (2 * CHIPS)
+        pl.semaphore_signal(barrier, inc=1, device_id={"dp": other // CHIPS, "seq": other % CHIPS}, device_id_type=MESH)
+        return carry
+
+    lax.fori_loop(1, 2 * CHIPS, greet, 0)
+    pl.semaphore_wait(barrier, 2 * CHIPS - 1)
+
+
+def spread(order, dx, dy, dz):
+    zero = {"x": dx == 0, "y": dy == 0, "z": dz == 0}
+    flags = {}
+    for position, axis in enumerate(order):
+        flag = zero[axis] if axis != "z" else None
+        for later in order[position + 1:]:
+            flag = zero[later] if flag is None else flag & zero[later]
+        flags[axis] = flag
+    up, down = dz <= 0, dz >= 0
+    if flags["z"] is not None:
+        up, down = up & flags["z"], down & flags["z"]
+    return flags["x"], flags["y"], up, down
+
+
+def gather_kernel(tok, cot, *refs):
+    count = len(ORDERS)
+    shards, refs = refs[:count], refs[count:]
+    (x_all, c_own), refs = refs[:2], refs[2:]
+    wides, refs = refs[:count], refs[count:]
+    send_sem, recv_sem, sib_sem, tok_send, tok_recv, tok_sib, cot_recv, own_sem = refs
+    core, chip, x, y, z = place()
+    other = 1 - core
+    slots, span = tok.shape[0], tok.shape[1]
+    half = CHIPS // 2
+
+    def region(m, owner, source):
+        if m == count - 1:
+            return wides[m].at[owner * CHIPS + source]
+        rows, cols = shards[m].shape
+        return wides[m].at[owner, pl.ds(pl.multiple_of(source * rows, rows), rows)]
+
+    def piece(m, source, link, device, own=None):
+        target = region(m, core, source)
+        if link == 4:
+            recv = sib_sem.at[m, source]
+        else:
+            recv = recv_sem.at[m, source]
+        return pltpu.make_async_remote_copy(
+            src_ref=target if own is None else own, dst_ref=target, send_sem=send_sem.at[m, link, source],
+            recv_sem=recv, device_id=device, device_id_type=MESH)
+
+    neighbours = (
+        {"dp": core, "seq": chip_at(1 - x, y, z)},
+        {"dp": core, "seq": chip_at(x, 1 - y, z)},
+        {"dp": core, "seq": chip_at(x, y, jnp.minimum(z + 1, ZS - 1))},
+        {"dp": core, "seq": chip_at(x, y, jnp.maximum(z - 1, 0))},
+        {"dp": other, "seq": chip},
+    )
+
+    def goes(m, dx, dy, dz):
+        fx, fy, up, down = spread(ORDERS[m], dx, dy, dz)
+        return fx, fy, up & (z < ZS - 1), down & (z > 0), None
+
+    meet_all(core, chip)
+
+    def deliver(source, target, sends, recvs):
+        mine = (chip // half == core)
+
+        def one(j, carry):
+            slot = (chip + 1 + j) % half
+            to = core * half + slot
+            src, dst = source.at[slot], target
+            self_copy = mine & (to == chip)
+
+            @pl.when(self_copy)
+            def _():
+                pltpu.make_async_copy(src, dst, recvs.at[chip % half]).start()
+
+            @pl.when(jnp.logical_not(self_copy))
+            def _():
+                pltpu.make_async_remote_copy(
+                    src_ref=src, dst_ref=dst, send_sem=sends.at[slot], recv_sem=recvs.at[chip % half],
+                    device_id={"dp": chip // half, "seq": to}, device_id_type=MESH).start()
+            return carry
+
+        lax.fori_loop(0, slots, one, 0)
+
+    def rows_of(ref, index):
+        return ref.at[pl.ds(pl.multiple_of(index * span, span), span)]
+
+    deliver(tok, rows_of(x_all, chip), tok_send.at[0], tok_recv)
+    for m in range(count):
+        for link in range(5):
+            copy = piece(m, chip, link, neighbours[link], own=shards[m])
+            if link == 2:
+                pl.when(z < ZS - 1)(copy.start)
+            elif link == 3:
+                pl.when(z > 0)(copy.start)
+            else:
+                copy.start()
+        pltpu.make_async_copy(shards[m], region(m, core, chip), own_sem.at[m]).start()
+    deliver(cot, rows_of(c_own, chip % half), tok_send.at[1], cot_recv)
+
+    def step(index, carry):
+        dx = pick(index, [o[0] for o in OFFSETS])
+        dy = pick(index, [o[1] for o in OFFSETS])
+        dz = pick(index, [o[2] for o in OFFSETS])
+
+        @pl.when((z + dz >= 0) & (z + dz < ZS))
+        def _():
+            source = chip_at((x + dx) % 2, (y + dy) % 2, z + dz)
+            for m in range(count):
+                piece(m, source, 0, neighbours[0]).wait_recv()
+                flags = goes(m, dx, dy, dz)
+                for link in range(5):
+                    copy = piece(m, source, link, neighbours[link])
+                    if flags[link] is None:
+                        copy.start()
+                    else:
+                        pl.when(flags[link])(copy.start)
+        return carry
+
+    lax.fori_loop(1, 5, step, 0)
+
+    def relay(i, carry):
+        source = core * half + i
+        block = rows_of(x_all, source)
+        pltpu.make_async_copy(block, block, tok_recv.at[i]).wait()
+        pltpu.make_async_remote_copy(
+            src_ref=block, dst_ref=block, send_sem=tok_send.at[2, i], recv_sem=tok_sib.at[i],
+            device_id=neighbours[4], device_id_type=MESH).start()
+        return carry
+
+    lax.fori_loop(0, half, relay, 0)
+    lax.fori_loop(5, len(OFFSETS), step, 0)
+
+    def ends(i, carry):
+        block = rows_of(c_own, i)
+        pltpu.make_async_copy(block, block, cot_recv.at[i]).wait()
+        block = rows_of(x_all, other * half + i)
+        pltpu.make_async_copy(block, block, tok_sib.at[i]).wait()
+        block = rows_of(x_all, core * half + i)
+        pltpu.make_async_copy(block, block, tok_send.at[2, i]).wait()
+        slot = i
+        self_copy = (chip // half == core) & (core * half + slot == chip)
+
+        @pl.when(jnp.logical_not(self_copy))
+        def _():
+            pltpu.make_async_copy(tok.at[slot], tok.at[slot], tok_send.at[0, slot]).wait()
+            pltpu.make_async_copy(cot.at[slot], cot.at[slot], tok_send.at[1, slot]).wait()
+        return carry
+
+    lax.fori_loop(0, half, ends, 0)
+
+    def last(source, carry):
+        dx, dy = (source % 2 - x) % 2, ((source // 2) % 2 - y) % 2
+        dz = source // 4 - z
+        for m in range(count):
+            block = region(m, other, source)
+            pltpu.make_async_copy(block, block, sib_sem.at[m, source]).wait()
+            block = region(m, core, source)
+            flags = goes(m, dx, dy, dz)
+            for link in range(5):
+                sent = pltpu.make_async_copy(block, block, send_sem.at[m, link, source])
+                if flags[link] is None:
+                    sent.wait()
+                else:
+                    pl.when(flags[link])(sent.wait)
+        return carry
+
+    lax.fori_loop(0, CHIPS, last, 0)
+    for m in range(count):
+        pltpu.make_async_copy(shards[m], region(m, core, chip), own_sem.at[m]).wait()
+
+
+def gather(tokens, cotangent, shards):
+    count = len(shards)
+    slots, span, width = tokens.shape
+    low = jnp.bfloat16
+    outs = [jax.ShapeDtypeStruct((span * CHIPS, width), low), jax.ShapeDtypeStruct((span * CHIPS // 2, width), low)]
+    for m, shard in enumerate(shards):
+        if m == count - 1:
+            outs.append(jax.ShapeDtypeStruct((2 * CHIPS,) + shard.shape, shard.dtype))
+        else:
+            outs.append(jax.ShapeDtypeStruct((2, shard.shape[0] * CHIPS, shard.shape[1]), shard.dtype))
+    dma = pltpu.SemaphoreType.DMA
+    anywhere = pl.BlockSpec(memory_space=pl.ANY)
+    return pl.pallas_call(
+        gather_kernel,
+        out_shape=outs,
+        in_specs=[anywhere] * (2 + count),
+        out_specs=[anywhere] * len(outs),
+        scratch_shapes=[dma((count, 5, CHIPS)), dma((count, CHIPS)), dma((count, CHIPS)), dma((3, 8)), dma((8,)), dma((8,)), dma((8,)), dma((count,))],
+        compiler_params=pltpu.CompilerParams(collective_id=0, has_side_effects=True),
+        name="gather",
+    )(tokens, cotangent, *shards)
+
+
+SIDES = {"x": 2, "y": 2, "z": ZS}
+
+
+def slots_of(order):
+    sizes = {}
+    room = 1
+    for axis in order:
+        sizes[axis] = room * (ZS if axis == "z" else 1)
+        room *= SIDES[axis]
+    return sizes["x"], sizes["y"], sizes["z"], sizes["z"]
+
+
+def slot_index(order, link, x, y, z):
+    axis = "xyzz"[link]
+    index = 0
+    for before in order:
+        if before == axis:
+            break
+        index = index * SIDES[before] + {"x": x, "y": y, "z": z}[before]
+    if axis == "z":
+        index = index * ZS + z
+    return index
+
+
+def scatter_kernel(y_own, gt_own, gt_other, *refs):
+    count = len(ORDERS)
+    grads, refs = refs[:count], refs[count:]
+    (y_out, gt_out), refs = refs[:2], refs[2:]
+    finals, refs = refs[:count], refs[count:]
+    accs, refs = refs[:count], refs[count:]
+    sibs, refs = refs[:count], refs[count:]
+    lands, refs = refs[:4 * count], refs[4 * count:]
+    tmps, refs = refs[:count], refs[count:]
+    gt_mine, gt_sib, gt_low, refs = refs[0], refs[1], refs[2], refs[3:]
+    send_sem, recv_sem, sib_send, sib_recv, own_sem, gt_sem, tok_send, y_recv, gt_recv = refs
+    core, chip, x, y, z = place()
+    other = 1 - core
+    half = CHIPS // 2
+    span = y_out.shape[1]
+    rows_of = [tmp.shape[0] for tmp in tmps]
+
+    neighbours = (
+        {"dp": core, "seq": chip_at(1 - x, y, z)},
+        {"dp": core, "seq": chip_at(x, 1 - y, z)},
+        {"dp": core, "seq": chip_at(x, y, jnp.minimum(z + 1, ZS - 1))},
+        {"dp": core, "seq": chip_at(x, y, jnp.maximum(z - 1, 0))},
+    )
+    sibling = {"dp": other, "seq": chip}
+
+    def block(ref, m, dest):
+        if m == count - 1:
+            return ref.at[dest]
+        return ref.at[pl.ds(pl.multiple_of(dest * rows_of[m], rows_of[m]), rows_of[m])]
+
+    def to_sibling(m, dest):
+        source = grads[m].at[other * CHIPS + dest] if m == count - 1 else block(grads[m].at[other], m, dest)
+        return pltpu.make_async_remote_copy(
+            src_ref=source, dst_ref=block(sibs[m], m, dest), send_sem=sib_send.at[m, dest], recv_sem=sib_recv.at[m, dest],
+            device_id=sibling, device_id_type=MESH)
+
+    def own_load(m, dest):
+        source = grads[m].at[core * CHIPS + dest] if m == count - 1 else block(grads[m].at[core], m, dest)
+        return pltpu.make_async_copy(source, block(accs[m], m, dest), own_sem.at[m, dest])
+
+    meet_all(core, chip)
+
+    mine = pltpu.make_async_copy(gt_own, gt_mine, gt_sem.at[0])
+    mine.start()
+    cross = pltpu.make_async_remote_copy(src_ref=gt_other, dst_ref=gt_sib, send_sem=gt_sem.at[1], recv_sem=gt_sem.at[2],
+                                         device_id=sibling, device_id_type=MESH)
+    cross.start()
+
+    def dest_of(index):
+        dx = pick(index, [o[0] for o in OFFSETS[::-1]])
+        dy = pick(index, [o[1] for o in OFFSETS[::-1]])
+        dz = pick(index, [o[2] for o in OFFSETS[::-1]])
+        return dx, dy, dz, (z + dz >= 0) & (z + dz < ZS), (x + dx) % 2, (y + dy) % 2, jnp.clip(z + dz, 0, ZS - 1)
+
+    def begin(index, carry):
+        dx, dy, dz, valid, tx, ty, tz = dest_of(index)
+
+        @pl.when(valid)
+        def _():
+            dest = chip_at(tx, ty, tz)
+            for m in range(count):
+                to_sibling(m, dest).start()
+                own_load(m, dest).start()
+        return carry
+
+    lax.fori_loop(0, len(OFFSETS), begin, 0)
+
+    def deliver(source, target, k, recvs):
+        def one(j, carry):
+            i = (chip + 1 + j) % half
+            to_core, to_chip = chip // half, core * half + i
+            src = source.at[pl.ds(pl.multiple_of(i * span, span), span)]
+            dst = target.at[chip % half]
+            self_copy = (to_core == core) & (to_chip == chip)
+
+            @pl.when(self_copy)
+            def _():
+                pltpu.make_async_copy(src, dst, recvs.at[chip % half]).start()
+
+            @pl.when(jnp.logical_not(self_copy))
+            def _():
+                pltpu.make_async_remote_copy(
+                    src_ref=src, dst_ref=dst, send_sem=tok_send.at[k, i], recv_sem=recvs.at[chip % half],
+                    device_id={"dp": to_core, "seq": to_chip}, device_id_type=MESH).start()
+            return carry
+
+        lax.fori_loop(0, half, one, 0)
+
+    deliver(y_own, y_out, 0, y_recv)
+    mine.wait()
+    cross.wait()
+    gt_low[...] = (gt_mine[...] + gt_sib[...].astype(jnp.float32)).astype(jnp.bfloat16)
+    deliver(gt_low, gt_out, 1, gt_recv)
+
+    def step(index, carry):
+        dx, dy, dz, valid, tx, ty, tz = dest_of(index)
+
+        @pl.when(valid)
+        def _():
+            dest = chip_at(tx, ty, tz)
+            for m in range(count):
+                order = ORDERS[m]
+                fx, fy, up, down = spread(order, dx, dy, dz)
+                flags = (fx, fy, up & (z < ZS - 1), down & (z > 0))
+                own_load(m, dest).wait()
+                to_sibling(m, dest).wait_recv()
+                tmp, acc = tmps[m], block(accs[m], m, dest)
+                tmp[...] = acc[...].astype(jnp.float32) + block(sibs[m], m, dest)[...].astype(jnp.float32)
+                for link in range(4):
+                    land = lands[4 * m + link].at[slot_index(order, link, tx, ty, tz)]
+
+                    @pl.when(flags[link])
+                    def _():
+                        pltpu.make_async_copy(land, land, recv_sem.at[m, link, dest]).wait()
+                        tmp[...] += land[...].astype(jnp.float32)
+                away = {"x": dx != 0, "y": dy != 0, "z": dz != 0}
+                taken = None
+                last = (index == len(OFFSETS) - 1)
+
+                @pl.when(jnp.logical_not(last))
+                def _():
+                    acc[...] = tmp[...].astype(acc.dtype)
+
+                for axis in order[::-1]:
+                    here = away[axis] if taken is None else away[axis] & jnp.logical_not(taken)
+                    taken = away[axis] if taken is None else taken | away[axis]
+                    for link in {"x": (0,), "y": (1,), "z": (2, 3)}[axis]:
+                        go = here if axis != "z" else (here & (dz > 0 if link == 2 else dz < 0))
+                        there = {0: 0, 1: 1, 2: 3, 3: 2}[link]
+
+                        @pl.when(go)
+                        def _():
+                            pltpu.make_async_remote_copy(
+                                src_ref=acc, dst_ref=lands[4 * m + there].at[slot_index(order, there, tx, ty, tz)],
+                                send_sem=send_sem.at[m, dest], recv_sem=recv_sem.at[m, there, dest],
+                                device_id=neighbours[link], device_id_type=MESH).start()
+
+                @pl.when(last)
+                def _():
+                    finals[m][...] = tmp[...]
+        return carry
+
+    lax.fori_loop(0, len(OFFSETS), step, 0)
+
+    def ends(i, carry):
+        for out, recvs, k in ((y_out, y_recv, 0), (gt_out, gt_recv, 1)):
+            pltpu.make_async_copy(out.at[i], out.at[i], recvs.at[i]).wait()
+            self_copy = (chip // half == core) & (core * half + i == chip)
+
+            @pl.when(jnp.logical_not(self_copy))
+            def _():
+                pltpu.make_async_copy(out.at[i], out.at[i], tok_send.at[k, i]).wait()
+        return carry
+
+    lax.fori_loop(0, half, ends, 0)
+
+    def last(dest, carry):
+        for m in range(count):
+            to_sibling(m, dest).wait_send()
+
+            @pl.when(dest != chip)
+            def _():
+                part = block(accs[m], m, dest)
+                pltpu.make_async_copy(part, part, send_sem.at[m, dest]).wait()
+        return carry
+
+    lax.fori_loop(0, CHIPS, last, 0)
+
+
+def scatter(y_own, gt_own, gt_other, grads):
+    count = len(grads)
+    half_rows, width = y_own.shape
+    span = half_rows // 8
+    anywhere, vmem = pl.BlockSpec(memory_space=pl.ANY), pl.BlockSpec(memory_space=pltpu.VMEM)
+    finals, accs, sibs, lands, tmps = [], [], [], [], []
+    for m, grad in enumerate(grads):
+        if m == count - 1:
+            piece, whole = grad.shape[1:], (CHIPS,) + grad.shape[1:]
+        else:
+            piece, whole = (grad.shape[1] // CHIPS, grad.shape[2]), grad.shape[1:]
+        finals.append(jax.ShapeDtypeStruct(piece, jnp.float32))
+        accs.append(pltpu.VMEM(whole, grad.dtype))
+        sibs.append(pltpu.VMEM(whole, grad.dtype))
+        lands += [pltpu.VMEM((n,) + piece, grad.dtype) for n in slots_of(ORDERS[m])]
+        tmps.append(pltpu.VMEM(piece, jnp.float32))
+    dma = pltpu.SemaphoreType.DMA
+    out8 = jax.ShapeDtypeStruct((8, span, width), jnp.bfloat16)
+    return pl.pallas_call(
+        scatter_kernel,
+        out_shape=[out8, out8] + finals,
+        in_specs=[anywhere] * (3 + count),
+        out_specs=[anywhere] * 2 + [vmem] * count,
+        scratch_shapes=accs + sibs + lands + tmps + [
+            pltpu.VMEM((half_rows, width), jnp.float32), pltpu.VMEM((half_rows, width), jnp.bfloat16), pltpu.VMEM((half_rows, width), jnp.bfloat16),
+            dma((count, CHIPS)), dma((count, 4, CHIPS)), dma((count, CHIPS)), dma((count, CHIPS)), dma((count, CHIPS)), dma((3,)), dma((2, 8)), dma((8,)), dma((8,))],
+        compiler_params=pltpu.CompilerParams(collective_id=1, has_side_effects=True, vmem_limit_bytes=60 << 20),
+        name="scatter",
+    )(y_own, gt_own, gt_other, *grads)
+
+
+LOW, F32 = jnp.bfloat16, jnp.float32
+EPS = 1e-12
+HEAD = 64
+LANES = 128
+GROUP = 256
+FULL = pl.BlockSpec(memory_space=pltpu.VMEM)
+
+
+def nn(a, b):
+    return jnp.dot(a, b, preferred_element_type=F32)
+
+
+def nt(a, b):
+    return lax.dot_general(a, b, (((1,), (1,)), ((), ())), preferred_element_type=F32)
+
+
+def tn(a, b):
+    return lax.dot_general(a, b, (((0,), (0,)), ((), ())), preferred_element_type=F32)
+
+
+def lane_of(shape):
+    return lax.broadcasted_iota(jnp.int32, shape, 1)
+
+
+def turn(u):
+    parts = []
+    for start in range(0, u.shape[1], LANES):
+        part = u[:, start:start + LANES]
+        first = lane_of(part.shape) % HEAD < HEAD // 2
+        parts.append(jnp.where(first, pltpu.roll(part, LANES - HEAD // 2, 1), pltpu.roll(part, HEAD // 2, 1)))
+    return jnp.concatenate(parts, 1)
+
+
+def weight_block(w_ref, block):
+    per = w_ref.shape[2] // LANES
+    cols = [w_ref[b // per, :, pl.ds(pl.multiple_of(b % per * LANES, LANES), LANES)] for b in (block, block + 1)]
+    return jnp.concatenate(cols, 1)
+
+
+def attend_kernel(x_ref, w_ref, cos_ref, sin_ref, bias_ref, q_ref, k_ref, v_ref, att_ref):
+    group = pl.program_id(0)
+    rows = q_ref.shape[0]
+    mine = pl.ds(pl.multiple_of(lax.axis_index("dp") * rows, rows), rows)
+    blocks = x_ref.shape[1] // LANES
+
+    def turned(u, cos, sin):
+        return u * cos + turn(u) * sin
+
+    q = turned(nn(x_ref[mine, :], weight_block(w_ref, 2 * group)), cos_ref[mine, :], sin_ref[mine, :]).astype(LOW)
+    q_ref[...] = q * jnp.asarray(0.125, LOW)
+    k_ref[...] = turned(nn(x_ref[...], weight_block(w_ref, blocks + 2 * group)), cos_ref[...], sin_ref[...]).astype(LOW)
+    v_ref[...] = nn(x_ref[...], weight_block(w_ref, 2 * blocks + 2 * group)).astype(LOW)
+    step = 256
+    bias = bias_ref[0:1, :]
+    for pair in range(GROUP // LANES):
+        lanes = slice(pair * LANES, pair * LANES + LANES)
+        for start in range(0, rows, step):
+            qp = q_ref[start:start + step, lanes]
+            low = lane_of(qp.shape) < HEAD
+            outs = []
+            for head in range(2):
+                qm = jnp.where(low if head == 0 else jnp.logical_not(low), qp, jnp.zeros_like(qp))
+                s = nt(qm, k_ref[:, lanes]) + bias
+                p = jnp.exp(s - jnp.max(s, axis=1, keepdims=True))
+                total = jnp.sum(p, axis=1, keepdims=True)
+                outs.append(nn(p.astype(LOW), v_ref[:, lanes]) / total)
+            att_ref[start:start + step, lanes] = jnp.where(low, outs[0], outs[1]).astype(LOW)
+
+
+def attend(x, w, cos, sin, bias):
+    tokens, width = x.shape
+    rows = tokens // 2
+    shapes = [jax.ShapeDtypeStruct((n, width), LOW) for n in (rows, tokens, tokens, rows)]
+    return pl.pallas_call(
+        attend_kernel, grid=(width // GROUP,), out_shape=shapes,
+        in_specs=[FULL] * 5,
+        out_specs=[pl.BlockSpec((s.shape[0], GROUP), lambda g: (0, g)) for s in shapes],
+        compiler_params=pltpu.CompilerParams(vmem_limit_bytes=60 << 20),
+        cost_estimate=pl.CostEstimate(flops=8 * 10**9, bytes_accessed=10**7, transcendentals=6 * 10**6),
+        name="attend")(x, w, cos, sin, bias)
+
+
+def attend_back_kernel(x_ref, w_ref, q_ref, k_ref, v_ref, g_ref, res_ref, cos_ref, sin_ref, bias_ref,
+                       dw_ref, own_ref, oth_ref, xt_ref, acc_ref, dq_ref, dk_ref, dv_ref):
+    group = pl.program_id(0)
+    rows = q_ref.shape[0]
+    core = lax.axis_index("dp")
+    mine = pl.ds(pl.multiple_of(core * rows, rows), rows)
+    theirs = pl.ds(pl.multiple_of((1 - core) * rows, rows), rows)
+    blocks = x_ref.shape[1] // LANES
+    step = 256
+
+    @pl.when(group == 0)
+    def _():
+        xt_ref[...] = x_ref[...].T
+        own_ref[...] = res_ref[...]
+        acc_ref[...] = jnp.zeros_like(acc_ref)
+
+    dk_ref[...] = jnp.zeros_like(dk_ref)
+    dv_ref[...] = jnp.zeros_like(dv_ref)
+    for pair in range(GROUP // LANES):
+        lanes = slice(pair * LANES, pair * LANES + LANES)
+        for start in range(0, rows, step):
+            qp, gp = q_ref[start:start + step, lanes], g_ref[start:start + step, lanes]
+            low = lane_of(qp.shape) < HEAD
+            dqs = []
+            for head in range(2):
+                keep = low if head == 0 else jnp.logical_not(low)
+                qm, gm = jnp.where(keep, qp, jnp.zeros_like(qp)), jnp.where(keep, gp, jnp.zeros_like(gp))
+                s = nt(k_ref[:, lanes], qm) + jnp.concatenate([bias_ref[...]] * (step // LANES), 1)
+                e = jnp.exp(s - jnp.max(s, axis=0, keepdims=True))
+                p = e * (1.0 / jnp.sum(e, axis=0, keepdims=True))
+                dp = nt(v_ref[:, lanes], gm)
+                delta = jnp.sum(p * dp, axis=0, keepdims=True)
+                ds = (p * (dp - delta)).astype(LOW)
+                dv_ref[:, lanes] += nn(p.astype(LOW), gm)
+                dk_ref[:, lanes] += nn(ds, qm)
+                dqs.append(tn(ds, k_ref[:, lanes]))
+            dq_ref[start:start + step, lanes] = jnp.where(low, dqs[0], dqs[1]) * 0.125
+
+    def back(u, cos, sin):
+        return (u * cos - turn(u) * sin).astype(LOW)
+
+    gq = back(dq_ref[...], cos_ref[mine, :], sin_ref[mine, :])
+    dk_ref[...] = dk_ref[...] * cos_ref[...] - turn(dk_ref[...]) * sin_ref[...]
+
+    def put(block, value):
+        per = dw_ref.shape[2] // LANES
+        for i in range(2):
+            b = block + i
+            dw_ref[b // per, :, pl.ds(pl.multiple_of(b % per * LANES, LANES), LANES)] = value[:, i * LANES:i * LANES + LANES].astype(LOW)
+
+    put(2 * group, nn(xt_ref[:, pl.ds(pl.multiple_of(core * rows, rows), rows)], gq))
+    put(blocks + 2 * group, nn(xt_ref[...], dk_ref[...].astype(LOW)))
+    put(2 * blocks + 2 * group, nn(xt_ref[...], dv_ref[...].astype(LOW)))
+    wq, wk, wv = (weight_block(w_ref, n * blocks + 2 * group) for n in range(3))
+    own_ref[...] += nt(gq, wq) + nt(dk_ref[mine, :].astype(LOW), wk) + nt(dv_ref[mine, :].astype(LOW), wv)
+    acc_ref[...] += nt(dk_ref[theirs, :].astype(LOW), wk) + nt(dv_ref[theirs, :].astype(LOW), wv)
+
+    @pl.when(group == pl.num_programs(0) - 1)
+    def _():
+        oth_ref[...] = acc_ref[...].astype(LOW)
+
+
+def attend_back(x, w, q, k, v, g_att, g_res1, cos, sin, bias_col):
+    tokens, width = x.shape
+    rows = tokens // 2
+    part = lambda n: pl.BlockSpec((n, GROUP), lambda g: (0, g))
+    shapes = [jax.ShapeDtypeStruct(w.shape, LOW), jax.ShapeDtypeStruct((rows, width), F32), jax.ShapeDtypeStruct((rows, width), LOW)]
+    return pl.pallas_call(
+        attend_back_kernel, grid=(width // GROUP,), out_shape=shapes,
+        in_specs=[FULL, FULL, part(rows), part(tokens), part(tokens), part(rows), FULL, FULL, FULL, FULL],
+        out_specs=[FULL] * 3,
+        scratch_shapes=[pltpu.VMEM((width, tokens), LOW), pltpu.VMEM((rows, width), F32), pltpu.VMEM((rows, GROUP), F32),
+                        pltpu.VMEM((tokens, GROUP), F32), pltpu.VMEM((tokens, GROUP), F32)],
+        compiler_params=pltpu.CompilerParams(vmem_limit_bytes=60 << 20),
+        cost_estimate=pl.CostEstimate(flops=16 * 10**9, bytes_accessed=10**7, transcendentals=6 * 10**6),
+        name="attend_back")(x, w, q, k, v, g_att, g_res1, cos, sin, bias_col)
+
+
+def ln_parts(u):
+    center = u - jnp.mean(u, axis=1, keepdims=True)
+    inv = lax.rsqrt(jnp.mean(center * center, axis=1, keepdims=True) + EPS)
+    return center * inv, inv
+
+
+def ln_back(g, n, inv):
+    return inv * (g - jnp.mean(g, axis=1, keepdims=True) - n * jnp.mean(g * n, axis=1, keepdims=True))
+
+
+def middle_kernel(tiles, x_ref, att_ref, wo_ref, wg_ref, wu_ref, wd_ref, cot_ref, ln_ref, valid_ref,
+                  y_ref, dwg_ref, dwu_ref, dwd_ref, dwo_ref, gatt_ref, gres_ref, dln_ref,
+                  n1_ref, inv1_ref, hid_ref, hidt_ref, gate_ref, up_ref, acc_ref, gb_ref):
+    index = pl.program_id(0)
+    width = x_ref.shape[1]
+    half = width // 2
+
+    def wide(ref):
+        return jnp.concatenate([ref[0], ref[1]], 1)
+
+    @pl.when(index == 0)
+    def _():
+        n1, inv1 = ln_parts(x_ref[...].astype(F32) + nn(att_ref[...], wide(wo_ref)))
+        hidden = n1 * ln_ref[0:1, :] + ln_ref[1:2, :]
+        n1_ref[...] = n1
+        inv1_ref[...] = jnp.broadcast_to(inv1, inv1_ref.shape)
+        acc_ref[...] = hidden
+        low = hidden.astype(LOW)
+        hid_ref[...] = low
+        hidt_ref[...] = low.T
+
+    tile = wg_ref.shape[2]
+    f = jnp.where(index < tiles, index, index - tiles)
+    cols = pl.ds(pl.multiple_of(f * tile, tile), tile)
+
+    @pl.when(index < tiles)
+    def _():
+        gate, up = nn(hid_ref[...], wg_ref[0]), nn(hid_ref[...], wu_ref[0])
+        gate_ref[:, cols] = gate
+        up_ref[:, cols] = up
+        acc_ref[...] += nn((gate * jax.nn.sigmoid(gate) * up).astype(LOW), wide(wd_ref))
+
+    @pl.when(index == tiles - 1)
+    def _():
+        n2, inv2 = ln_parts(acc_ref[...])
+        valid = valid_ref[:, 0:1]
+        y_ref[...] = ((n2 * ln_ref[2:3, :] + ln_ref[3:4, :]) * valid).astype(LOW)
+        g_y = cot_ref[...].astype(F32) * valid
+        dln_ref[2:3, :] = jnp.sum(g_y * n2, axis=0, keepdims=True)
+        dln_ref[3:4, :] = jnp.sum(g_y, axis=0, keepdims=True)
+        g_res2 = ln_back(g_y * ln_ref[2:3, :], n2, inv2)
+        acc_ref[...] = g_res2
+        gb_ref[...] = g_res2.astype(LOW)
+
+    @pl.when(index >= tiles)
+    def _():
+        gate, up = gate_ref[:, cols], up_ref[:, cols]
+        sig = jax.nn.sigmoid(gate)
+        act = gate * sig
+        gb = gb_ref[...]
+        dwd = tn((act * up).astype(LOW), gb)
+        dwd_ref[0] = dwd[:, :half].astype(LOW)
+        dwd_ref[1] = dwd[:, half:].astype(LOW)
+        g_inner = nt(gb, wide(wd_ref))
+        g_gate = (g_inner * up * sig * (1.0 + gate * (1.0 - sig))).astype(LOW)
+        g_up = (g_inner * act).astype(LOW)
+        dwg_ref[0] = nn(hidt_ref[...], g_gate).astype(LOW)
+        dwu_ref[0] = nn(hidt_ref[...], g_up).astype(LOW)
+        acc_ref[...] += nt(g_gate, wg_ref[0]) + nt(g_up, wu_ref[0])
+
+    @pl.when(index == 2 * tiles - 1)
+    def _():
+        g_hidden, n1 = acc_ref[...], n1_ref[...]
+        dln_ref[0:1, :] = jnp.sum(g_hidden * n1, axis=0, keepdims=True)
+        dln_ref[1:2, :] = jnp.sum(g_hidden, axis=0, keepdims=True)
+        g_res1 = ln_back(g_hidden * ln_ref[0:1, :], n1, inv1_ref[:, 0:1])
+        gres_ref[...] = g_res1
+        gb1 = g_res1.astype(LOW)
+        dwo = tn(att_ref[...], gb1)
+        dwo_ref[0] = dwo[:, :half].astype(LOW)
+        dwo_ref[1] = dwo[:, half:].astype(LOW)
+        gatt_ref[...] = nt(gb1, wide(wo_ref)).astype(LOW)
+
+
+def middle(x_own, att, wo, wg, wu, wd, cot, ln, valid):
+    rows, width = x_own.shape
+    hidden = wd.shape[1]
+    tile = 512
+    tiles = hidden // tile
+    per = wg.shape[2] // tile
+    at = lambda i: jnp.where(i < tiles, i, i - tiles)
+    late = lambda i: jnp.maximum(i - tiles, 0)
+    cols = lambda pick: pl.BlockSpec((1, width, tile), lambda i: (pick(i) // per, 0, pick(i) % per))
+    rowb = lambda pick: pl.BlockSpec((2, tile, wd.shape[2]), lambda i: (0, pick(i), 0))
+    sds = jax.ShapeDtypeStruct
+    return pl.pallas_call(
+        functools.partial(middle_kernel, tiles), grid=(2 * tiles,),
+        out_shape=[sds((rows, width), LOW), sds(wg.shape, LOW), sds(wu.shape, LOW), sds(wd.shape, LOW), sds(wo.shape, LOW),
+                   sds((rows, width), LOW), sds((rows, width), F32), sds((8, width), F32)],
+        in_specs=[FULL, FULL, FULL, cols(at), cols(at), rowb(at), FULL, FULL, FULL],
+        out_specs=[FULL, cols(late), cols(late), rowb(late), FULL, FULL, FULL, FULL],
+        scratch_shapes=[pltpu.VMEM((rows, width), F32), pltpu.VMEM((rows, LANES), F32), pltpu.VMEM((rows, width), LOW),
+                        pltpu.VMEM((width, rows), LOW), pltpu.VMEM((rows, hidden), F32), pltpu.VMEM((rows, hidden), F32),
+                        pltpu.VMEM((rows, width), F32), pltpu.VMEM((rows, width), LOW)],
+        compiler_params=pltpu.CompilerParams(vmem_limit_bytes=60 << 20),
+        cost_estimate=pl.CostEstimate(flops=24 * 10**9, bytes_accessed=6 * 10**7, transcendentals=3 * 10**6),
+        name="middle")(x_own, att, wo, wg, wu, wd, cot, ln, valid)
+
+
+def rotary_lanes(tokens):
+    lane = jnp.arange(GROUP)
+    pair_index = (lane % (HEAD // 2)).astype(F32)
+    inverse = jnp.power(jnp.float32(1000.0), -2.0 * pair_index / HEAD)
+    angles = jnp.arange(tokens).astype(F32)[:, None] * inverse[None, :]
+    sign = jnp.where(lane % HEAD < HEAD // 2, -1.0, 1.0).astype(F32)
+    return jnp.cos(angles), jnp.sin(angles) * sign[None, :]
+
+
+def local_by_slot(tokens, lengths, w_qkv, w_out, w_gate, w_up, w_down, ln_params, cotangent):
+    slots, span, width = tokens.shape
+    core, chip = lax.axis_index("dp"), lax.axis_index("seq")
+    half = CHIPS // 2
+    small = jnp.zeros((8, LANES), F32)
+    share = ln_params.shape[1]
+    small = small.at[:4, :share].set(ln_params.astype(F32)).at[4, :slots].set(lengths.astype(F32))
+    x, cot, wq, wo, wg, wu, wd, smalls = gather(tokens, cotangent, [w_qkv, w_out, w_gate, w_up, w_down, small])
+    total, rows = x.shape[0], x.shape[0] // 2
+    ln = jnp.pad(smalls[:, :4, :share].transpose(1, 0, 2).reshape(4, width), ((0, 4), (0, 0)))
+    length = lax.dynamic_slice(smalls, (chip // half * CHIPS, 4, chip % half), (1, 1, 1)).reshape(()).astype(jnp.int32)
+    cos, sin = rotary_lanes(total)
+    position = jnp.arange(total)
+    out_of = jnp.where(position < length, 0.0, masked_score).astype(F32)
+    bias = jnp.broadcast_to(out_of[None, :], (8, total))
+    bias_col = jnp.broadcast_to(out_of[:, None], (total, LANES))
+    valid = jnp.broadcast_to((core * rows + jnp.arange(rows) < length).astype(F32)[:, None], (rows, LANES))
+    q, k, v, att = attend(x, wq, cos, sin, bias)
+    x_own = lax.dynamic_slice_in_dim(x, core * rows, rows, 0)
+    y, dwg, dwu, dwd, dwo, g_att, g_res1, dln = middle(x_own, att, wo, wg, wu, wd, cot, ln, valid)
+    dwq, gt_own, gt_other = attend_back(x, wq, q, k, v, g_att, g_res1, cos, sin, bias_col)
+    dsmall = dln[:4].reshape(4, 2 * CHIPS, share).transpose(1, 0, 2)
+    dsmall = jnp.pad(dsmall, ((0, 0), (0, 4), (0, LANES - share)))
+    output, grad_tokens, *finals = scatter(y, gt_own, gt_other, [dwq, dwo, dwg, dwu, dwd, dsmall])
+    finals[-1] = finals[-1][:4, :share]
+    return (output, grad_tokens, *finals)
+
+
 def solution(mesh):
     placed = (
         P("dp", "seq", None),
@@ -327,19 +1086,25 @@
         P(None, ("dp", "seq")),
         P("dp", "seq", None),
     )
-    return jax.shard_map(
-        local,
-        mesh=mesh,
-        in_specs=placed,
-        out_specs=(
-            P("dp", "seq", None),
-            P("dp", "seq", None),
-            P("seq", "dp"),
-            P("seq", "dp"),
-            P("seq", "dp"),
-            P("seq", "dp"),
-            P("seq", "dp"),
-            P(None, ("dp", "seq")),
-        ),
-        check_vma=False,
-    )
+
+    def run(tokens, *rest):
+        by_slot = mesh.shape["dp"] == 2 and mesh.shape["seq"] == CHIPS and tokens.shape[0] == CHIPS
+        body = local_by_slot if by_slot else local
+        return jax.shard_map(
+            body,
+            mesh=mesh,
+            in_specs=placed,
+            out_specs=(
+                P("dp", "seq", None),
+                P("dp", "seq", None),
+                P("seq", "dp"),
+                P("seq", "dp"),
+                P("seq", "dp"),
+                P("seq", "dp"),
+                P("seq", "dp"),
+                P(None, ("dp", "seq")),
+            ),
+            check_vma=False,
+        )(tokens, *rest)
+
+    return run

time: 3390 us -> 344 us (0.10)
  waiting for transfers between devices: 1690 us -> 0 us
  local copies, waits for them, and re-layouts: 868 us -> 15.5 us
  matrix products: 377 us -> 0 us
  Pallas kernels: 0 us -> 318 us
  other arithmetic: 281 us -> 9.48 us
  blocking collectives: 131 us -> 0 us
    ppermute x62 -> x0, waiting for transfers between devices: 599 us -> none  [shifted(): lax.ppermute(shard, axis, [(i, (i + by) % count) for i in range(count)])]
    reduce_scatter x7 -> x0, waiting for transfers between devices: 482 us -> none  [the longest x1 132 us: local(): lax.psum_scatter(col_down.astype(jnp.bfloat16), 'seq', scatter_dimension=...]
    all_gather x11 -> x0, waiting for transfers between devices: 451 us -> none  [the longest x1 152 us: local(): value_piece = lax.all_gather(values, 'seq', axis=1, tiled=True)]
    reshape x116 -> x3, local copies, waits for them, and re-layouts: 420 us -> 0.24 us  [the longest x2 0.14 us: local_by_slot(): dsmall = dln[:4].reshape(4, 2 * CHIPS, share).transpose(1, 0, 2)]
    dot_general x127 -> x0, matrix products: 377 us -> none  [the longest x16 79.8 us: attend_block(): jnp.einsum('shqk,skhd->shqd', exp_scores.astype(jnp.bfloat16), heads_view...]
    pallas_call x0 -> x5, Pallas kernels: none -> 318 us  [the longest x1 112 us: gather(): pl.pallas_call(gather_kernel, out_shape=outs, in_specs=[anywhere] * (2 +...]
    convert_element_type x73 -> x3, other arithmetic: 186 us -> 1.9 us  [the longest x1 1.25 us: local_by_slot(): lax.dynamic_slice(smalls, (chip // half * CHIPS, 4, chip % half), (1, 1, 1))]
    unnamed x26 -> x0, waiting for transfers between devices: 155 us -> none
  transfers between devices with their start and end apart: 84 -> 0, of which waited for: 59 -> 0; matrix products, arithmetic and copies ran while one was open for 28% -> 0% of each run, Pallas kernels for 0% -> 0%
where the time goes in v1:
time: 344 us
  Pallas kernels  318 us (92%)
  local copies, waits for them, and re-layouts  15.5 us (5%)
  other arithmetic  9.48 us (3%)
    pallas_call x1, Pallas kernels, gather(): pl.pallas_call(gather_kernel, out_shape=outs, in_specs=[anywhere] * (2 +...  112 us
    pallas_call x1, Pallas kernels, scatter(): pl.pallas_call(scatter_kernel, out_shape=[out8, out8] + finals, in_specs=...  103 us
    pallas_call x1, Pallas kernels, attend_back(): pl.pallas_call(attend_back_kernel, grid=(width // GROUP,), out_shape=shap...  42.7 us
    pallas_call x1, Pallas kernels, middle(): pl.pallas_call(functools.partial(middle_kernel, tiles), grid=(2 * tiles,)...  39.9 us
    pallas_call x1, Pallas kernels, attend(): pl.pallas_call(attend_kernel, grid=(width // GROUP,), out_shape=shapes, i...  20.7 us
    unnamed x23, local copies, waits for them, and re-layouts  9.15 us

profile of v1, /device:TPU:0, one launch (start us, length us, event | category | flops | bytes accessed | tf_op | source)
XLA Modules:
  0.0 343.6 jit_solution(16580371003533792300)
XLA Ops:
  0.7 0.7 pad_convert_fusion
  1.3 0.7 convert_bitcast_fusion
  2.0 0.1 scatter.15.refs_5_
  2.1 0.0 copy-start.6
  2.1 0.6 copy-done.6
  2.7 111.9 %gather.1 = (bf16[1024,768]{1,0:T(8,128)(2,1)}, bf16[512,768]{1,0:T(8,128)(2,1)}, bf16[2,768,1152]{2,1,0:T(8,128)(2,1)}, bf16[2,768,384]{2,1,0:T(8,128)(2,1)}, b...) custom-call(bf16[8,64,768]{2,1,0:T(8,128)(2,1)} %tok.1, ...), custom_call_target="tpu_custom_call" | custom-call | tf_op jit(solution)/shard_map/gather/pallas_call | solution.py:536
  114.6 1.3 fusion.6
  115.9 0.6 fusion.1
  116.5 0.6 broadcast_in_dim.42.bias_ref
  117.2 5.6 %fusion = (f32[1024,256]{1,0:T(8,128)}, f32[1024,256]{1,0:T(8,128)}) fusion(f32[256]{0:T(256)S(1)} %get-tuple-element.96, f32[256]{0:T(256)S(1)} %get-tuple-element.97, f32[1024]{0:T(1024)S(1)} %iota_convert_fusion), kind=kLoop, calls=%fused_computation.2 | loop fusion | flops 524288 | bytes 2103296 | tf_op jit(solution)/shard_map/mul | solution.py:1046
  122.8 20.7 %attend.1 = (bf16[512,768]{1,0:T(8,128)(2,1)}, bf16[1024,768]{1,0:T(8,128)(2,1)}, bf16[1024,768]{1,0:T(8,128)(2,1)}, bf16[512,768]{1,0:T(8,128)(2,1)}) custom-call(bf16[1024,768]{1,0:T(8,128)(2,1)} %get-tuple-element.63.x_ref, bf16[2,768,1152]{2,1,0:T(8,128)(2,1)} %get-tuple-element.64.w_ref, f32[1024,256]{1,0:T(8,128)} %get-tuple-element.95.cos_ref, ...), custom_call_target="tpu_custom_call" | custom-call | flops 8000000000 | bytes 10000000 | tf_op jit(solution)/shard_map/attend/pallas_call | solution.py:844
  143.4 0.6 fusion.2
  144.1 0.8 broadcast_in_dim.43.valid_ref
  144.9 0.9 constant_dynamic-slice_fusion.x_ref
  145.9 0.1 reshape.128
  146.0 0.6 pad.18.ln_ref
  146.6 39.9 %middle.1 = (bf16[512,768]{1,0:T(8,128)(2,1)}, bf16[2,768,1536]{2,1,0:T(8,128)(2,1)}, bf16[2,768,1536]{2,1,0:T(8,128)(2,1)}, bf16[2,3072,384]{2,1,0:T(8,128)(2,1...) custom-call(bf16[512,768]{1,0:T(8,128)(2,1)} %constant_dynamic-slice_fusion., ...), custom_call_target="tpu_custom_call" | custom-call | flops 24000000000 | bytes 60000000 | tf_op jit(solution)/shard_map/middle/pallas_call | solution.py:1026
  186.5 1.0 broadcast_in_dim.44.bias_ref
  187.5 42.7 %attend_back.1 = (bf16[2,768,1152]{2,1,0:T(8,128)(2,1)}, f32[512,768]{1,0:T(8,128)}, bf16[512,768]{1,0:T(8,128)(2,1)}) custom-call(bf16[1024,768]{1,0:T(8,128)(2,1)} %get-tuple-element.63.x_ref, bf16[2,768,1152]{2,1,0:T(8,128)(2,1)} %get-tuple-element.64.w_ref, bf16[512,768]{1,0:T(8,128)(2,1)} %get-tuple-element.73.q_ref, ...), custom_call_target="tpu_custom_call" | custom-call | flops 16000000000 | bytes 10000000 | tf_op jit(solution)/shard_map/attend_back/pallas_call | solution.py:920
  230.3 0.1 reshape.129
  230.4 0.7 pad.19.refs_5_
  231.1 102.6 %scatter.18 = (bf16[8,64,768]{2,1,0:T(8,128)(2,1)}, bf16[8,64,768]{2,1,0:T(8,128)(2,1)}, f32[48,1152]{1,0:T(8,128)}, f32[48,384]{1,0:T(8,128)}, f32[48,1536]{1,0...) custom-call(bf16[512,768]{1,0:T(8,128)(2,1)} %get-tuple-element.72.y_own, ...), custom_call_target="tpu_custom_call" | custom-call | tf_op jit(solution)/shard_map/scatter/pallas_call | solution.py:758
  333.7 0.0 copy-start.4
  333.7 0.0 copy-start.3
  333.8 1.3 slice.50
  335.1 2.1 copy.30
  337.2 2.1 copy.31
  339.2 1.6 copy.32
  340.9 0.6 copy.33
  341.5 0.7 copy.34
  342.2 0.7 copy.35
  342.9 0.7 copy.36
  (18 shorter events, 0.1 us)
Async XLA Ops:
  2.1 0.6 copy-start.6
  122.7 22.2 %copy-start = (bf16[1024,768]{1,0:T(8,128)(2,1)S(1)}, bf16[1024,768]{1,0:T(8,128)(2,1)}, u32[]{:S(2)}) copy-start(bf16[1024,768]{1,0:T(8,128)(2,1)} %get-tuple-element.63.x_ref) | copy-start | bytes 4718596
  122.8 23.1 %copy-start.5 = (f32[32,8,128]{2,1,0:T(8,128)S(1)}, f32[32,8,128]{2,1,0:T(8,128)}, u32[]{:S(2)}) copy-start(f32[32,8,128]{2,1,0:T(8,128)} %get-tuple-element.65) | copy-start | bytes 393220
  187.5 42.7 %copy-start.7 = (f32[8,768]{1,0:T(8,128)S(1)}, f32[8,768]{1,0:T(8,128)}, u32[]{:S(2)}) copy-start(f32[8,768]{1,0:T(8,128)} %get-tuple-element.85) | copy-start | bytes 73732
  333.7 7.1 %copy-start.4 = (f32[48,384]{1,0:T(8,128)S(1)}, f32[48,384]{1,0:T(8,128)}, u32[]{:S(2)}) copy-start(f32[48,384]{1,0:T(8,128)} %get-tuple-element.109) | copy-start | bytes 221188
  333.7 7.8 %copy-start.3 = (f32[48,1536]{1,0:T(8,128)S(1)}, f32[48,1536]{1,0:T(8,128)}, u32[]{:S(2)}) copy-start(f32[48,1536]{1,0:T(8,128)} %get-tuple-element.110) | copy-start | bytes 884740
  333.7 8.5 %copy-start.2 = (f32[48,1536]{1,0:T(8,128)S(1)}, f32[48,1536]{1,0:T(8,128)}, u32[]{:S(2)}) copy-start(f32[48,1536]{1,0:T(8,128)} %get-tuple-element.111) | copy-start | bytes 884740
  333.8 9.2 %copy-start.1 = (f32[192,384]{1,0:T(8,128)S(1)}, f32[192,384]{1,0:T(8,128)}, u32[]{:S(2)}) copy-start(f32[192,384]{1,0:T(8,128)} %get-tuple-element.112) | copy-start | bytes 884740

commit v2 on v0

--- a/solution.py
+++ b/solution.py
@@ -1,6 +1,10 @@
+import functools
+
 import jax
 import jax.numpy as jnp
 from jax import lax
+from jax.experimental import pallas as pl
+from jax.experimental.pallas import tpu as pltpu
 from jax.sharding import PartitionSpec as P
 
 HEADS = 12
@@ -315,6 +319,880 @@
     return (output, grad_tokens, own_qkv, own_out, own_gate, own_up, own_down, own_norm)
 
 
+MESH = pl.DeviceIdType.MESH
+CHIPS, ZS = 16, 4
+OFFSETS = sorted(((dx, dy, dz) for dx in (0, 1) for dy in (0, 1) for dz in range(-3, 4)),
+                 key=lambda o: (2 * (o[0] + o[1]) + abs(o[2]), abs(o[2]), o))
+ORDERS = ("zxy", "zyx", "xzy", "yzx")
+
+
+def pick(index, values):
+    out = jnp.int32(0)
+    for position, value in enumerate(values):
+        if value:
+            out = out + jnp.where(index == position, jnp.int32(value), 0)
+    return out
+
+
+def spread(order, dx, dy, dz):
+    zero = {"x": dx == 0, "y": dy == 0, "z": dz == 0}
+    flags = {}
+    for position, axis in enumerate(order):
+        flag = zero[axis] if axis != "z" else None
+        for later in order[position + 1:]:
+            flag = zero[later] if flag is None else flag & zero[later]
+        flags[axis] = flag
+    up, down = dz <= 0, dz >= 0
+    if flags["z"] is not None:
+        up, down = up & flags["z"], down & flags["z"]
+    return flags["x"], flags["y"], up, down
+
+
+def place():
+    core, chip = lax.axis_index("dp"), lax.axis_index("seq")
+    return core, chip, chip % 2, (chip // 2) % 2, chip // 4
+
+
+def chip_at(x, y, z):
+    return (z * 2 + y) * 2 + x
+
+
+def meet_all(core, chip):
+    barrier = pltpu.get_barrier_semaphore()
+    me = core * CHIPS + chip
+
+    def greet(step, carry):
+        other = (me + step) % (2 * CHIPS)
+        pl.semaphore_signal(barrier, inc=1, device_id={"dp": other // CHIPS, "seq": other % CHIPS}, device_id_type=MESH)
+        return carry
+
+    lax.fori_loop(1, 2 * CHIPS, greet, 0)
+    pl.semaphore_wait(barrier, 2 * CHIPS - 1)
+
+
+def onward(order, dx, dy, dz):
+    zero = {"x": dx == 0, "y": dy == 0, "z": dz == 0}
+    links = []
+    for position, axis in enumerate(order):
+        if all(zero[later] for later in order[position + 1:]):
+            if axis == "z":
+                links += [2] * (dz <= 0) + [3] * (dz >= 0)
+            elif zero[axis]:
+                links.append("xy".index(axis))
+    return links
+
+
+def when(condition, action):
+    if condition is True:
+        action()
+    else:
+        pl.when(condition)(action)
+
+
+def gather_kernel(tok, cot, small, *refs):
+    count = len(ORDERS)
+    shards, refs = refs[:count], refs[count:]
+    (x_all, c_own, smalls), refs = refs[:3], refs[3:]
+    wides, refs = refs[:count], refs[count:]
+    send_sem, recv_sem, sib_sem, tok_send, tok_recv, tok_sib, cot_recv, own_sem, small_send, small_recv = refs
+    core, chip, x, y, z = place()
+    other = 1 - core
+    slots, span = tok.shape[0], tok.shape[1]
+    half = CHIPS // 2
+    me = core * CHIPS + chip
+    can = (True, True, z < ZS - 1, z > 0, True)
+    neighbours = (
+        {"dp": core, "seq": chip_at(1 - x, y, z)},
+        {"dp": core, "seq": chip_at(x, 1 - y, z)},
+        {"dp": core, "seq": chip_at(x, y, jnp.minimum(z + 1, ZS - 1))},
+        {"dp": core, "seq": chip_at(x, y, jnp.maximum(z - 1, 0))},
+        {"dp": other, "seq": chip},
+    )
+
+    def region(m, owner, source):
+        rows = shards[m].shape[0]
+        return wides[m].at[owner, pl.ds(pl.multiple_of(source * rows, rows), rows)]
+
+    def piece(m, source, link, own=False):
+        target = region(m, core, source)
+        return pltpu.make_async_remote_copy(
+            src_ref=shards[m] if own else target, dst_ref=target, send_sem=send_sem.at[m, link, source],
+            recv_sem=sib_sem.at[m, source] if link == 4 else recv_sem.at[m, source],
+            device_id=neighbours[link], device_id_type=MESH)
+
+    meet_all(core, chip)
+
+    def deliver(source, target, sends, recvs):
+        def one(j, carry):
+            slot = (chip + 1 + j) % half
+            to = core * half + slot
+            src, dst = source.at[slot], target
+            self_copy = (chip // half == core) & (to == chip)
+
+            @pl.when(self_copy)
+            def _():
+                pltpu.make_async_copy(src, dst, recvs.at[chip % half]).start()
+
+            @pl.when(jnp.logical_not(self_copy))
+            def _():
+                pltpu.make_async_remote_copy(
+                    src_ref=src, dst_ref=dst, send_sem=sends.at[slot], recv_sem=recvs.at[chip % half],
+                    device_id={"dp": chip // half, "seq": to}, device_id_type=MESH).start()
+            return carry
+
+        lax.fori_loop(0, slots, one, 0)
+
+    def rows_of(ref, index):
+        return ref.at[pl.ds(pl.multiple_of(index * span, span), span)]
+
+    def small_to(step):
+        to = (me + step) % (2 * CHIPS)
+        return pltpu.make_async_remote_copy(
+            src_ref=small, dst_ref=smalls.at[me], send_sem=small_send.at[step], recv_sem=small_recv.at[me],
+            device_id={"dp": to // CHIPS, "seq": to % CHIPS}, device_id_type=MESH)
+
+    deliver(tok, rows_of(x_all, chip), tok_send.at[0], tok_recv)
+    own_small = pltpu.make_async_copy(small, smalls.at[me], small_recv.at[me])
+    own_small.start()
+    for m in range(count):
+        for link in onward(ORDERS[m], 0, 0, 0) + [4]:
+            when(can[link], piece(m, chip, link, own=True).start)
+        pltpu.make_async_copy(shards[m], region(m, core, chip), own_sem.at[m]).start()
+    lax.fori_loop(1, 2 * CHIPS, lambda s, c: (small_to(s).start(), c)[1], 0)
+    deliver(cot, rows_of(c_own, chip % half), tok_send.at[1], cot_recv)
+
+    def arrived(m, offset):
+        dx, dy, dz = offset
+        source = chip_at((x + dx) % 2, (y + dy) % 2, z + dz)
+        piece(m, source, 0).wait_recv()
+        for link in onward(ORDERS[m], dx, dy, dz) + [4]:
+            when(can[link], piece(m, source, link).start)
+
+    def valid(offset):
+        dz = offset[2]
+        return True if dz == 0 else (z < ZS - dz if dz > 0 else z >= -dz)
+
+    def steps(offsets):
+        for offset in offsets:
+            def one():
+                for m in range(count):
+                    arrived(m, offset)
+            when(valid(offset), one)
+
+    steps(OFFSETS[1:5])
+
+    def relay(i, carry):
+        block = rows_of(x_all, core * half + i)
+        pltpu.make_async_copy(block, block, tok_recv.at[i]).wait()
+        pltpu.make_async_remote_copy(
+            src_ref=block, dst_ref=block, send_sem=tok_send.at[2, i], recv_sem=tok_sib.at[i],
+            device_id=neighbours[4], device_id_type=MESH).start()
+        return carry
+
+    lax.fori_loop(0, half, relay, 0)
+    steps(OFFSETS[5:])
+
+    def ends(i, carry):
+        block = rows_of(c_own, i)
+        pltpu.make_async_copy(block, block, cot_recv.at[i]).wait()
+        block = rows_of(x_all, other * half + i)
+        pltpu.make_async_copy(block, block, tok_sib.at[i]).wait()
+        block = rows_of(x_all, core * half + i)
+        pltpu.make_async_copy(block, block, tok_send.at[2, i]).wait()
+        self_copy = (chip // half == core) & (core * half + i == chip)
+
+        @pl.when(jnp.logical_not(self_copy))
+        def _():
+            pltpu.make_async_copy(tok.at[i], tok.at[i], tok_send.at[0, i]).wait()
+            pltpu.make_async_copy(cot.at[i], cot.at[i], tok_send.at[1, i]).wait()
+        return carry
+
+    lax.fori_loop(0, half, ends, 0)
+
+    def small_end(step, carry):
+        small_to(step).wait_send()
+        source = (me + step) % (2 * CHIPS)
+        pltpu.make_async_copy(small, smalls.at[source], small_recv.at[source]).wait()
+        return carry
+
+    lax.fori_loop(1, 2 * CHIPS, small_end, 0)
+    own_small.wait()
+
+    def sibling(source, carry):
+        for m in range(count):
+            block = region(m, other, source)
+            pltpu.make_async_copy(block, block, sib_sem.at[m, source]).wait()
+        return carry
+
+    lax.fori_loop(0, CHIPS, sibling, 0)
+    for offset in OFFSETS:
+        def sent():
+            source = chip_at((x + offset[0]) % 2, (y + offset[1]) % 2, z + offset[2])
+            for m in range(count):
+                for link in onward(ORDERS[m], *offset) + [4]:
+                    when(can[link], piece(m, source, link).wait_send)
+        when(valid(offset), sent)
+    for m in range(count):
+        pltpu.make_async_copy(shards[m], region(m, core, chip), own_sem.at[m]).wait()
+
+
+def gather(tokens, cotangent, small, shards):
+    count = len(shards)
+    slots, span, width = tokens.shape
+    low = jnp.bfloat16
+    outs = [jax.ShapeDtypeStruct((span * CHIPS, width), low), jax.ShapeDtypeStruct((span * CHIPS // 2, width), low),
+            jax.ShapeDtypeStruct((2 * CHIPS,) + small.shape, small.dtype)]
+    outs += [jax.ShapeDtypeStruct((2, s.shape[0] * CHIPS, s.shape[1]), s.dtype) for s in shards]
+    dma = pltpu.SemaphoreType.DMA
+    anywhere = pl.BlockSpec(memory_space=pl.ANY)
+    return pl.pallas_call(
+        gather_kernel,
+        out_shape=outs,
+        in_specs=[anywhere] * (3 + count),
+        out_specs=[anywhere] * len(outs),
+        scratch_shapes=[dma((count, 5, CHIPS)), dma((count, CHIPS)), dma((count, CHIPS)), dma((3, 8)), dma((8,)), dma((8,)), dma((8,)), dma((count,)),
+                        dma((2 * CHIPS,)), dma((2 * CHIPS,))],
+        compiler_params=pltpu.CompilerParams(collective_id=0, has_side_effects=True),
+        name="gather",
+    )(tokens, cotangent, small, *shards)
+
+
+LOW, F32 = jnp.bfloat16, jnp.float32
+EPS = 1e-12
+HEAD = 64
+LANES = 128
+GROUP = 256
+FULL = pl.BlockSpec(memory_space=pltpu.VMEM)
+
+
+def nn(a, b):
+    return jnp.dot(a, b, preferred_element_type=F32)
+
+
+def nt(a, b):
+    return lax.dot_general(a, b, (((1,), (1,)), ((), ())), preferred_element_type=F32)
+
+
+def tn(a, b):
+    return lax.dot_general(a, b, (((0,), (0,)), ((), ())), preferred_element_type=F32)
+
+
+def lane_of(shape):
+    return lax.broadcasted_iota(jnp.int32, shape, 1)
+
+
+def turn(u):
+    parts = []
+    for start in range(0, u.shape[1], LANES):
+        part = u[:, start:start + LANES]
+        first = lane_of(part.shape) % HEAD < HEAD // 2
+        parts.append(jnp.where(first, pltpu.roll(part, LANES - HEAD // 2, 1), pltpu.roll(part, HEAD // 2, 1)))
+    return jnp.concatenate(parts, 1)
+
+
+def weight_block(w_ref, block):
+    per = 3 * w_ref.shape[1] // 2 // LANES
+    cols = [w_ref[b // per, :, pl.ds(pl.multiple_of(b % per * LANES, LANES), LANES)] for b in (block, block + 1)]
+    return jnp.concatenate(cols, 1)
+
+
+def attend_kernel(x_ref, w_ref, cos_ref, sin_ref, bias_ref, q_ref, k_ref, v_ref, att_ref):
+    group = pl.program_id(0)
+    rows = q_ref.shape[0]
+    mine = pl.ds(pl.multiple_of(lax.axis_index("dp") * rows, rows), rows)
+    blocks = x_ref.shape[1] // LANES
+
+    def turned(u, cos, sin):
+        return u * jnp.concatenate([cos, cos], 1) + turn(u) * jnp.concatenate([sin, sin], 1)
+
+    q = turned(nn(x_ref[mine, :], weight_block(w_ref, 2 * group)), cos_ref[mine, :], sin_ref[mine, :]).astype(LOW)
+    q_ref[...] = q * jnp.asarray(0.125, LOW)
+    k_ref[...] = turned(nn(x_ref[...], weight_block(w_ref, blocks + 2 * group)), cos_ref[...], sin_ref[...]).astype(LOW)
+    v_ref[...] = nn(x_ref[...], weight_block(w_ref, 2 * blocks + 2 * group)).astype(LOW)
+    step = 256
+    bias = bias_ref[0:1, :]
+    for pair in range(GROUP // LANES):
+        lanes = slice(pair * LANES, pair * LANES + LANES)
+        for start in range(0, rows, step):
+            qp = q_ref[start:start + step, lanes]
+            low = lane_of(qp.shape) < HEAD
+            outs = []
+            for head in range(2):
+                qm = jnp.where(low if head == 0 else jnp.logical_not(low), qp, jnp.zeros_like(qp))
+                s = nt(qm, k_ref[:, lanes]) + bias
+                p = jnp.exp(s - jnp.max(s, axis=1, keepdims=True))
+                total = jnp.sum(p, axis=1, keepdims=True)
+                outs.append(nn(p.astype(LOW), v_ref[:, lanes]) / total)
+            att_ref[start:start + step, lanes] = jnp.where(low, outs[0], outs[1]).astype(LOW)
+
+
+def attend(x, w, cos, sin, bias):
+    tokens, width = x.shape
+    rows = tokens // 2
+    shapes = [jax.ShapeDtypeStruct((n, width), LOW) for n in (rows, tokens, tokens, rows)]
+    return pl.pallas_call(
+        attend_kernel, grid=(width // GROUP,), out_shape=shapes,
+        in_specs=[FULL] * 5,
+        out_specs=[pl.BlockSpec((s.shape[0], GROUP), lambda g: (0, g)) for s in shapes],
+        compiler_params=pltpu.CompilerParams(vmem_limit_bytes=60 << 20),
+        cost_estimate=pl.CostEstimate(flops=8 * 10**9, bytes_accessed=10**7, transcendentals=6 * 10**6),
+        name="attend")(x, w, cos, sin, bias)
+
+
+def ln_parts(u):
+    center = u - jnp.mean(u, axis=1, keepdims=True)
+    inv = lax.rsqrt(jnp.mean(center * center, axis=1, keepdims=True) + EPS)
+    return center * inv, inv
+
+
+def ln_back(g, n, inv):
+    return inv * (g - jnp.mean(g, axis=1, keepdims=True) - n * jnp.mean(g * n, axis=1, keepdims=True))
+
+
+def middle_kernel(tiles, x_ref, att_ref, wo_ref, wg_ref, wu_ref, wd_ref, cot_ref, ln_ref, valid_ref,
+                  y_ref, dwg_ref, dwu_ref, dwd_ref, dwo_ref, gatt_ref, gres_ref, dln_ref,
+                  n1_ref, inv1_ref, hid_ref, hidt_ref, gate_ref, up_ref, acc_ref, gb_ref):
+    index = pl.program_id(0)
+    width = x_ref.shape[1]
+    half = width // 2
+
+    def wide(ref):
+        return jnp.concatenate([ref[0], ref[1]], 1)
+
+    @pl.when(index == 0)
+    def _():
+        n1, inv1 = ln_parts(x_ref[...].astype(F32) + nn(att_ref[...], wide(wo_ref)))
+        hidden = n1 * ln_ref[0:1, :] + ln_ref[1:2, :]
+        n1_ref[...] = n1
+        inv1_ref[...] = jnp.broadcast_to(inv1, inv1_ref.shape)
+        acc_ref[...] = hidden
+        low = hidden.astype(LOW)
+        hid_ref[...] = low
+        hidt_ref[...] = low.T
+
+    tile = wg_ref.shape[2]
+    f = jnp.where(index < tiles, index, index - tiles)
+    cols = pl.ds(pl.multiple_of(f * tile, tile), tile)
+
+    @pl.when(index < tiles)
+    def _():
+        gate, up = nn(hid_ref[...], wg_ref[0]), nn(hid_ref[...], wu_ref[0])
+        gate_ref[:, cols] = gate
+        up_ref[:, cols] = up
+        acc_ref[...] += nn((gate * jax.nn.sigmoid(gate) * up).astype(LOW), wide(wd_ref))
+
+    @pl.when(index == tiles - 1)
+    def _():
+        n2, inv2 = ln_parts(acc_ref[...])
+        valid = valid_ref[:, 0:1]
+        y_ref[...] = ((n2 * ln_ref[2:3, :] + ln_ref[3:4, :]) * valid).astype(LOW)
+        g_y = cot_ref[...].astype(F32) * valid
+        dln_ref[2:3, :] = jnp.sum(g_y * n2, axis=0, keepdims=True)
+        dln_ref[3:4, :] = jnp.sum(g_y, axis=0, keepdims=True)
+        g_res2 = ln_back(g_y * ln_ref[2:3, :], n2, inv2)
+        acc_ref[...] = g_res2
+        gb_ref[...] = g_res2.astype(LOW)
+
+    @pl.when(index >= tiles)
+    def _():
+        gate, up = gate_ref[:, cols], up_ref[:, cols]
+        sig = jax.nn.sigmoid(gate)
+        act = gate * sig
+        gb = gb_ref[...]
+        dwd = tn((act * up).astype(LOW), gb)
+        dwd_ref[0] = dwd[:, :half].astype(LOW)
+        dwd_ref[1] = dwd[:, half:].astype(LOW)
+        g_inner = nt(gb, wide(wd_ref))
+        g_gate = (g_inner * up * sig * (1.0 + gate * (1.0 - sig))).astype(LOW)
+        g_up = (g_inner * act).astype(LOW)
+        dwg_ref[0] = nn(hidt_ref[...], g_gate).astype(LOW)
+        dwu_ref[0] = nn(hidt_ref[...], g_up).astype(LOW)
+        acc_ref[...] += nt(g_gate, wg_ref[0]) + nt(g_up, wu_ref[0])
+
+    @pl.when(index == 2 * tiles - 1)
+    def _():
+        g_hidden, n1 = acc_ref[...], n1_ref[...]
+        dln_ref[0:1, :] = jnp.sum(g_hidden * n1, axis=0, keepdims=True)
+        dln_ref[1:2, :] = jnp.sum(g_hidden, axis=0, keepdims=True)
+        g_res1 = ln_back(g_hidden * ln_ref[0:1, :], n1, inv1_ref[:, 0:1])
+        gres_ref[...] = g_res1
+        gb1 = g_res1.astype(LOW)
+        dwo = tn(att_ref[...], gb1)
+        dwo_ref[0] = dwo[:, :half].astype(LOW)
+        dwo_ref[1] = dwo[:, half:].astype(LOW)
+        gatt_ref[...] = nt(gb1, wide(wo_ref)).astype(LOW)
+
+
+def middle(x_own, att, wo, wg, wu, wd, cot, ln, valid):
+    rows, width = x_own.shape
+    hidden = wd.shape[1]
+    tile = 512
+    tiles = hidden // tile
+    per = wg.shape[2] // tile
+    at = lambda i: jnp.where(i < tiles, i, i - tiles)
+    late = lambda i: jnp.maximum(i - tiles, 0)
+    cols = lambda pick: pl.BlockSpec((1, width, tile), lambda i: (pick(i) // per, 0, pick(i) % per))
+    rowb = lambda pick: pl.BlockSpec((2, tile, wd.shape[2]), lambda i: (0, pick(i), 0))
+    sds = jax.ShapeDtypeStruct
+    return pl.pallas_call(
+        functools.partial(middle_kernel, tiles), grid=(2 * tiles,),
+        out_shape=[sds((rows, width), LOW), sds(wg.shape, LOW), sds(wu.shape, LOW), sds(wd.shape, LOW), sds((2, width, width // 2), LOW),
+                   sds((rows, width), LOW), sds((rows, width), F32), sds((8, width), F32)],
+        in_specs=[FULL, FULL, pl.BlockSpec((2, width, width // 2), lambda i: (0, 0, 3)), cols(at), cols(at), rowb(at), FULL, FULL, FULL],
+        out_specs=[FULL, cols(late), cols(late), rowb(late), FULL, FULL, FULL, FULL],
+        scratch_shapes=[pltpu.VMEM((rows, width), F32), pltpu.VMEM((rows, LANES), F32), pltpu.VMEM((rows, width), LOW),
+                        pltpu.VMEM((width, rows), LOW), pltpu.VMEM((rows, hidden), F32), pltpu.VMEM((rows, hidden), F32),
+                        pltpu.VMEM((rows, width), F32), pltpu.VMEM((rows, width), LOW)],
+        compiler_params=pltpu.CompilerParams(vmem_limit_bytes=60 << 20),
+        cost_estimate=pl.CostEstimate(flops=24 * 10**9, bytes_accessed=6 * 10**7, transcendentals=3 * 10**6),
+        name="middle")(x_own, att, wo, wg, wu, wd, cot, ln, valid)
+
+BACK_ORDERS = ("xzy", "zyx", "zyx")
+LATE_ORDERS = ("zxy", "zyx", "zxy")
+FAR_FIRST = OFFSETS[::-1]
+SIDES = {"x": 2, "y": 2, "z": ZS}
+
+
+def landing_slots(order):
+    sizes, room = {}, 1
+    for axis in order:
+        sizes[axis] = room * (ZS if axis == "z" else 1)
+        room *= SIDES[axis]
+    return sizes["x"], sizes["y"], sizes["z"], sizes["z"]
+
+
+def landing_index(order, link, x, y, z):
+    axis = "xyzz"[link]
+    index = 0
+    for before in order:
+        if before == axis:
+            break
+        index = index * SIDES[before] + {"x": x, "y": y, "z": z}[before]
+    return index * ZS + z if axis == "z" else index
+
+
+def back_scatter_kernel(y_own, dwg, dwu, dwd, dwo, dsmall, x_in, w_in, q_in, k_in, v_in, g_in, res_in, cos_in, sin_in, bias_in,
+                        y_out, gt_out, f_gate, f_up, f_down, f_out, f_qkv, f_small, *refs):
+    (xv, wv, qv, kv, vv, gv, own_acc, cosv, sinv, biasv, xt, oth_acc, dq, dk, dv, dw), refs = refs[:16], refs[16:]
+    owns, refs = refs[:3], refs[3:]
+    sibs, refs = refs[:4], refs[4:]
+    down_out, refs = refs[0], refs[1:]
+    lands, refs = refs[:24], refs[24:]
+    (gt_low, gt_sib, smalls), refs = refs[:3], refs[3:]
+    (in_sem, send_sem, recv_sem, sib_send, sib_recv, own_sem, late_send, late_recv, late_sib_send, late_sib_recv,
+     gt_sem, tok_send, y_recv, gt_recv, small_send, small_recv) = refs
+    core, chip, x, y, z = place()
+    other = 1 - core
+    half = CHIPS // 2
+    me = core * CHIPS + chip
+    span = y_out.shape[1]
+    rows = qv.shape[0]
+    mine = pl.ds(pl.multiple_of(core * rows, rows), rows)
+    theirs = pl.ds(pl.multiple_of(other * rows, rows), rows)
+    neighbours = (
+        {"dp": core, "seq": chip_at(1 - x, y, z)},
+        {"dp": core, "seq": chip_at(x, 1 - y, z)},
+        {"dp": core, "seq": chip_at(x, y, jnp.minimum(z + 1, ZS - 1))},
+        {"dp": core, "seq": chip_at(x, y, jnp.maximum(z - 1, 0))},
+    )
+    sibling = {"dp": other, "seq": chip}
+
+    loads = [pltpu.make_async_copy(source, target, in_sem.at[n]) for n, (source, target) in enumerate((
+        (k_in, kv), (q_in, qv), (bias_in, biasv), (v_in, vv), (g_in, gv), (x_in, xv), (w_in, wv), (res_in, own_acc), (cos_in, cosv), (sin_in, sinv)))]
+    for load in loads:
+        load.start()
+
+    def cut(ref, size, index):
+        return ref.at[pl.ds(pl.multiple_of(index * size, size), size)]
+
+    rows_gate, rows_down, rows_out = f_gate.shape[0], f_down.shape[0], f_out.shape[0]
+
+    def parts(m, owner, dest):
+        if m == 0:
+            return [(cut(dwg.at[owner], rows_gate, dest), 0, rows_gate)]
+        if m == 1:
+            return [(cut(dwu.at[owner], rows_gate, dest), 0, rows_gate)]
+        return [(cut(dwd.at[owner], rows_down, dest), 0, rows_down), (cut(dwo.at[owner], rows_out, dest), rows_down, rows_out)]
+
+    def to_sibling(m, dest):
+        return [pltpu.make_async_remote_copy(
+            src_ref=source, dst_ref=sibs[m].at[dest, pl.ds(start, size)], send_sem=sib_send.at[m + n, dest],
+            recv_sem=sib_recv.at[m + n, dest], device_id=sibling, device_id_type=MESH)
+            for n, (source, start, size) in enumerate(parts(m, other, dest))]
+
+    def own_load(m, dest, slot):
+        return [pltpu.make_async_copy(source, owns[m].at[slot, pl.ds(start, size)], own_sem.at[m + n, slot])
+                for n, (source, start, size) in enumerate(parts(m, core, dest))]
+
+    def dest_of(index):
+        dx = pick(index, [o[0] for o in FAR_FIRST])
+        dy = pick(index, [o[1] for o in FAR_FIRST])
+        dz = pick(index, [o[2] for o in FAR_FIRST])
+        return dx, dy, dz, (z + dz >= 0) & (z + dz < ZS), (x + dx) % 2, (y + dy) % 2, jnp.clip(z + dz, 0, ZS - 1)
+
+    meet_all(core, chip)
+
+    def begin(index, carry):
+        dx, dy, dz, valid, tx, ty, tz = dest_of(index)
+
+        @pl.when(valid)
+        def _():
+            for m in range(3):
+                for copy in to_sibling(m, chip_at(tx, ty, tz)):
+                    copy.start()
+        return carry
+
+    lax.fori_loop(0, len(FAR_FIRST), begin, 0)
+
+    def prefetch(index):
+        dx, dy, dz, valid, tx, ty, tz = dest_of(index)
+
+        @pl.when(valid & (index < len(FAR_FIRST)))
+        def _():
+            for m in range(3):
+                for copy in own_load(m, chip_at(tx, ty, tz), index % 3):
+                    copy.start()
+
+    prefetch(jnp.int32(0))
+    prefetch(jnp.int32(1))
+
+    def deliver(source, target, k, recvs):
+        def one(j, carry):
+            i = (chip + 1 + j) % half
+            to_core, to_chip = chip // half, core * half + i
+            src, dst = cut(source, span, i), target.at[chip % half]
+            self_copy = (to_core == core) & (to_chip == chip)
+
+            @pl.when(self_copy)
+            def _():
+                pltpu.make_async_copy(src, dst, recvs.at[chip % half]).start()
+
+            @pl.when(jnp.logical_not(self_copy))
+            def _():
+                pltpu.make_async_remote_copy(
+                    src_ref=src, dst_ref=dst, send_sem=tok_send.at[k, i], recv_sem=recvs.at[chip % half],
+                    device_id={"dp": to_core, "seq": to_chip}, device_id_type=MESH).start()
+            return carry
+
+        lax.fori_loop(0, half, one, 0)
+
+    def small_to(step):
+        to = (me + step) % (2 * CHIPS)
+        return pltpu.make_async_remote_copy(
+            src_ref=dsmall.at[to], dst_ref=smalls.at[me], send_sem=small_send.at[step], recv_sem=small_recv.at[me],
+            device_id={"dp": to // CHIPS, "seq": to % CHIPS}, device_id_type=MESH)
+
+    deliver(y_own, y_out, 0, y_recv)
+    lax.fori_loop(1, 2 * CHIPS, lambda s, c: (small_to(s).start(), c)[1], 0)
+    own_small = pltpu.make_async_copy(dsmall.at[me], smalls.at[me], small_recv.at[me])
+    own_small.start()
+
+    def reduce_piece(order, lands_m, send_at, recv_at, own, acc, offset, target, last, final):
+        dx, dy, dz = offset
+        tx, ty, tz = target
+        fx, fy, up, down = spread(order, dx, dy, dz)
+        flags = (fx, fy, up & (z < ZS - 1), down & (z > 0))
+
+        @pl.when(jnp.logical_not(last))
+        def _():
+            acc[...] += own()
+
+        @pl.when(last)
+        def _():
+            final[...] = acc[...].astype(F32) + own().astype(F32)
+
+        for link in range(4):
+            land = lands_m[link].at[landing_index(order, link, tx, ty, tz)]
+
+            @pl.when(flags[link])
+            def _():
+                pltpu.make_async_copy(land, land, recv_at(link)).wait()
+
+            @pl.when(flags[link] & jnp.logical_not(last))
+            def _():
+                acc[...] += land[...]
+
+            @pl.when(flags[link] & last)
+            def _():
+                final[...] += land[...].astype(F32)
+
+        away = {"x": dx != 0, "y": dy != 0, "z": dz != 0}
+        taken = None
+        for axis in order[::-1]:
+            here = away[axis] if taken is None else away[axis] & jnp.logical_not(taken)
+            taken = away[axis] if taken is None else taken | away[axis]
+            for link in {"x": (0,), "y": (1,), "z": (2, 3)}[axis]:
+                go = here if axis != "z" else (here & (dz > 0 if link == 2 else dz < 0))
+                there = {0: 0, 1: 1, 2: 3, 3: 2}[link]
+
+                @pl.when(go)
+                def _():
+                    pltpu.make_async_remote_copy(
+                        src_ref=acc, dst_ref=lands_m[there].at[landing_index(order, there, tx, ty, tz)],
+                        send_sem=send_at, recv_sem=recv_at(there), device_id=neighbours[link], device_id_type=MESH).start()
+
+    def early(index):
+        dx, dy, dz, valid, tx, ty, tz = dest_of(index)
+        last = index == len(FAR_FIRST) - 1
+        prefetch(index + 2)
+
+        @pl.when(valid)
+        def _():
+            dest = chip_at(tx, ty, tz)
+            for m in range(3):
+                for copy in own_load(m, dest, index % 3):
+                    copy.wait()
+                for copy in to_sibling(m, dest):
+                    copy.wait_recv()
+                reduce_piece(BACK_ORDERS[m], lands[4 * m:4 * m + 4], send_sem.at[m, dest], lambda link: recv_sem.at[m, link, dest],
+                             lambda: owns[m][index % 3], sibs[m].at[dest], (dx, dy, dz), (tx, ty, tz), last, (f_gate, f_up, down_out)[m])
+
+    step = 256
+    per_group = (GROUP // LANES) * (rows // step) * 2
+    groups = xv.shape[1] // GROUP
+    chunks = groups * per_group
+    blocks = xv.shape[1] // LANES
+    for load in loads[:5]:
+        load.wait()
+
+    def chunk(index):
+        group, inner = index // per_group, index % per_group
+        pair, block, head = inner // (per_group // 2), inner // 2 % (rows // step), inner % 2
+        here = pl.ds(pl.multiple_of(block * step, step), step)
+        lanes = pl.ds(pl.multiple_of(group * GROUP + pair * LANES, LANES), LANES)
+        out_lanes = pl.ds(pl.multiple_of(pair * LANES, LANES), LANES)
+
+        @pl.when(inner == 0)
+        def _():
+            dq[...] = jnp.zeros_like(dq)
+            dk[...] = jnp.zeros_like(dk)
+            dv[...] = jnp.zeros_like(dv)
+
+        qp, gp = qv[here, lanes], gv[here, lanes]
+        keep = lane_of(qp.shape) // HEAD == head
+        qm, gm = jnp.where(keep, qp, jnp.zeros_like(qp)), jnp.where(keep, gp, jnp.zeros_like(gp))
+        kp, vp = kv[:, lanes], vv[:, lanes]
+        s = nt(kp, qm) + jnp.concatenate([biasv[...]] * (step // LANES), 1)
+        e = jnp.exp(s - jnp.max(s, axis=0, keepdims=True))
+        p = e * (1.0 / jnp.sum(e, axis=0, keepdims=True))
+        dp = nt(vp, gm)
+        delta = jnp.sum(p * dp, axis=0, keepdims=True)
+        ds = (p * (dp - delta)).astype(LOW)
+        dv[:, out_lanes] += nn(p.astype(LOW), gm)
+        dk[:, out_lanes] += nn(ds, qm)
+        dq[here, out_lanes] += jnp.where(keep, tn(ds, kp), 0.0)
+
+        @pl.when(index == per_group - 1)
+        def _():
+            for load in loads[5:]:
+                load.wait()
+            xt[...] = xv[...].T
+            oth_acc[...] = jnp.zeros_like(oth_acc)
+
+        @pl.when(inner == per_group - 1)
+        def _():
+            finish(group)
+
+    def finish(group):
+        def back(u, cos, sin):
+            return u * jnp.concatenate([cos, cos], 1) - turn(u) * jnp.concatenate([sin, sin], 1)
+
+        def put(block, value):
+            per = dw.shape[2] // LANES
+            for i in range(2):
+                b = block + i
+                dw[b // per, :, pl.ds(pl.multiple_of(b % per * LANES, LANES), LANES)] = value[:, i * LANES:i * LANES + LANES].astype(LOW)
+
+        def weights(block):
+            per = dw.shape[2] // LANES
+            return jnp.concatenate([wv[b // per, :, pl.ds(pl.multiple_of(b % per * LANES, LANES), LANES)] for b in (block, block + 1)], 1)
+
+        gq = back(dq[...] * 0.125, cosv[mine, :], sinv[mine, :]).astype(LOW)
+        dk[...] = back(dk[...], cosv[...], sinv[...])
+        put(2 * group, nn(xt[:, mine], gq))
+        put(blocks + 2 * group, nn(xt[...], dk[...].astype(LOW)))
+        put(2 * blocks + 2 * group, nn(xt[...], dv[...].astype(LOW)))
+        wq, wk, wvv = (weights(n * blocks + 2 * group) for n in range(3))
+        own_acc[...] += nt(gq, wq) + nt(dk[mine, :].astype(LOW), wk) + nt(dv[mine, :].astype(LOW), wvv)
+        oth_acc[...] += nt(dk[theirs, :].astype(LOW), wk) + nt(dv[theirs, :].astype(LOW), wvv)
+
+    def turn_of(index, carry):
+        chunk(index)
+
+        @pl.when(index < mixed)
+        def _():
+            early(index)
+        return carry
+
+    mixed = min(chunks, len(FAR_FIRST) - 4)
+    lax.fori_loop(0, chunks, turn_of, 0)
+
+    gt_low[...] = oth_acc[...].astype(LOW)
+    third = f_qkv.shape[1] // len(LATE_ORDERS)
+
+    def late_to_sibling(dest):
+        return pltpu.make_async_remote_copy(
+            src_ref=cut(dw.at[other], rows_gate, dest), dst_ref=sibs[3].at[dest], send_sem=late_sib_send.at[dest],
+            recv_sem=late_sib_recv.at[dest], device_id=sibling, device_id_type=MESH)
+
+    def late_begin(index, carry):
+        dx, dy, dz, valid, tx, ty, tz = dest_of(index)
+
+        @pl.when(valid)
+        def _():
+            late_to_sibling(chip_at(tx, ty, tz)).start()
+        return carry
+
+    lax.fori_loop(0, len(FAR_FIRST), late_begin, 0)
+    cross = pltpu.make_async_remote_copy(src_ref=gt_low, dst_ref=gt_sib, send_sem=gt_sem.at[0], recv_sem=gt_sem.at[1],
+                                         device_id=sibling, device_id_type=MESH)
+    cross.start()
+
+    def late(index, carry):
+        dx, dy, dz, valid, tx, ty, tz = dest_of(index)
+        last = index == len(FAR_FIRST) - 1
+
+        @pl.when(valid)
+        def _():
+            dest = chip_at(tx, ty, tz)
+            late_to_sibling(dest).wait_recv()
+            for n, order in enumerate(LATE_ORDERS):
+                lanes = slice(n * third, n * third + third)
+                acc = sibs[3].at[dest, :, lanes]
+                reduce_piece(order, lands[12 + 4 * n:16 + 4 * n], late_send.at[n, dest], lambda link: late_recv.at[n, link, dest],
+                             lambda: dw[core, pl.ds(pl.multiple_of(dest * rows_gate, rows_gate), rows_gate), lanes],
+                             acc, (dx, dy, dz), (tx, ty, tz), last, f_qkv.at[:, lanes])
+
+        @pl.when((index % 2 == 1) & (mixed + index // 2 < len(FAR_FIRST)))
+        def _():
+            early(mixed + index // 2)
+        return carry
+
+    early_steps = 8
+    lax.fori_loop(0, early_steps, late, 0)
+    cross.wait()
+    gt_low[...] = (own_acc[...] + gt_sib[...].astype(F32)).astype(LOW)
+    deliver(gt_low, gt_out, 1, gt_recv)
+    lax.fori_loop(early_steps, len(FAR_FIRST), late, 0)
+    f_down[...] = down_out[0:rows_down, :]
+    f_out[...] = down_out[rows_down:rows_down + rows_out, :]
+
+    def small_end(s, carry):
+        small_to(s).wait_send()
+        source = (me + s) % (2 * CHIPS)
+        pltpu.make_async_copy(smalls.at[source], smalls.at[source], small_recv.at[source]).wait()
+        return carry
+
+    lax.fori_loop(1, 2 * CHIPS, small_end, 0)
+    own_small.wait()
+    f_small[...] = jnp.sum(smalls[...], axis=0)
+
+    def ends(i, carry):
+        for out, recvs, k in ((y_out, y_recv, 0), (gt_out, gt_recv, 1)):
+            pltpu.make_async_copy(out.at[i], out.at[i], recvs.at[i]).wait()
+            self_copy = (chip // half == core) & (core * half + i == chip)
+
+            @pl.when(jnp.logical_not(self_copy))
+            def _():
+                pltpu.make_async_copy(out.at[i], out.at[i], tok_send.at[k, i]).wait()
+        return carry
+
+    lax.fori_loop(0, half, ends, 0)
+
+    def sent(dest, carry):
+        for m in range(3):
+            for copy in to_sibling(m, dest):
+                copy.wait_send()
+        late_to_sibling(dest).wait_send()
+
+        @pl.when(dest != chip)
+        def _():
+            for m in range(3):
+                pltpu.make_async_copy(sibs[m].at[dest], sibs[m].at[dest], send_sem.at[m, dest]).wait()
+            for n in range(len(LATE_ORDERS)):
+                part = sibs[3].at[dest, :, pl.ds(n * third, third)]
+                pltpu.make_async_copy(part, part, late_send.at[n, dest]).wait()
+        return carry
+
+    lax.fori_loop(0, CHIPS, sent, 0)
+
+
+def back_scatter(y_own, dwg, dwu, dwd, dwo, dsmall, x, w, q, k, v, g_att, g_res1, cos, sin, bias_col):
+    tokens, width = x.shape
+    rows = tokens // 2
+    span = rows // 8
+    anywhere, vmem = pl.BlockSpec(memory_space=pl.ANY), pl.BlockSpec(memory_space=pltpu.VMEM)
+    n_gate, n_down, n_out = width // CHIPS, dwd.shape[1] // CHIPS, dwo.shape[1] // CHIPS
+    c_gate, c_down = dwg.shape[2], dwd.shape[2]
+    c_qkv = 3 * width // 2
+    third = c_qkv // len(LATE_ORDERS)
+    sds, mem = jax.ShapeDtypeStruct, pltpu.VMEM
+    out8 = sds((8, span, width), LOW)
+    finals = [sds((n_gate, c_gate), F32), sds((n_gate, c_gate), F32), sds((n_down, c_down), F32), sds((n_out, c_down), F32),
+              sds((n_gate, c_qkv), F32), sds(dsmall.shape[1:], F32)]
+    pieces = [(n_gate, c_gate), (n_gate, c_gate), (n_down + n_out, c_down)]
+    scratch = [mem((tokens, width), LOW), mem(w.shape, LOW), mem((rows, width), LOW), mem((tokens, width), LOW), mem((tokens, width), LOW),
+               mem((rows, width), LOW), mem((rows, width), F32), mem(cos.shape, F32), mem(sin.shape, F32), mem(bias_col.shape, F32),
+               mem((width, tokens), LOW), mem((rows, width), F32), mem((rows, GROUP), F32), mem((tokens, GROUP), F32), mem((tokens, GROUP), F32),
+               mem((2, width, c_qkv), LOW)]
+    scratch += [mem((3,) + piece, LOW) for piece in pieces]
+    scratch += [mem((CHIPS,) + piece, LOW) for piece in pieces] + [mem((CHIPS, n_gate, c_qkv), LOW)]
+    scratch += [mem(pieces[2], F32)]
+    for order, piece in zip(BACK_ORDERS, pieces):
+        scratch += [mem((n,) + piece, LOW) for n in landing_slots(order)]
+    for order in LATE_ORDERS:
+        scratch += [mem((n, n_gate, third), LOW) for n in landing_slots(order)]
+    scratch += [mem((rows, width), LOW), mem((rows, width), LOW), mem(dsmall.shape, F32)]
+    dma = pltpu.SemaphoreType.DMA
+    scratch += [dma((10,)), dma((3, CHIPS)), dma((3, 4, CHIPS)), dma((4, CHIPS)), dma((4, CHIPS)), dma((4, 3)), dma((3, CHIPS)), dma((3, 4, CHIPS)),
+                dma((CHIPS,)), dma((CHIPS,)), dma((2,)), dma((2, 8)), dma((8,)), dma((8,)), dma((2 * CHIPS,)), dma((2 * CHIPS,))]
+    return pl.pallas_call(
+        back_scatter_kernel,
+        out_shape=[out8, out8] + finals,
+        in_specs=[anywhere] * 16,
+        out_specs=[anywhere] * 2 + [vmem] * len(finals),
+        scratch_shapes=scratch,
+        compiler_params=pltpu.CompilerParams(collective_id=1, has_side_effects=True, vmem_limit_bytes=67043328),
+        name="back_scatter",
+    )(y_own, dwg, dwu, dwd, dwo, dsmall, x, w, q, k, v, g_att, g_res1, cos, sin, bias_col)
+
+
+def rotary_lanes(tokens):
+    lane = jnp.arange(LANES)
+    pair_index = (lane % (HEAD // 2)).astype(F32)
+    inverse = jnp.power(jnp.float32(1000.0), -2.0 * pair_index / HEAD)
+    angles = jnp.arange(tokens).astype(F32)[:, None] * inverse[None, :]
+    sign = jnp.where(lane % HEAD < HEAD // 2, -1.0, 1.0).astype(F32)
+    return jnp.cos(angles), jnp.sin(angles) * sign[None, :]
+
+
+def local_by_slot(tokens, lengths, w_qkv, w_out, w_gate, w_up, w_down, ln_params, cotangent):
+    slots, span, width = tokens.shape
+    core, chip = lax.axis_index("dp"), lax.axis_index("seq")
+    half = CHIPS // 2
+    small = jnp.zeros((8, LANES), F32)
+    share = ln_params.shape[1]
+    small = small.at[:4, :share].set(ln_params.astype(F32)).at[4, :slots].set(lengths.astype(F32))
+    x, cot, smalls, w_in, wg, wu, wd = gather(tokens, cotangent, small, [jnp.concatenate([w_qkv, w_out], 1), w_gate, w_up, w_down])
+    total, rows = x.shape[0], x.shape[0] // 2
+    ln = jnp.pad(smalls[:, :4, :share].transpose(1, 0, 2).reshape(4, width), ((0, 4), (0, 0)))
+    length = lax.dynamic_slice(smalls, (chip // half * CHIPS, 4, chip % half), (1, 1, 1)).reshape(()).astype(jnp.int32)
+    cos, sin = rotary_lanes(total)
+    position = jnp.arange(total)
+    out_of = jnp.where(position < length, 0.0, masked_score).astype(F32)
+    bias = jnp.broadcast_to(out_of[None, :], (8, total))
+    bias_col = jnp.broadcast_to(out_of[:, None], (total, LANES))
+    valid = jnp.broadcast_to((core * rows + jnp.arange(rows) < length).astype(F32)[:, None], (rows, LANES))
+    q, k, v, att = attend(x, w_in, cos, sin, bias)
+    x_own = lax.dynamic_slice_in_dim(x, core * rows, rows, 0)
+    y, dwg, dwu, dwd, dwo, g_att, g_res1, dln = middle(x_own, att, w_in, wg, wu, wd, cot, ln, valid)
+    dsmall = dln[:4].reshape(4, 2 * CHIPS, share).transpose(1, 0, 2)
+    dsmall = jnp.pad(dsmall, ((0, 0), (0, 4), (0, LANES - share)))
+    output, grad_tokens, d_gate, d_up, d_down, d_out, d_qkv, d_small = back_scatter(
+        y, dwg, dwu, dwd, dwo, dsmall, x, w_in, q, k, v, g_att, g_res1, cos, sin, bias_col)
+    return (output, grad_tokens, d_qkv, d_out, d_gate, d_up, d_down, d_small[:4, :share])
+
+
 def solution(mesh):
     placed = (
         P("dp", "seq", None),
@@ -327,19 +1205,25 @@
         P(None, ("dp", "seq")),
         P("dp", "seq", None),
     )
-    return jax.shard_map(
-        local,
-        mesh=mesh,
-        in_specs=placed,
-        out_specs=(
-            P("dp", "seq", None),
-            P("dp", "seq", None),
-            P("seq", "dp"),
-            P("seq", "dp"),
-            P("seq", "dp"),
-            P("seq", "dp"),
-            P("seq", "dp"),
-            P(None, ("dp", "seq")),
-        ),
-        check_vma=False,
-    )
+
+    def run(tokens, *rest):
+        by_slot = mesh.shape["dp"] == 2 and mesh.shape["seq"] == CHIPS and tokens.shape[0] == CHIPS
+        body = local_by_slot if by_slot else local
+        return jax.shard_map(
+            body,
+            mesh=mesh,
+            in_specs=placed,
+            out_specs=(
+                P("dp", "seq", None),
+                P("dp", "seq", None),
+                P("seq", "dp"),
+                P("seq", "dp"),
+                P("seq", "dp"),
+                P("seq", "dp"),
+                P("seq", "dp"),
+                P(None, ("dp", "seq")),
+            ),
+            check_vma=False,
+        )(tokens, *rest)
+
+    return run

time: 3390 us -> 310 us (0.09)
  waiting for transfers between devices: 1690 us -> 0 us
  local copies, waits for them, and re-layouts: 868 us -> 19 us
  matrix products: 377 us -> 0 us
  Pallas kernels: 0 us -> 281 us
  other arithmetic: 281 us -> 8.58 us
  blocking collectives: 131 us -> 0 us
    ppermute x62 -> x0, waiting for transfers between devices: 599 us -> none  [shifted(): lax.ppermute(shard, axis, [(i, (i + by) % count) for i in range(count)])]
    reduce_scatter x7 -> x0, waiting for transfers between devices: 482 us -> none  [the longest x1 132 us: local(): lax.psum_scatter(col_down.astype(jnp.bfloat16), 'seq', scatter_dimension=...]
    all_gather x11 -> x0, waiting for transfers between devices: 451 us -> none  [the longest x1 152 us: local(): value_piece = lax.all_gather(values, 'seq', axis=1, tiled=True)]
    reshape x116 -> x3, local copies, waits for them, and re-layouts: 420 us -> 0.24 us  [the longest x2 0.14 us: local_by_slot(): dsmall = dln[:4].reshape(4, 2 * CHIPS, share).transpose(1, 0, 2)]
    dot_general x127 -> x0, matrix products: 377 us -> none  [the longest x16 79.8 us: attend_block(): jnp.einsum('shqk,skhd->shqd', exp_scores.astype(jnp.bfloat16), heads_view...]
    pallas_call x0 -> x4, Pallas kernels: none -> 281 us  [the longest x1 115 us: back_scatter(): pl.pallas_call(back_scatter_kernel, out_shape=[out8, out8] + finals, in_s...]
    convert_element_type x73 -> x3, other arithmetic: 186 us -> 1.92 us  [the longest x1 1.27 us: local_by_slot(): lax.dynamic_slice(smalls, (chip // half * CHIPS, 4, chip % half), (1, 1, 1))]
    unnamed x26 -> x0, waiting for transfers between devices: 155 us -> none
  transfers between devices with their start and end apart: 84 -> 0, of which waited for: 59 -> 0; matrix products, arithmetic and copies ran while one was open for 28% -> 0% of each run, Pallas kernels for 0% -> 0%
where the time goes in v2:
time: 310 us; the launch traced here: 309 us
  Pallas kernels  281 us (91%)
  local copies, waits for them, and re-layouts  19 us (6%)
  other arithmetic  8.58 us (3%)
    pallas_call x1, Pallas kernels, back_scatter(): pl.pallas_call(back_scatter_kernel, out_shape=[out8, out8] + finals, in_s...  115 us
    pallas_call x1, Pallas kernels, gather(): pl.pallas_call(gather_kernel, out_shape=outs, in_specs=[anywhere] * (3 +...  105 us
    pallas_call x1, Pallas kernels, middle(): pl.pallas_call(functools.partial(middle_kernel, tiles), grid=(2 * tiles,)...  39.9 us
    pallas_call x1, Pallas kernels, attend(): pl.pallas_call(attend_kernel, grid=(width // GROUP,), out_shape=shapes, i...  20.7 us
    unnamed x15, local copies, waits for them, and re-layouts  12 us

profile of v2, /device:TPU:0, one launch (start us, length us, event | category | flops | bytes accessed | tf_op | source)
XLA Modules:
  0.0 308.9 jit_solution(680050285381435666)
XLA Ops:
  0.7 1.6 pad_maximum_fusion.refs_0_
  2.3 0.7 pad_convert_fusion
  2.9 0.7 convert_bitcast_fusion
  3.6 0.1 scatter.14.small
  3.7 0.0 copy-start.3
  3.7 0.6 copy-done.3
  4.3 105.0 %gather.1 = (bf16[1024,768]{1,0:T(8,128)(2,1)}, bf16[512,768]{1,0:T(8,128)(2,1)}, f32[32,8,128]{2,1,0:T(8,128)}, bf16[2,768,1536]{2,1,0:T(8,128)(2,1)}, bf16[2,7...) custom-call(bf16[8,64,768]{2,1,0:T(8,128)(2,1)} %tok.1, ...), custom_call_target="tpu_custom_call" | custom-call | tf_op jit(solution)/shard_map/gather/pallas_call | solution.py:548
  109.3 1.3 fusion.6
  110.6 0.6 fusion.1
  111.2 0.6 broadcast_in_dim.42.bias_ref
  111.8 3.1 fusion
  114.9 20.7 %attend.1 = (bf16[512,768]{1,0:T(8,128)(2,1)}, bf16[1024,768]{1,0:T(8,128)(2,1)}, bf16[1024,768]{1,0:T(8,128)(2,1)}, bf16[512,768]{1,0:T(8,128)(2,1)}) custom-call(bf16[1024,768]{1,0:T(8,128)(2,1)} %get-tuple-element.59.x_ref.x_in, bf16[2,768,1536]{2,1,0:T(8,128)(2,1)} %get-tuple-element.60.w_ref.wo_ref.w_in, f32[1024,128]{1,0:T(8,128)} %get-tuple-element.87.cos_ref.cos_in, ...), custom_call_target="tpu_custom_call" | custom-call | flops 8000000000 | bytes 10000000 | tf_op jit(solution)/shard_map/attend/pallas_call | solution.py:633
  135.6 0.6 fusion.2
  136.3 0.8 broadcast_in_dim.43.valid_ref
  137.1 0.0 copy-done
  137.1 0.9 constant_dynamic-slice_fusion.x_ref
  138.1 0.1 reshape.128
  138.2 0.6 pad.18.ln_ref
  138.8 39.9 %middle.1 = (bf16[512,768]{1,0:T(8,128)(2,1)}, bf16[2,768,1536]{2,1,0:T(8,128)(2,1)}, bf16[2,768,1536]{2,1,0:T(8,128)(2,1)}, bf16[2,3072,384]{2,1,0:T(8,128)(2,1...) custom-call(bf16[512,768]{1,0:T(8,128)(2,1)} %constant_dynamic-slice_fusion., ...), custom_call_target="tpu_custom_call" | custom-call | flops 24000000000 | bytes 60000000 | tf_op jit(solution)/shard_map/middle/pallas_call | solution.py:737
  178.7 0.7 slice.49
  179.4 0.1 reshape.129
  179.6 0.7 pad.19.dsmall
  180.2 1.0 broadcast_in_dim.44.bias_in
  181.2 115.0 %back_scatter.1 = (bf16[8,64,768]{2,1,0:T(8,128)(2,1)}, bf16[8,64,768]{2,1,0:T(8,128)(2,1)}, f32[48,1536]{1,0:T(8,128)}, f32[48,1536]{1,0:T(8,128)}, f32[192,384...) custom-call(bf16[512,768]{1,0:T(8,128)(2,1)} %get-tuple-element.67.y_own, ...), custom_call_target="tpu_custom_call" | custom-call | tf_op jit(solution)/shard_map/back_scatter/pallas_call | solution.py:1149
  296.2 1.3 slice.50
  297.5 2.1 copy.30
  299.6 2.1 copy.31
  301.6 1.6 copy.32
  303.3 1.5 copy.33
  304.8 1.7 copy.34
  306.5 1.7 copy.35
  308.2 0.7 copy.36
  (10 shorter events, 0.1 us)
Async XLA Ops:
  3.7 0.6 copy-start.3
  114.9 22.2 %copy-start = (bf16[1024,768]{1,0:T(8,128)(2,1)S(1)}, bf16[1024,768]{1,0:T(8,128)(2,1)}, u32[]{:S(2)}) copy-start(bf16[1024,768]{1,0:T(8,128)(2,1)} %get-tuple-element.59.x_ref.x_in) | copy-start | bytes 4718596
  114.9 23.2 %copy-start.2 = (f32[32,8,128]{2,1,0:T(8,128)S(1)}, f32[32,8,128]{2,1,0:T(8,128)}, u32[]{:S(2)}) copy-start(f32[32,8,128]{2,1,0:T(8,128)} %get-tuple-element.61) | copy-start | bytes 393220
  296.2 12.0 %copy-start.1 = (f32[192,384]{1,0:T(8,128)S(1)}, f32[192,384]{1,0:T(8,128)}, u32[]{:S(2)}) copy-start(f32[192,384]{1,0:T(8,128)} %get-tuple-element.104) | copy-start | bytes 884740

commit v3 on v2

--- a/solution.py
+++ b/solution.py
@@ -323,7 +323,6 @@
 CHIPS, ZS = 16, 4
 OFFSETS = sorted(((dx, dy, dz) for dx in (0, 1) for dy in (0, 1) for dz in range(-3, 4)),
                  key=lambda o: (2 * (o[0] + o[1]) + abs(o[2]), abs(o[2]), o))
-ORDERS = ("zxy", "zyx", "xzy", "yzx")
 
 
 def pick(index, values):
@@ -389,174 +388,6 @@
         pl.when(condition)(action)
 
 
-def gather_kernel(tok, cot, small, *refs):
-    count = len(ORDERS)
-    shards, refs = refs[:count], refs[count:]
-    (x_all, c_own, smalls), refs = refs[:3], refs[3:]
-    wides, refs = refs[:count], refs[count:]
-    send_sem, recv_sem, sib_sem, tok_send, tok_recv, tok_sib, cot_recv, own_sem, small_send, small_recv = refs
-    core, chip, x, y, z = place()
-    other = 1 - core
-    slots, span = tok.shape[0], tok.shape[1]
-    half = CHIPS // 2
-    me = core * CHIPS + chip
-    can = (True, True, z < ZS - 1, z > 0, True)
-    neighbours = (
-        {"dp": core, "seq": chip_at(1 - x, y, z)},
-        {"dp": core, "seq": chip_at(x, 1 - y, z)},
-        {"dp": core, "seq": chip_at(x, y, jnp.minimum(z + 1, ZS - 1))},
-        {"dp": core, "seq": chip_at(x, y, jnp.maximum(z - 1, 0))},
-        {"dp": other, "seq": chip},
-    )
-
-    def region(m, owner, source):
-        rows = shards[m].shape[0]
-        return wides[m].at[owner, pl.ds(pl.multiple_of(source * rows, rows), rows)]
-
-    def piece(m, source, link, own=False):
-        target = region(m, core, source)
-        return pltpu.make_async_remote_copy(
-            src_ref=shards[m] if own else target, dst_ref=target, send_sem=send_sem.at[m, link, source],
-            recv_sem=sib_sem.at[m, source] if link == 4 else recv_sem.at[m, source],
-            device_id=neighbours[link], device_id_type=MESH)
-
-    meet_all(core, chip)
-
-    def deliver(source, target, sends, recvs):
-        def one(j, carry):
-            slot = (chip + 1 + j) % half
-            to = core * half + slot
-            src, dst = source.at[slot], target
-            self_copy = (chip // half == core) & (to == chip)
-
-            @pl.when(self_copy)
-            def _():
-                pltpu.make_async_copy(src, dst, recvs.at[chip % half]).start()
-
-            @pl.when(jnp.logical_not(self_copy))
-            def _():
-                pltpu.make_async_remote_copy(
-                    src_ref=src, dst_ref=dst, send_sem=sends.at[slot], recv_sem=recvs.at[chip % half],
-                    device_id={"dp": chip // half, "seq": to}, device_id_type=MESH).start()
-            return carry
-
-        lax.fori_loop(0, slots, one, 0)
-
-    def rows_of(ref, index):
-        return ref.at[pl.ds(pl.multiple_of(index * span, span), span)]
-
-    def small_to(step):
-        to = (me + step) % (2 * CHIPS)
-        return pltpu.make_async_remote_copy(
-            src_ref=small, dst_ref=smalls.at[me], send_sem=small_send.at[step], recv_sem=small_recv.at[me],
-            device_id={"dp": to // CHIPS, "seq": to % CHIPS}, device_id_type=MESH)
-
-    deliver(tok, rows_of(x_all, chip), tok_send.at[0], tok_recv)
-    own_small = pltpu.make_async_copy(small, smalls.at[me], small_recv.at[me])
-    own_small.start()
-    for m in range(count):
-        for link in onward(ORDERS[m], 0, 0, 0) + [4]:
-            when(can[link], piece(m, chip, link, own=True).start)
-        pltpu.make_async_copy(shards[m], region(m, core, chip), own_sem.at[m]).start()
-    lax.fori_loop(1, 2 * CHIPS, lambda s, c: (small_to(s).start(), c)[1], 0)
-    deliver(cot, rows_of(c_own, chip % half), tok_send.at[1], cot_recv)
-
-    def arrived(m, offset):
-        dx, dy, dz = offset
-        source = chip_at((x + dx) % 2, (y + dy) % 2, z + dz)
-        piece(m, source, 0).wait_recv()
-        for link in onward(ORDERS[m], dx, dy, dz) + [4]:
-            when(can[link], piece(m, source, link).start)
-
-    def valid(offset):
-        dz = offset[2]
-        return True if dz == 0 else (z < ZS - dz if dz > 0 else z >= -dz)
-
-    def steps(offsets):
-        for offset in offsets:
-            def one():
-                for m in range(count):
-                    arrived(m, offset)
-            when(valid(offset), one)
-
-    steps(OFFSETS[1:5])
-
-    def relay(i, carry):
-        block = rows_of(x_all, core * half + i)
-        pltpu.make_async_copy(block, block, tok_recv.at[i]).wait()
-        pltpu.make_async_remote_copy(
-            src_ref=block, dst_ref=block, send_sem=tok_send.at[2, i], recv_sem=tok_sib.at[i],
-            device_id=neighbours[4], device_id_type=MESH).start()
-        return carry
-
-    lax.fori_loop(0, half, relay, 0)
-    steps(OFFSETS[5:])
-
-    def ends(i, carry):
-        block = rows_of(c_own, i)
-        pltpu.make_async_copy(block, block, cot_recv.at[i]).wait()
-        block = rows_of(x_all, other * half + i)
-        pltpu.make_async_copy(block, block, tok_sib.at[i]).wait()
-        block = rows_of(x_all, core * half + i)
-        pltpu.make_async_copy(block, block, tok_send.at[2, i]).wait()
-        self_copy = (chip // half == core) & (core * half + i == chip)
-
-        @pl.when(jnp.logical_not(self_copy))
-        def _():
-            pltpu.make_async_copy(tok.at[i], tok.at[i], tok_send.at[0, i]).wait()
-            pltpu.make_async_copy(cot.at[i], cot.at[i], tok_send.at[1, i]).wait()
-        return carry
-
-    lax.fori_loop(0, half, ends, 0)
-
-    def small_end(step, carry):
-        small_to(step).wait_send()
-        source = (me + step) % (2 * CHIPS)
-        pltpu.make_async_copy(small, smalls.at[source], small_recv.at[source]).wait()
-        return carry
-
-    lax.fori_loop(1, 2 * CHIPS, small_end, 0)
-    own_small.wait()
-
-    def sibling(source, carry):
-        for m in range(count):
-            block = region(m, other, source)
-            pltpu.make_async_copy(block, block, sib_sem.at[m, source]).wait()
-        return carry
-
-    lax.fori_loop(0, CHIPS, sibling, 0)
-    for offset in OFFSETS:
-        def sent():
-            source = chip_at((x + offset[0]) % 2, (y + offset[1]) % 2, z + offset[2])
-            for m in range(count):
-                for link in onward(ORDERS[m], *offset) + [4]:
-                    when(can[link], piece(m, source, link).wait_send)
-        when(valid(offset), sent)
-    for m in range(count):
-        pltpu.make_async_copy(shards[m], region(m, core, chip), own_sem.at[m]).wait()
-
-
-def gather(tokens, cotangent, small, shards):
-    count = len(shards)
-    slots, span, width = tokens.shape
-    low = jnp.bfloat16
-    outs = [jax.ShapeDtypeStruct((span * CHIPS, width), low), jax.ShapeDtypeStruct((span * CHIPS // 2, width), low),
-            jax.ShapeDtypeStruct((2 * CHIPS,) + small.shape, small.dtype)]
-    outs += [jax.ShapeDtypeStruct((2, s.shape[0] * CHIPS, s.shape[1]), s.dtype) for s in shards]
-    dma = pltpu.SemaphoreType.DMA
-    anywhere = pl.BlockSpec(memory_space=pl.ANY)
-    return pl.pallas_call(
-        gather_kernel,
-        out_shape=outs,
-        in_specs=[anywhere] * (3 + count),
-        out_specs=[anywhere] * len(outs),
-        scratch_shapes=[dma((count, 5, CHIPS)), dma((count, CHIPS)), dma((count, CHIPS)), dma((3, 8)), dma((8,)), dma((8,)), dma((8,)), dma((count,)),
-                        dma((2 * CHIPS,)), dma((2 * CHIPS,))],
-        compiler_params=pltpu.CompilerParams(collective_id=0, has_side_effects=True),
-        name="gather",
-    )(tokens, cotangent, small, *shards)
-
-
 LOW, F32 = jnp.bfloat16, jnp.float32
 EPS = 1e-12
 HEAD = 64
@@ -590,55 +421,6 @@
     return jnp.concatenate(parts, 1)
 
 
-def weight_block(w_ref, block):
-    per = 3 * w_ref.shape[1] // 2 // LANES
-    cols = [w_ref[b // per, :, pl.ds(pl.multiple_of(b % per * LANES, LANES), LANES)] for b in (block, block + 1)]
-    return jnp.concatenate(cols, 1)
-
-
-def attend_kernel(x_ref, w_ref, cos_ref, sin_ref, bias_ref, q_ref, k_ref, v_ref, att_ref):
-    group = pl.program_id(0)
-    rows = q_ref.shape[0]
-    mine = pl.ds(pl.multiple_of(lax.axis_index("dp") * rows, rows), rows)
-    blocks = x_ref.shape[1] // LANES
-
-    def turned(u, cos, sin):
-        return u * jnp.concatenate([cos, cos], 1) + turn(u) * jnp.concatenate([sin, sin], 1)
-
-    q = turned(nn(x_ref[mine, :], weight_block(w_ref, 2 * group)), cos_ref[mine, :], sin_ref[mine, :]).astype(LOW)
-    q_ref[...] = q * jnp.asarray(0.125, LOW)
-    k_ref[...] = turned(nn(x_ref[...], weight_block(w_ref, blocks + 2 * group)), cos_ref[...], sin_ref[...]).astype(LOW)
-    v_ref[...] = nn(x_ref[...], weight_block(w_ref, 2 * blocks + 2 * group)).astype(LOW)
-    step = 256
-    bias = bias_ref[0:1, :]
-    for pair in range(GROUP // LANES):
-        lanes = slice(pair * LANES, pair * LANES + LANES)
-        for start in range(0, rows, step):
-            qp = q_ref[start:start + step, lanes]
-            low = lane_of(qp.shape) < HEAD
-            outs = []
-            for head in range(2):
-                qm = jnp.where(low if head == 0 else jnp.logical_not(low), qp, jnp.zeros_like(qp))
-                s = nt(qm, k_ref[:, lanes]) + bias
-                p = jnp.exp(s - jnp.max(s, axis=1, keepdims=True))
-                total = jnp.sum(p, axis=1, keepdims=True)
-                outs.append(nn(p.astype(LOW), v_ref[:, lanes]) / total)
-            att_ref[start:start + step, lanes] = jnp.where(low, outs[0], outs[1]).astype(LOW)
-
-
-def attend(x, w, cos, sin, bias):
-    tokens, width = x.shape
-    rows = tokens // 2
-    shapes = [jax.ShapeDtypeStruct((n, width), LOW) for n in (rows, tokens, tokens, rows)]
-    return pl.pallas_call(
-        attend_kernel, grid=(width // GROUP,), out_shape=shapes,
-        in_specs=[FULL] * 5,
-        out_specs=[pl.BlockSpec((s.shape[0], GROUP), lambda g: (0, g)) for s in shapes],
-        compiler_params=pltpu.CompilerParams(vmem_limit_bytes=60 << 20),
-        cost_estimate=pl.CostEstimate(flops=8 * 10**9, bytes_accessed=10**7, transcendentals=6 * 10**6),
-        name="attend")(x, w, cos, sin, bias)
-
-
 def ln_parts(u):
     center = u - jnp.mean(u, axis=1, keepdims=True)
     inv = lax.rsqrt(jnp.mean(center * center, axis=1, keepdims=True) + EPS)
@@ -649,19 +431,21 @@
     return inv * (g - jnp.mean(g, axis=1, keepdims=True) - n * jnp.mean(g * n, axis=1, keepdims=True))
 
 
-def middle_kernel(tiles, x_ref, att_ref, wo_ref, wg_ref, wu_ref, wd_ref, cot_ref, ln_ref, valid_ref,
+def middle_kernel(tiles, x_ref, att_ref, wo_ref, wg_ref, wu_ref, wd_ref, cot_ref, ln_ref, bias_ref,
                   y_ref, dwg_ref, dwu_ref, dwd_ref, dwo_ref, gatt_ref, gres_ref, dln_ref,
                   n1_ref, inv1_ref, hid_ref, hidt_ref, gate_ref, up_ref, acc_ref, gb_ref):
     index = pl.program_id(0)
     width = x_ref.shape[1]
     half = width // 2
+    rows = att_ref.shape[0]
+    mine = pl.ds(pl.multiple_of(lax.axis_index("dp") * rows, rows), rows)
 
     def wide(ref):
         return jnp.concatenate([ref[0], ref[1]], 1)
 
     @pl.when(index == 0)
     def _():
-        n1, inv1 = ln_parts(x_ref[...].astype(F32) + nn(att_ref[...], wide(wo_ref)))
+        n1, inv1 = ln_parts(x_ref[mine, :].astype(F32) + nn(att_ref[...], wide(wo_ref)))
         hidden = n1 * ln_ref[0:1, :] + ln_ref[1:2, :]
         n1_ref[...] = n1
         inv1_ref[...] = jnp.broadcast_to(inv1, inv1_ref.shape)
@@ -684,7 +468,7 @@
     @pl.when(index == tiles - 1)
     def _():
         n2, inv2 = ln_parts(acc_ref[...])
-        valid = valid_ref[:, 0:1]
+        valid = jnp.where(bias_ref[mine, 0:1] == 0.0, 1.0, 0.0)
         y_ref[...] = ((n2 * ln_ref[2:3, :] + ln_ref[3:4, :]) * valid).astype(LOW)
         g_y = cot_ref[...].astype(F32) * valid
         dln_ref[2:3, :] = jnp.sum(g_y * n2, axis=0, keepdims=True)
@@ -723,8 +507,8 @@
         gatt_ref[...] = nt(gb1, wide(wo_ref)).astype(LOW)
 
 
-def middle(x_own, att, wo, wg, wu, wd, cot, ln, valid):
-    rows, width = x_own.shape
+def middle(x, att, wo, wg, wu, wd, cot, ln, bias_col):
+    rows, width = att.shape
     hidden = wd.shape[1]
     tile = 512
     tiles = hidden // tile
@@ -745,7 +529,333 @@
                         pltpu.VMEM((rows, width), F32), pltpu.VMEM((rows, width), LOW)],
         compiler_params=pltpu.CompilerParams(vmem_limit_bytes=60 << 20),
         cost_estimate=pl.CostEstimate(flops=24 * 10**9, bytes_accessed=6 * 10**7, transcendentals=3 * 10**6),
-        name="middle")(x_own, att, wo, wg, wu, wd, cot, ln, valid)
+        name="middle")(x, att, wo, wg, wu, wd, cot, ln, bias_col)
+
+
+def finish_kernel(count, *refs):
+    sources, targets, holds, (in_sem, out_sem) = refs[:count], refs[count:2 * count], refs[2 * count:3 * count], refs[3 * count:]
+    loads = [pltpu.make_async_copy(source, hold, in_sem.at[n]) for n, (source, hold) in enumerate(zip(sources, holds))]
+    stores = [pltpu.make_async_copy(hold, target, out_sem.at[n]) for n, (hold, target) in enumerate(zip(holds, targets))]
+    for load in loads:
+        load.start()
+    for load, store in zip(loads, stores):
+        load.wait()
+        store.start()
+    for store in stores:
+        store.wait()
+
+
+def finish(results):
+    count = len(results)
+    anywhere = pl.BlockSpec(memory_space=pl.ANY)
+    return pl.pallas_call(
+        functools.partial(finish_kernel, count), out_shape=[jax.ShapeDtypeStruct(r.shape, r.dtype) for r in results],
+        in_specs=[anywhere] * count, out_specs=[anywhere] * count,
+        scratch_shapes=[pltpu.VMEM(r.shape, r.dtype) for r in results] + [pltpu.SemaphoreType.DMA((count,))] * 2,
+        name="finish")(*results)
+
+FIRST_ORDERS = ("yzx", "xzy", "zyx", "zxy")
+REST_ORDERS = ("xzy", "zyx", "zyx")
+REST_STARTS = (12, 6, 0)
+REST_MIXES = 20
+TOKENS_AT = (1, 4, 7, 10, 13, 16, 18, 20)
+COTS_AT = (2, 3, 4, 5, 6, 7, 8, 9)
+CHUNK = 256
+
+
+def front_kernel(tok, cot, w_qkv, w_out, w_gate, w_up, w_down, ln_in, len_in, turns_far, turns_near,
+                 x_all, c_own, ln_out, w_first, wide_gate, wide_up, wide_down, q_out, k_out, v_out, att_out, cos_out, sin_out, bias_out, *refs):
+    (xv, wv, qv, kv, vv, attv, cosv, sinv, biasv, rowv, small, smalls, lnv), refs = refs[:13], refs[13:]
+    (first_send, first_recv, first_sib, rest_send, rest_recv, rest_sib, own_sem, tok_send, tok_recv, tok_sib, cot_recv,
+     small_send, small_recv, out_sem) = refs
+    core, chip, x, y, z = place()
+    other = 1 - core
+    slots, span = tok.shape[0], tok.shape[1]
+    half = CHIPS // 2
+    me = core * CHIPS + chip
+    rows, width = qv.shape
+    can = (True, True, z < ZS - 1, z > 0, True)
+    neighbours = (
+        {"dp": core, "seq": chip_at(1 - x, y, z)},
+        {"dp": core, "seq": chip_at(x, 1 - y, z)},
+        {"dp": core, "seq": chip_at(x, y, jnp.minimum(z + 1, ZS - 1))},
+        {"dp": core, "seq": chip_at(x, y, jnp.maximum(z - 1, 0))},
+        {"dp": other, "seq": chip},
+    )
+    shards, wides = (w_gate, w_up, w_down), (wide_gate, wide_up, wide_down)
+    n_first = w_out.shape[0]
+    c_first = w_out.shape[1]
+
+    def first_region(n, owner, source):
+        return wv.at[owner, pl.ds(pl.multiple_of(source * n_first, n_first), n_first), n * c_first:n * c_first + c_first]
+
+    def first_own(n):
+        return w_out if n == 3 else w_qkv.at[:, n * c_first:n * c_first + c_first]
+
+    def rest_region(m, owner, source):
+        size = shards[m].shape[0]
+        return wides[m].at[owner, pl.ds(pl.multiple_of(source * size, size), size)]
+
+    def first_piece(n, source, link, own=False):
+        target = first_region(n, core, source)
+        return pltpu.make_async_remote_copy(
+            src_ref=first_own(n) if own else target, dst_ref=target, send_sem=first_send.at[n, link, source],
+            recv_sem=first_sib.at[n, source] if link == 4 else first_recv.at[n, source],
+            device_id=neighbours[link], device_id_type=MESH)
+
+    def rest_piece(m, source, link, own=False):
+        target = rest_region(m, core, source)
+        return pltpu.make_async_remote_copy(
+            src_ref=shards[m] if own else target, dst_ref=target, send_sem=rest_send.at[m, link, source],
+            recv_sem=rest_sib.at[m, source] if link == 4 else rest_recv.at[m, source],
+            device_id=neighbours[link], device_id_type=MESH)
+
+    def valid(offset):
+        dz = offset[2]
+        return True if dz == 0 else (z < ZS - dz if dz > 0 else z >= -dz)
+
+    def source_at(offset):
+        return chip_at((x + offset[0]) % 2, (y + offset[1]) % 2, z + offset[2])
+
+    def arrive(piece, orders, offset):
+        def one():
+            source = source_at(offset)
+            for m, order in enumerate(orders):
+                piece(m, source, 0).wait_recv()
+                for link in onward(order, *offset) + [4]:
+                    when(can[link], piece(m, source, link).start)
+        when(valid(offset), one)
+
+    def send_own(piece, orders, m):
+        for link in onward(orders[m], 0, 0, 0) + [4]:
+            when(can[link], piece(m, chip, link, own=True).start)
+
+    def drain(piece, orders):
+        for offset in OFFSETS:
+            def one():
+                source = source_at(offset)
+                for m, order in enumerate(orders):
+                    for link in onward(order, *offset) + [4]:
+                        when(can[link], piece(m, source, link).wait_send)
+            when(valid(offset), one)
+
+    def rows_of(ref, index):
+        return ref.at[pl.ds(pl.multiple_of(index * span, span), span)]
+
+    def deliver(j, source, target, sends, recvs):
+        slot = (chip + 1 + j) % half
+        to = core * half + slot
+        src, dst = source.at[slot], target
+        self_copy = (chip // half == core) & (to == chip)
+
+        @pl.when(self_copy)
+        def _():
+            pltpu.make_async_copy(src, dst, recvs.at[chip % half]).start()
+
+        @pl.when(jnp.logical_not(self_copy))
+        def _():
+            pltpu.make_async_remote_copy(
+                src_ref=src, dst_ref=dst, send_sem=sends.at[slot], recv_sem=recvs.at[chip % half],
+                device_id={"dp": chip // half, "seq": to}, device_id_type=MESH).start()
+
+    def small_to(step):
+        to = (me + step) % (2 * CHIPS)
+        return pltpu.make_async_remote_copy(
+            src_ref=small, dst_ref=smalls.at[me], send_sem=small_send.at[step], recv_sem=small_recv.at[me],
+            device_id={"dp": to // CHIPS, "seq": to % CHIPS}, device_id_type=MESH)
+
+    lane = lax.broadcasted_iota(jnp.int32, (1, LANES), 1)
+    counts = jnp.zeros((1, LANES), F32)
+    for j in range(slots):
+        counts = counts + jnp.where(lane == j, len_in[j].astype(F32), 0.0)
+    small[...] = jnp.zeros_like(small)
+    small[0:ln_in.shape[0], 0:ln_in.shape[1]] = ln_in[...].astype(F32)
+    small[4:5, :] = counts
+    meet_all(core, chip)
+
+    for n in range(4):
+        send_own(first_piece, FIRST_ORDERS, n)
+        pltpu.make_async_copy(first_own(n), first_region(n, core, chip), own_sem.at[n]).start()
+    lax.fori_loop(1, 2 * CHIPS, lambda s, c: (small_to(s).start(), c)[1], 0)
+    own_small = pltpu.make_async_copy(small, smalls.at[me], small_recv.at[me])
+    own_small.start()
+
+    sign = jnp.where(lane % HEAD < HEAD // 2, -1.0, 1.0).astype(F32)
+    near = turns_near.shape[1]
+    for far in range(turns_far.shape[1]):
+        part = slice(far * near, far * near + near)
+        ca, sa = turns_far[0, far:far + 1, :], turns_far[1, far:far + 1, :]
+        cosv[part, :] = ca * turns_near[0] - sa * turns_near[1]
+        sinv[part, :] = (sa * turns_near[0] + ca * turns_near[1]) * sign
+
+    def relay(i, carry):
+        block = rows_of(xv, core * half + i)
+        pltpu.make_async_copy(block, block, tok_recv.at[i]).wait()
+        pltpu.make_async_remote_copy(
+            src_ref=block, dst_ref=block, send_sem=tok_send.at[2, i], recv_sem=tok_sib.at[i],
+            device_id=neighbours[4], device_id_type=MESH).start()
+        return carry
+
+    waiting = list(OFFSETS[1:])
+    for index, offset in enumerate(OFFSETS[1:]):
+        for j in range(half):
+            if index == TOKENS_AT[j]:
+                deliver(j, tok, rows_of(xv, chip), tok_send.at[0], tok_recv)
+        for m in range(3):
+            if index == REST_STARTS[m]:
+                send_own(rest_piece, REST_ORDERS, m)
+                pltpu.make_async_copy(shards[m], rest_region(m, core, chip), own_sem.at[4 + m]).start()
+        arrive(first_piece, FIRST_ORDERS, offset)
+        if index >= REST_MIXES:
+            arrive(rest_piece, REST_ORDERS, waiting.pop(0))
+
+    def first_in(source, carry):
+        for n in range(4):
+            block = first_region(n, other, source)
+            pltpu.make_async_copy(block, block, first_sib.at[n, source]).wait()
+        return carry
+
+    def small_in(step, carry):
+        source = (me + step) % (2 * CHIPS)
+        pltpu.make_async_copy(smalls.at[source], smalls.at[source], small_recv.at[source]).wait()
+        return carry
+
+    def tok_in(i, carry):
+        block = rows_of(xv, other * half + i)
+        pltpu.make_async_copy(block, block, tok_sib.at[i]).wait()
+        return carry
+
+    lax.fori_loop(0, half, relay, 0)
+    lax.fori_loop(0, half, tok_in, 0)
+    lax.fori_loop(0, CHIPS, first_in, 0)
+    for n in range(4):
+        pltpu.make_async_copy(first_own(n), first_region(n, core, chip), own_sem.at[n]).wait()
+    lax.fori_loop(1, 2 * CHIPS, small_in, 0)
+    own_small.wait()
+    norms, share = ln_in.shape
+    lnv[...] = jnp.zeros_like(lnv)
+    lnv[0:norms, :] = jnp.concatenate([smalls[device, 0:norms, 0:share] for device in range(2 * CHIPS)], 1)
+    counted = smalls[chip // half * CHIPS, 4:5, :]
+    length = jnp.sum(jnp.where(lane == chip % half, counted, 0.0), axis=1, keepdims=True)
+    at_row = lax.broadcasted_iota(jnp.int32, biasv.shape, 0).astype(F32)
+    biasv[...] = jnp.where(at_row < length, 0.0, masked_score)
+    at_lane = lax.broadcasted_iota(jnp.int32, rowv.shape, 1).astype(F32)
+    rowv[...] = jnp.where(at_lane < length, 0.0, masked_score)
+    outs = [pltpu.make_async_copy(source, target, out_sem.at[n]) for n, (source, target) in enumerate((
+        (xv, x_all), (wv, w_first), (lnv, ln_out), (cosv, cos_out), (sinv, sin_out), (biasv, bias_out),
+        (qv, q_out), (kv, k_out), (vv, v_out), (attv, att_out)))]
+    for copy in outs[:6]:
+        copy.start()
+
+    mine = pl.ds(pl.multiple_of(core * rows, rows), rows)
+    blocks = width // LANES
+    per = 3 * blocks // 2
+
+    def weights(block):
+        return jnp.concatenate([wv[b // per, :, pl.ds(pl.multiple_of(b % per * LANES, LANES), LANES)] for b in (block, block + 1)], 1)
+
+    def turned(u, cos, sin):
+        return u * jnp.concatenate([cos, cos], 1) + turn(u) * jnp.concatenate([sin, sin], 1)
+
+    per_group = (GROUP // LANES) * (rows // CHUNK)
+    chunks = width // GROUP * per_group
+
+    def chunk(index, carry):
+        group, inner = index // per_group, index % per_group
+        cols = pl.ds(pl.multiple_of(group * GROUP, GROUP), GROUP)
+
+        @pl.when(inner == 0)
+        def _():
+            q = turned(nn(xv[mine, :], weights(2 * group)), cosv[mine, :], sinv[mine, :]).astype(LOW)
+            qv[:, cols] = q * jnp.asarray(0.125, LOW)
+            kv[:, cols] = turned(nn(xv[...], weights(blocks + 2 * group)), cosv[...], sinv[...]).astype(LOW)
+            vv[:, cols] = nn(xv[...], weights(2 * blocks + 2 * group)).astype(LOW)
+
+        pair, block = inner // (rows // CHUNK), inner % (rows // CHUNK)
+        here = pl.ds(pl.multiple_of(block * CHUNK, CHUNK), CHUNK)
+        lanes = pl.ds(pl.multiple_of(group * GROUP + pair * LANES, LANES), LANES)
+        qp, kp, vp = qv[here, lanes], kv[:, lanes], vv[:, lanes]
+        low = lane_of(qp.shape) < HEAD
+        parts = []
+        for head in range(2):
+            qm = jnp.where(low if head == 0 else jnp.logical_not(low), qp, jnp.zeros_like(qp))
+            s = nt(qm, kp) + rowv[0:1, :]
+            p = jnp.exp(s - jnp.max(s, axis=1, keepdims=True))
+            total = jnp.sum(p, axis=1, keepdims=True)
+            parts.append(nn(p.astype(LOW), vp) / total)
+        attv[here, lanes] = jnp.where(low, parts[0], parts[1]).astype(LOW)
+
+        for k in range(chunks):
+            @pl.when(index == k)
+            def _():
+                for j in range(half):
+                    if k == COTS_AT[j]:
+                        deliver(j, cot, rows_of(c_own, chip % half), tok_send.at[1], cot_recv)
+                if waiting:
+                    arrive(rest_piece, REST_ORDERS, waiting.pop(0))
+        return carry
+
+    lax.fori_loop(0, chunks, chunk, 0)
+    for copy in outs[6:]:
+        copy.start()
+    while waiting:
+        arrive(rest_piece, REST_ORDERS, waiting.pop(0))
+
+    def ends(i, carry):
+        block = rows_of(c_own, i)
+        pltpu.make_async_copy(block, block, cot_recv.at[i]).wait()
+        block = rows_of(xv, core * half + i)
+        pltpu.make_async_copy(block, block, tok_send.at[2, i]).wait()
+        self_copy = (chip // half == core) & (core * half + i == chip)
+
+        @pl.when(jnp.logical_not(self_copy))
+        def _():
+            pltpu.make_async_copy(tok.at[i], tok.at[i], tok_send.at[0, i]).wait()
+            pltpu.make_async_copy(cot.at[i], cot.at[i], tok_send.at[1, i]).wait()
+        return carry
+
+    def rest_in(source, carry):
+        for m in range(3):
+            block = rest_region(m, other, source)
+            pltpu.make_async_copy(block, block, rest_sib.at[m, source]).wait()
+        return carry
+
+    lax.fori_loop(1, 2 * CHIPS, lambda s, c: (small_to(s).wait_send(), c)[1], 0)
+    lax.fori_loop(0, half, ends, 0)
+    drain(first_piece, FIRST_ORDERS)
+    drain(rest_piece, REST_ORDERS)
+    lax.fori_loop(0, CHIPS, rest_in, 0)
+    for m in range(3):
+        pltpu.make_async_copy(shards[m], rest_region(m, core, chip), own_sem.at[4 + m]).wait()
+    for copy in outs:
+        copy.wait()
+
+
+def front(tokens, cotangent, w_qkv, w_out, w_gate, w_up, w_down, ln_params, lengths, turns_far, turns_near):
+    slots, span, width = tokens.shape
+    total, rows = span * CHIPS, span * CHIPS // 2
+    sds, mem, dma = jax.ShapeDtypeStruct, pltpu.VMEM, pltpu.SemaphoreType.DMA
+    anywhere, vmem, smem = (pl.BlockSpec(memory_space=s) for s in (pl.ANY, pltpu.VMEM, pltpu.SMEM))
+    wide = lambda w: sds((2, w.shape[0] * CHIPS, w.shape[1]), LOW)
+    first = (2, width, w_qkv.shape[1] + w_out.shape[1])
+    table, small = (total, LANES), (8, LANES)
+    outs = [sds((total, width), LOW), sds((rows, width), LOW), sds((8, width), F32), sds(first, LOW),
+            wide(w_gate), wide(w_up), wide(w_down), sds((rows, width), LOW), sds((total, width), LOW), sds((total, width), LOW),
+            sds((rows, width), LOW), sds(table, F32), sds(table, F32), sds(table, F32)]
+    return pl.pallas_call(
+        front_kernel,
+        out_shape=outs,
+        in_specs=[anywhere] * 7 + [vmem, smem, vmem, vmem],
+        out_specs=[anywhere] * len(outs),
+        scratch_shapes=[
+            mem((total, width), LOW), mem(first, LOW), mem((rows, width), LOW), mem((total, width), LOW), mem((total, width), LOW),
+            mem((rows, width), LOW), mem(table, F32), mem(table, F32), mem(table, F32), mem((8, total), F32), mem(small, F32),
+            mem((2 * CHIPS,) + small, F32), mem((8, width), F32),
+            dma((4, 5, CHIPS)), dma((4, CHIPS)), dma((4, CHIPS)), dma((3, 5, CHIPS)), dma((3, CHIPS)), dma((3, CHIPS)), dma((7,)),
+            dma((3, 8)), dma((8,)), dma((8,)), dma((8,)), dma((2 * CHIPS,)), dma((2 * CHIPS,)), dma((10,))],
+        compiler_params=pltpu.CompilerParams(collective_id=0, has_side_effects=True, vmem_limit_bytes=60 << 20),
+        name="front",
+    )(tokens, cotangent, w_qkv, w_out, w_gate, w_up, w_down, ln_params, lengths, turns_far, turns_near)
 
 BACK_ORDERS = ("xzy", "zyx", "zyx")
 LATE_ORDERS = ("zxy", "zyx", "zxy")
@@ -1157,39 +1267,28 @@
     )(y_own, dwg, dwu, dwd, dwo, dsmall, x, w, q, k, v, g_att, g_res1, cos, sin, bias_col)
 
 
-def rotary_lanes(tokens):
+def rotary_turns(tokens, near):
     lane = jnp.arange(LANES)
-    pair_index = (lane % (HEAD // 2)).astype(F32)
-    inverse = jnp.power(jnp.float32(1000.0), -2.0 * pair_index / HEAD)
-    angles = jnp.arange(tokens).astype(F32)[:, None] * inverse[None, :]
-    sign = jnp.where(lane % HEAD < HEAD // 2, -1.0, 1.0).astype(F32)
-    return jnp.cos(angles), jnp.sin(angles) * sign[None, :]
+    inverse = jnp.power(jnp.float32(1000.0), -2.0 * (lane % (HEAD // 2)).astype(F32) / HEAD)
+
+    def table(positions):
+        angles = positions.astype(F32)[:, None] * inverse[None, :]
+        return jnp.stack([jnp.cos(angles), jnp.sin(angles)])
+
+    return table(jnp.arange(0, tokens, near)), table(jnp.arange(near))
 
 
 def local_by_slot(tokens, lengths, w_qkv, w_out, w_gate, w_up, w_down, ln_params, cotangent):
     slots, span, width = tokens.shape
-    core, chip = lax.axis_index("dp"), lax.axis_index("seq")
-    half = CHIPS // 2
-    small = jnp.zeros((8, LANES), F32)
     share = ln_params.shape[1]
-    small = small.at[:4, :share].set(ln_params.astype(F32)).at[4, :slots].set(lengths.astype(F32))
-    x, cot, smalls, w_in, wg, wu, wd = gather(tokens, cotangent, small, [jnp.concatenate([w_qkv, w_out], 1), w_gate, w_up, w_down])
-    total, rows = x.shape[0], x.shape[0] // 2
-    ln = jnp.pad(smalls[:, :4, :share].transpose(1, 0, 2).reshape(4, width), ((0, 4), (0, 0)))
-    length = lax.dynamic_slice(smalls, (chip // half * CHIPS, 4, chip % half), (1, 1, 1)).reshape(()).astype(jnp.int32)
-    cos, sin = rotary_lanes(total)
-    position = jnp.arange(total)
-    out_of = jnp.where(position < length, 0.0, masked_score).astype(F32)
-    bias = jnp.broadcast_to(out_of[None, :], (8, total))
-    bias_col = jnp.broadcast_to(out_of[:, None], (total, LANES))
-    valid = jnp.broadcast_to((core * rows + jnp.arange(rows) < length).astype(F32)[:, None], (rows, LANES))
-    q, k, v, att = attend(x, w_in, cos, sin, bias)
-    x_own = lax.dynamic_slice_in_dim(x, core * rows, rows, 0)
-    y, dwg, dwu, dwd, dwo, g_att, g_res1, dln = middle(x_own, att, w_in, wg, wu, wd, cot, ln, valid)
+    turns_far, turns_near = rotary_turns(span * CHIPS, span)
+    x, cot, ln, w_in, wg, wu, wd, q, k, v, att, cos, sin, bias_col = front(
+        tokens, cotangent, w_qkv, w_out, w_gate, w_up, w_down, ln_params, lengths, turns_far, turns_near)
+    y, dwg, dwu, dwd, dwo, g_att, g_res1, dln = middle(x, att, w_in, wg, wu, wd, cot, ln, bias_col)
     dsmall = dln[:4].reshape(4, 2 * CHIPS, share).transpose(1, 0, 2)
     dsmall = jnp.pad(dsmall, ((0, 0), (0, 4), (0, LANES - share)))
-    output, grad_tokens, d_gate, d_up, d_down, d_out, d_qkv, d_small = back_scatter(
-        y, dwg, dwu, dwd, dwo, dsmall, x, w_in, q, k, v, g_att, g_res1, cos, sin, bias_col)
+    output, grad_tokens, d_gate, d_up, d_down, d_out, d_qkv, d_small = finish(back_scatter(
+        y, dwg, dwu, dwd, dwo, dsmall, x, w_in, q, k, v, g_att, g_res1, cos, sin, bias_col))
     return (output, grad_tokens, d_qkv, d_out, d_gate, d_up, d_down, d_small[:4, :share])
 
 

time: 310 us -> 277 us (0.89)
  local copies, waits for them, and re-layouts: 19 us -> 2.81 us
  Pallas kernels: 281 us -> 272 us
  other arithmetic: 8.58 us -> 1.57 us
    unnamed x15 -> x0, local copies, waits for them, and re-layouts: 12 us -> none
    pallas_call x2, Pallas kernels: 126 us -> 116 us  [the longest x1 113 us: front(): pl.pallas_call(front_kernel, out_shape=outs, in_specs=[anywhere] * 7 + [v...]
where the time goes in v3:
time: 277 us
  Pallas kernels  272 us (98%)
  local copies, waits for them, and re-layouts  2.81 us (1%)
    pallas_call x1, Pallas kernels, back_scatter(): pl.pallas_call(back_scatter_kernel, out_shape=[out8, out8] + finals, in_s...  115 us
    pallas_call x1, Pallas kernels, front(): pl.pallas_call(front_kernel, out_shape=outs, in_specs=[anywhere] * 7 + [v...  113 us
    pallas_call x1, Pallas kernels, middle(): pl.pallas_call(functools.partial(middle_kernel, tiles), grid=(2 * tiles,)...  40.3 us

profile of v3, /device:TPU:0, one launch (start us, length us, event | category | flops | bytes accessed | tf_op | source)
XLA Modules:
  0.0 276.6 jit_solution(10309170301106625950)
XLA Ops:
  0.7 0.1 multiply_cosine_fusion.1
  0.8 0.6 pad_maximum_fusion.1.turns_far
  1.4 0.2 multiply_cosine_fusion
  1.6 0.6 pad_maximum_fusion.turns_near
  2.2 113.4 %front.1 = (bf16[1024,768]{1,0:T(8,128)(2,1)}, bf16[512,768]{1,0:T(8,128)(2,1)}, f32[8,768]{1,0:T(8,128)}, bf16[2,768,1536]{2,1,0:T(8,128)(2,1)}, bf16[2,768,153...) custom-call(bf16[8,64,768]{2,1,0:T(8,128)(2,1)} %tok.1, ...), custom_call_target="tpu_custom_call" | custom-call | tf_op jit(solution)/shard_map/front/pallas_call | solution.py:845
  115.6 40.3 %middle.1 = (bf16[512,768]{1,0:T(8,128)(2,1)}, bf16[2,768,1536]{2,1,0:T(8,128)(2,1)}, bf16[2,768,1536]{2,1,0:T(8,128)(2,1)}, bf16[2,3072,384]{2,1,0:T(8,128)(2,1...) custom-call(bf16[1024,768]{1,0:T(8,128)(2,1)} %get-tuple-element.46.x_ref.x_, ...), custom_call_target="tpu_custom_call" | custom-call | flops 24000000000 | bytes 60000000 | tf_op jit(solution)/shard_map/middle/pallas_call | solution.py:521
  155.9 0.7 slice.6
  156.6 0.1 reshape.218
  156.8 0.7 pad.4.dsmall
  157.5 115.1 %back_scatter.1 = (bf16[8,64,768]{2,1,0:T(8,128)(2,1)}, bf16[8,64,768]{2,1,0:T(8,128)(2,1)}, f32[48,1536]{1,0:T(8,128)}, f32[48,1536]{1,0:T(8,128)}, f32[192,384...) custom-call(bf16[512,768]{1,0:T(8,128)(2,1)} %get-tuple-element.55.y_own, ...), custom_call_target="tpu_custom_call" | custom-call | tf_op jit(solution)/shard_map/back_scatter/pallas_call | solution.py:1259
  272.6 2.8 %finish.1 = (bf16[8,64,768]{2,1,0:T(8,128)(2,1)}, bf16[8,64,768]{2,1,0:T(8,128)(2,1)}, f32[48,1536]{1,0:T(8,128)}, f32[48,1536]{1,0:T(8,128)}, f32[192,384]{1,0:...) custom-call(bf16[8,64,768]{2,1,0:T(8,128)(2,1)} %get-tuple-element.68.refs_0_, ...), custom_call_target="tpu_custom_call" | custom-call | tf_op jit(solution)/shard_map/finish/pallas_call | solution.py:551
  275.4 1.3 slice.7
  (4 shorter events, 0.1 us)

commit v4 on v3

--- a/solution.py
+++ b/solution.py
@@ -357,16 +357,8 @@
 
 
 def meet_all(core, chip):
-    barrier = pltpu.get_barrier_semaphore()
-    me = core * CHIPS + chip
-
-    def greet(step, carry):
-        other = (me + step) % (2 * CHIPS)
-        pl.semaphore_signal(barrier, inc=1, device_id={"dp": other // CHIPS, "seq": other % CHIPS}, device_id_type=MESH)
-        return carry
-
-    lax.fori_loop(1, 2 * CHIPS, greet, 0)
-    pl.semaphore_wait(barrier, 2 * CHIPS - 1)
+    greet_all(core, chip)
+    all_here()
 
 
 def onward(order, dx, dy, dz):
@@ -388,6 +380,71 @@
         pl.when(condition)(action)
 
 
+def to_slot(core, chip, j, source, target, sends, recvs):
+    half = CHIPS // 2
+    slot = (chip + 1 + j) % half
+    to = core * half + slot
+    src = source.at[slot]
+    self_copy = (chip // half == core) & (to == chip)
+
+    @pl.when(self_copy)
+    def _():
+        pltpu.make_async_copy(src, target, recvs.at[chip % half]).start()
+
+    @pl.when(jnp.logical_not(self_copy))
+    def _():
+        pltpu.make_async_remote_copy(
+            src_ref=src, dst_ref=target, send_sem=sends.at[slot], recv_sem=recvs.at[chip % half],
+            device_id={"dp": chip // half, "seq": to}, device_id_type=MESH).start()
+
+
+def from_slot(core, chip, j, source, target, sends, recvs):
+    half = CHIPS // 2
+    i = (chip + 1 + j) % half
+    to_core, to_chip = chip // half, core * half + i
+    span = target.shape[1]
+    src, dst = source.at[pl.ds(pl.multiple_of(i * span, span), span)], target.at[chip % half]
+    self_copy = (to_core == core) & (to_chip == chip)
+
+    @pl.when(self_copy)
+    def _():
+        pltpu.make_async_copy(src, dst, recvs.at[chip % half]).start()
+
+    @pl.when(jnp.logical_not(self_copy))
+    def _():
+        pltpu.make_async_remote_copy(
+            src_ref=src, dst_ref=dst, send_sem=sends.at[i], recv_sem=recvs.at[chip % half],
+            device_id={"dp": to_core, "seq": to_chip}, device_id_type=MESH).start()
+
+
+def sent_blocks(core, chip, part, sends):
+    half = CHIPS // 2
+
+    def one(i, carry):
+        @pl.when(jnp.logical_not((chip // half == core) & (core * half + i == chip)))
+        def _():
+            pltpu.make_async_copy(part, part, sends.at[i]).wait()
+        return carry
+
+    lax.fori_loop(0, half, one, 0)
+
+
+def greet_all(core, chip):
+    barrier = pltpu.get_barrier_semaphore()
+    me = core * CHIPS + chip
+
+    def greet(step, carry):
+        other = (me + step) % (2 * CHIPS)
+        pl.semaphore_signal(barrier, inc=1, device_id={"dp": other // CHIPS, "seq": other % CHIPS}, device_id_type=MESH)
+        return carry
+
+    lax.fori_loop(1, 2 * CHIPS, greet, 0)
+
+
+def all_here():
+    pl.semaphore_wait(pltpu.get_barrier_semaphore(), 2 * CHIPS - 1)
+
+
 LOW, F32 = jnp.bfloat16, jnp.float32
 EPS = 1e-12
 HEAD = 64
@@ -432,19 +489,22 @@
 
 
 def middle_kernel(tiles, x_ref, att_ref, wo_ref, wg_ref, wu_ref, wd_ref, cot_ref, ln_ref, bias_ref,
-                  y_ref, dwg_ref, dwu_ref, dwd_ref, dwo_ref, gatt_ref, gres_ref, dln_ref,
-                  n1_ref, inv1_ref, hid_ref, hidt_ref, gate_ref, up_ref, acc_ref, gb_ref):
+                  y_out, dwg_ref, dwu_ref, dwd_ref, dwo_ref, gatt_ref, gres_ref, dln_ref,
+                  n1_ref, inv1_ref, hid_ref, hidt_ref, gate_ref, up_ref, acc_ref, gb_ref, y_ref, y_send, y_recv):
     index = pl.program_id(0)
     width = x_ref.shape[1]
     half = width // 2
     rows = att_ref.shape[0]
-    mine = pl.ds(pl.multiple_of(lax.axis_index("dp") * rows, rows), rows)
+    core, chip = lax.axis_index("dp"), lax.axis_index("seq")
+    mine = pl.ds(pl.multiple_of(core * rows, rows), rows)
+    eighth = CHIPS // 2
 
     def wide(ref):
         return jnp.concatenate([ref[0], ref[1]], 1)
 
     @pl.when(index == 0)
     def _():
+        greet_all(core, chip)
         n1, inv1 = ln_parts(x_ref[mine, :].astype(F32) + nn(att_ref[...], wide(wo_ref)))
         hidden = n1 * ln_ref[0:1, :] + ln_ref[1:2, :]
         n1_ref[...] = n1
@@ -468,8 +528,11 @@
     @pl.when(index == tiles - 1)
     def _():
         n2, inv2 = ln_parts(acc_ref[...])
+        all_here()
         valid = jnp.where(bias_ref[mine, 0:1] == 0.0, 1.0, 0.0)
         y_ref[...] = ((n2 * ln_ref[2:3, :] + ln_ref[3:4, :]) * valid).astype(LOW)
+        for j in range(eighth):
+            from_slot(core, chip, j, y_ref, y_out, y_send, y_recv)
         g_y = cot_ref[...].astype(F32) * valid
         dln_ref[2:3, :] = jnp.sum(g_y * n2, axis=0, keepdims=True)
         dln_ref[3:4, :] = jnp.sum(g_y, axis=0, keepdims=True)
@@ -505,6 +568,8 @@
         dwo_ref[0] = dwo[:, :half].astype(LOW)
         dwo_ref[1] = dwo[:, half:].astype(LOW)
         gatt_ref[...] = nt(gb1, wide(wo_ref)).astype(LOW)
+        sent_blocks(core, chip, y_out.at[0], y_send)
+        lax.fori_loop(0, eighth, lambda i, carry: (pltpu.make_async_copy(y_out.at[i], y_out.at[i], y_recv.at[i]).wait(), carry)[1], 0)
 
 
 def middle(x, att, wo, wg, wu, wd, cot, ln, bias_col):
@@ -512,6 +577,7 @@
     hidden = wd.shape[1]
     tile = 512
     tiles = hidden // tile
+    anywhere = pl.BlockSpec(memory_space=pl.ANY)
     per = wg.shape[2] // tile
     at = lambda i: jnp.where(i < tiles, i, i - tiles)
     late = lambda i: jnp.maximum(i - tiles, 0)
@@ -520,37 +586,42 @@
     sds = jax.ShapeDtypeStruct
     return pl.pallas_call(
         functools.partial(middle_kernel, tiles), grid=(2 * tiles,),
-        out_shape=[sds((rows, width), LOW), sds(wg.shape, LOW), sds(wu.shape, LOW), sds(wd.shape, LOW), sds((2, width, width // 2), LOW),
+        out_shape=[sds((8, rows // 8, width), LOW), sds(wg.shape, LOW), sds(wu.shape, LOW), sds(wd.shape, LOW), sds((2, width, width // 2), LOW),
                    sds((rows, width), LOW), sds((rows, width), F32), sds((8, width), F32)],
         in_specs=[FULL, FULL, pl.BlockSpec((2, width, width // 2), lambda i: (0, 0, 3)), cols(at), cols(at), rowb(at), FULL, FULL, FULL],
-        out_specs=[FULL, cols(late), cols(late), rowb(late), FULL, FULL, FULL, FULL],
+        out_specs=[anywhere, cols(late), cols(late), rowb(late), FULL, FULL, FULL, FULL],
         scratch_shapes=[pltpu.VMEM((rows, width), F32), pltpu.VMEM((rows, LANES), F32), pltpu.VMEM((rows, width), LOW),
                         pltpu.VMEM((width, rows), LOW), pltpu.VMEM((rows, hidden), F32), pltpu.VMEM((rows, hidden), F32),
-                        pltpu.VMEM((rows, width), F32), pltpu.VMEM((rows, width), LOW)],
-        compiler_params=pltpu.CompilerParams(vmem_limit_bytes=60 << 20),
+                        pltpu.VMEM((rows, width), F32), pltpu.VMEM((rows, width), LOW), pltpu.VMEM((rows, width), LOW)]
+        + [pltpu.SemaphoreType.DMA((8,))] * 2,
+        compiler_params=pltpu.CompilerParams(collective_id=2, has_side_effects=True, vmem_limit_bytes=60 << 20),
         cost_estimate=pl.CostEstimate(flops=24 * 10**9, bytes_accessed=6 * 10**7, transcendentals=3 * 10**6),
         name="middle")(x, att, wo, wg, wu, wd, cot, ln, bias_col)
 
 
-def finish_kernel(count, *refs):
+def finish_kernel(count, share, *refs):
     sources, targets, holds, (in_sem, out_sem) = refs[:count], refs[count:2 * count], refs[2 * count:3 * count], refs[3 * count:]
     loads = [pltpu.make_async_copy(source, hold, in_sem.at[n]) for n, (source, hold) in enumerate(zip(sources, holds))]
-    stores = [pltpu.make_async_copy(hold, target, out_sem.at[n]) for n, (hold, target) in enumerate(zip(holds, targets))]
+    stores = [pltpu.make_async_copy(hold, target, out_sem.at[n]) for n, (hold, target) in enumerate(zip(holds[:-1], targets[:-1]))]
     for load in loads:
         load.start()
-    for load, store in zip(loads, stores):
+    for load, store in zip(loads[:-1], stores):
         load.wait()
         store.start()
+    loads[-1].wait()
+    targets[-1][...] = holds[-1][0:4, 0:share]
     for store in stores:
         store.wait()
 
 
-def finish(results):
+def finish(results, share):
     count = len(results)
     anywhere = pl.BlockSpec(memory_space=pl.ANY)
+    shapes = [jax.ShapeDtypeStruct(r.shape, r.dtype) for r in results]
+    shapes[-1] = jax.ShapeDtypeStruct((4, share), results[-1].dtype)
     return pl.pallas_call(
-        functools.partial(finish_kernel, count), out_shape=[jax.ShapeDtypeStruct(r.shape, r.dtype) for r in results],
-        in_specs=[anywhere] * count, out_specs=[anywhere] * count,
+        functools.partial(finish_kernel, count, share), out_shape=shapes,
+        in_specs=[anywhere] * count, out_specs=[anywhere] * (count - 1) + [FULL],
         scratch_shapes=[pltpu.VMEM(r.shape, r.dtype) for r in results] + [pltpu.SemaphoreType.DMA((count,))] * 2,
         name="finish")(*results)
 
@@ -564,8 +635,8 @@
 
 
 def front_kernel(tok, cot, w_qkv, w_out, w_gate, w_up, w_down, ln_in, len_in, turns_far, turns_near,
-                 x_all, c_own, ln_out, w_first, wide_gate, wide_up, wide_down, q_out, k_out, v_out, att_out, cos_out, sin_out, bias_out, *refs):
-    (xv, wv, qv, kv, vv, attv, cosv, sinv, biasv, rowv, small, smalls, lnv), refs = refs[:13], refs[13:]
+                 x_all, c_own, ln_out, w_first, wide_gate, wide_up, wide_down, q_out, k_out, v_out, att_out, cos_out, sin_out, bias_out, lse_out, *refs):
+    (xv, wv, qv, kv, vv, attv, cosv, sinv, biasv, rowv, small, smalls, lnv, lsev), refs = refs[:14], refs[14:]
     (first_send, first_recv, first_sib, rest_send, rest_recv, rest_sib, own_sem, tok_send, tok_recv, tok_sib, cot_recv,
      small_send, small_recv, out_sem) = refs
     core, chip, x, y, z = place()
@@ -743,7 +814,7 @@
     rowv[...] = jnp.where(at_lane < length, 0.0, masked_score)
     outs = [pltpu.make_async_copy(source, target, out_sem.at[n]) for n, (source, target) in enumerate((
         (xv, x_all), (wv, w_first), (lnv, ln_out), (cosv, cos_out), (sinv, sin_out), (biasv, bias_out),
-        (qv, q_out), (kv, k_out), (vv, v_out), (attv, att_out)))]
+        (qv, q_out), (kv, k_out), (vv, v_out), (attv, att_out), (lsev, lse_out)))]
     for copy in outs[:6]:
         copy.start()
 
@@ -780,8 +851,11 @@
         for head in range(2):
             qm = jnp.where(low if head == 0 else jnp.logical_not(low), qp, jnp.zeros_like(qp))
             s = nt(qm, kp) + rowv[0:1, :]
-            p = jnp.exp(s - jnp.max(s, axis=1, keepdims=True))
+            top = jnp.max(s, axis=1, keepdims=True)
+            p = jnp.exp(s - top)
             total = jnp.sum(p, axis=1, keepdims=True)
+            at_head = pl.ds(2 * (group * (GROUP // LANES) + pair) + head, 1)
+            lsev[at_head, here] = jnp.broadcast_to(top + jnp.log(total), (CHUNK, LANES)).T[0:1, :]
             parts.append(nn(p.astype(LOW), vp) / total)
         attv[here, lanes] = jnp.where(low, parts[0], parts[1]).astype(LOW)
 
@@ -841,7 +915,7 @@
     table, small = (total, LANES), (8, LANES)
     outs = [sds((total, width), LOW), sds((rows, width), LOW), sds((8, width), F32), sds(first, LOW),
             wide(w_gate), wide(w_up), wide(w_down), sds((rows, width), LOW), sds((total, width), LOW), sds((total, width), LOW),
-            sds((rows, width), LOW), sds(table, F32), sds(table, F32), sds(table, F32)]
+            sds((rows, width), LOW), sds(table, F32), sds(table, F32), sds(table, F32), sds((16, rows), F32)]
     return pl.pallas_call(
         front_kernel,
         out_shape=outs,
@@ -850,9 +924,9 @@
         scratch_shapes=[
             mem((total, width), LOW), mem(first, LOW), mem((rows, width), LOW), mem((total, width), LOW), mem((total, width), LOW),
             mem((rows, width), LOW), mem(table, F32), mem(table, F32), mem(table, F32), mem((8, total), F32), mem(small, F32),
-            mem((2 * CHIPS,) + small, F32), mem((8, width), F32),
+            mem((2 * CHIPS,) + small, F32), mem((8, width), F32), mem((16, rows), F32),
             dma((4, 5, CHIPS)), dma((4, CHIPS)), dma((4, CHIPS)), dma((3, 5, CHIPS)), dma((3, CHIPS)), dma((3, CHIPS)), dma((7,)),
-            dma((3, 8)), dma((8,)), dma((8,)), dma((8,)), dma((2 * CHIPS,)), dma((2 * CHIPS,)), dma((10,))],
+            dma((3, 8)), dma((8,)), dma((8,)), dma((8,)), dma((2 * CHIPS,)), dma((2 * CHIPS,)), dma((11,))],
         compiler_params=pltpu.CompilerParams(collective_id=0, has_side_effects=True, vmem_limit_bytes=60 << 20),
         name="front",
     )(tokens, cotangent, w_qkv, w_out, w_gate, w_up, w_down, ln_params, lengths, turns_far, turns_near)
@@ -861,6 +935,16 @@
 LATE_ORDERS = ("zxy", "zyx", "zxy")
 FAR_FIRST = OFFSETS[::-1]
 SIDES = {"x": 2, "y": 2, "z": ZS}
+
+
+def far_first(index):
+    words = [sum((o[0] + 2 * o[1] + 4 * (o[2] + 3)) << (5 * place) for place, o in enumerate(FAR_FIRST[start:start + 6]))
+             for start in range(0, len(FAR_FIRST), 6)]
+    word = jnp.int32(words[0])
+    for place, value in enumerate(words[1:], 1):
+        word = jnp.where(index >= 6 * place, jnp.int32(value), word)
+    code = lax.shift_right_logical(word, 5 * (index % 6)) & 31
+    return code & 1, lax.shift_right_logical(code, 1) & 1, lax.shift_right_logical(code, 2) - 3
 
 
 def landing_slots(order):
@@ -881,21 +965,20 @@
     return index * ZS + z if axis == "z" else index
 
 
-def back_scatter_kernel(y_own, dwg, dwu, dwd, dwo, dsmall, x_in, w_in, q_in, k_in, v_in, g_in, res_in, cos_in, sin_in, bias_in,
-                        y_out, gt_out, f_gate, f_up, f_down, f_out, f_qkv, f_small, *refs):
-    (xv, wv, qv, kv, vv, gv, own_acc, cosv, sinv, biasv, xt, oth_acc, dq, dk, dv, dw), refs = refs[:16], refs[16:]
+def back_scatter_kernel(dwg, dwu, dwd, dwo, dsmall, x_in, w_in, q_in, k_in, v_in, g_in, res_in, cos_in, sin_in, bias_in, att_in, lse_in,
+                        gt_out, f_gate, f_up, f_down, f_out, f_qkv, f_small, *refs):
+    (xv, wv, qv, kv, vv, gv, own_acc, cosv, sinv, biasv, xt, oth_acc, dq, dk, dv, dw, attv, lsev), refs = refs[:18], refs[18:]
     owns, refs = refs[:3], refs[3:]
     sibs, refs = refs[:4], refs[4:]
     down_out, refs = refs[0], refs[1:]
     lands, refs = refs[:24], refs[24:]
     (gt_low, gt_sib, smalls), refs = refs[:3], refs[3:]
     (in_sem, send_sem, recv_sem, sib_send, sib_recv, own_sem, late_send, late_recv, late_sib_send, late_sib_recv,
-     gt_sem, tok_send, y_recv, gt_recv, small_send, small_recv) = refs
+     gt_sem, tok_send, gt_recv, small_send, small_recv) = refs
     core, chip, x, y, z = place()
     other = 1 - core
     half = CHIPS // 2
     me = core * CHIPS + chip
-    span = y_out.shape[1]
     rows = qv.shape[0]
     mine = pl.ds(pl.multiple_of(core * rows, rows), rows)
     theirs = pl.ds(pl.multiple_of(other * rows, rows), rows)
@@ -908,7 +991,7 @@
     sibling = {"dp": other, "seq": chip}
 
     loads = [pltpu.make_async_copy(source, target, in_sem.at[n]) for n, (source, target) in enumerate((
-        (k_in, kv), (q_in, qv), (bias_in, biasv), (v_in, vv), (g_in, gv), (x_in, xv), (w_in, wv), (res_in, own_acc), (cos_in, cosv), (sin_in, sinv)))]
+        (k_in, kv), (q_in, qv), (bias_in, biasv), (v_in, vv), (g_in, gv), (att_in, attv), (lse_in, lsev), (x_in, xv), (w_in, wv), (res_in, own_acc), (cos_in, cosv), (sin_in, sinv)))]
     for load in loads:
         load.start()
 
@@ -935,9 +1018,7 @@
                 for n, (source, start, size) in enumerate(parts(m, core, dest))]
 
     def dest_of(index):
-        dx = pick(index, [o[0] for o in FAR_FIRST])
-        dy = pick(index, [o[1] for o in FAR_FIRST])
-        dz = pick(index, [o[2] for o in FAR_FIRST])
+        dx, dy, dz = far_first(index)
         return dx, dy, dz, (z + dz >= 0) & (z + dz < ZS), (x + dx) % 2, (y + dy) % 2, jnp.clip(z + dz, 0, ZS - 1)
 
     meet_all(core, chip)
@@ -965,26 +1046,6 @@
 
     prefetch(jnp.int32(0))
     prefetch(jnp.int32(1))
-
-    def deliver(source, target, k, recvs):
-        def one(j, carry):
-            i = (chip + 1 + j) % half
-            to_core, to_chip = chip // half, core * half + i
-            src, dst = cut(source, span, i), target.at[chip % half]
-            self_copy = (to_core == core) & (to_chip == chip)
-
-            @pl.when(self_copy)
-            def _():
-                pltpu.make_async_copy(src, dst, recvs.at[chip % half]).start()
-
-            @pl.when(jnp.logical_not(self_copy))
-            def _():
-                pltpu.make_async_remote_copy(
-                    src_ref=src, dst_ref=dst, send_sem=tok_send.at[k, i], recv_sem=recvs.at[chip % half],
-                    device_id={"dp": to_core, "seq": to_chip}, device_id_type=MESH).start()
-            return carry
-
-        lax.fori_loop(0, half, one, 0)
 
     def small_to(step):
         to = (me + step) % (2 * CHIPS)
@@ -992,7 +1053,6 @@
             src_ref=dsmall.at[to], dst_ref=smalls.at[me], send_sem=small_send.at[step], recv_sem=small_recv.at[me],
             device_id={"dp": to // CHIPS, "seq": to % CHIPS}, device_id_type=MESH)
 
-    deliver(y_own, y_out, 0, y_recv)
     lax.fori_loop(1, 2 * CHIPS, lambda s, c: (small_to(s).start(), c)[1], 0)
     own_small = pltpu.make_async_copy(dsmall.at[me], smalls.at[me], small_recv.at[me])
     own_small.start()
@@ -1062,7 +1122,7 @@
     groups = xv.shape[1] // GROUP
     chunks = groups * per_group
     blocks = xv.shape[1] // LANES
-    for load in loads[:5]:
+    for load in loads[:7]:
         load.wait()
 
     def chunk(index):
@@ -1083,10 +1143,11 @@
         qm, gm = jnp.where(keep, qp, jnp.zeros_like(qp)), jnp.where(keep, gp, jnp.zeros_like(gp))
         kp, vp = kv[:, lanes], vv[:, lanes]
         s = nt(kp, qm) + jnp.concatenate([biasv[...]] * (step // LANES), 1)
-        e = jnp.exp(s - jnp.max(s, axis=0, keepdims=True))
-        p = e * (1.0 / jnp.sum(e, axis=0, keepdims=True))
+        p = jnp.exp(s - lsev[pl.ds(2 * (group * (GROUP // LANES) + pair) + head, 1), here])
         dp = nt(vp, gm)
-        delta = jnp.sum(p * dp, axis=0, keepdims=True)
+        shares = gm.astype(F32) * attv[here, lanes].astype(F32)
+        delta = lax.dot_general(jnp.ones((8, LANES), F32), shares, (((1,), (1,)), ((), ())),
+                                precision=lax.Precision.HIGHEST, preferred_element_type=F32)[0:1, :]
         ds = (p * (dp - delta)).astype(LOW)
         dv[:, out_lanes] += nn(p.astype(LOW), gm)
         dk[:, out_lanes] += nn(ds, qm)
@@ -1094,7 +1155,7 @@
 
         @pl.when(index == per_group - 1)
         def _():
-            for load in loads[5:]:
+            for load in loads[7:]:
                 load.wait()
             xt[...] = xv[...].T
             oth_acc[...] = jnp.zeros_like(oth_acc)
@@ -1158,32 +1219,47 @@
                                          device_id=sibling, device_id_type=MESH)
     cross.start()
 
-    def late(index, carry):
-        dx, dy, dz, valid, tx, ty, tz = dest_of(index)
-        last = index == len(FAR_FIRST) - 1
-
-        @pl.when(valid)
-        def _():
+    def late(offset):
+        dx, dy, dz = offset
+        final_step = offset == (0, 0, 0)
+
+        def one():
+            tx, ty, tz = (x + dx) % 2, (y + dy) % 2, z + dz
             dest = chip_at(tx, ty, tz)
             late_to_sibling(dest).wait_recv()
             for n, order in enumerate(LATE_ORDERS):
                 lanes = slice(n * third, n * third + third)
                 acc = sibs[3].at[dest, :, lanes]
-                reduce_piece(order, lands[12 + 4 * n:16 + 4 * n], late_send.at[n, dest], lambda link: late_recv.at[n, link, dest],
-                             lambda: dw[core, pl.ds(pl.multiple_of(dest * rows_gate, rows_gate), rows_gate), lanes],
-                             acc, (dx, dy, dz), (tx, ty, tz), last, f_qkv.at[:, lanes])
-
-        @pl.when((index % 2 == 1) & (mixed + index // 2 < len(FAR_FIRST)))
-        def _():
-            early(mixed + index // 2)
-        return carry
-
-    early_steps = 8
-    lax.fori_loop(0, early_steps, late, 0)
-    cross.wait()
-    gt_low[...] = (own_acc[...] + gt_sib[...].astype(F32)).astype(LOW)
-    deliver(gt_low, gt_out, 1, gt_recv)
-    lax.fori_loop(early_steps, len(FAR_FIRST), late, 0)
+                own = dw[core, pl.ds(pl.multiple_of(dest * rows_gate, rows_gate), rows_gate), lanes]
+                total = f_qkv.at[:, lanes] if final_step else acc
+                total[...] = (acc[...].astype(F32) + own.astype(F32)).astype(total.dtype)
+                for link in onward(order, dx, dy, dz):
+                    land = lands[12 + 4 * n + link].at[landing_index(order, link, tx, ty, tz)]
+
+                    def add():
+                        pltpu.make_async_copy(land, land, late_recv.at[n, link, dest]).wait()
+                        total[...] += land[...].astype(total.dtype)
+                    when({2: z < ZS - 1, 3: z > 0}.get(link, True), add)
+                if not final_step:
+                    link = next({"x": 0, "y": 1, "z": 2 if dz > 0 else 3}[axis] for axis in order[::-1] if {"x": dx, "y": dy, "z": dz}[axis])
+                    there = {0: 0, 1: 1, 2: 3, 3: 2}[link]
+                    pltpu.make_async_remote_copy(
+                        src_ref=acc, dst_ref=lands[12 + 4 * n + there].at[landing_index(order, there, tx, ty, tz)],
+                        send_sem=late_send.at[n, dest], recv_sem=late_recv.at[n, there, dest],
+                        device_id=neighbours[link], device_id_type=MESH).start()
+        when(True if dz == 0 else (z < ZS - dz if dz > 0 else z >= -dz), one)
+
+    early_steps, left = 4, mixed
+    for step_index, offset in enumerate(FAR_FIRST):
+        if step_index == early_steps:
+            cross.wait()
+            gt_low[...] = (own_acc[...] + gt_sib[...].astype(F32)).astype(LOW)
+            for j in range(half):
+                from_slot(core, chip, j, gt_low, gt_out, tok_send, gt_recv)
+        late(offset)
+        if step_index % 2 == 1 and left < len(FAR_FIRST):
+            early(jnp.int32(left))
+            left += 1
     f_down[...] = down_out[0:rows_down, :]
     f_out[...] = down_out[rows_down:rows_down + rows_out, :]
 
@@ -1197,17 +1273,8 @@
     own_small.wait()
     f_small[...] = jnp.sum(smalls[...], axis=0)
 
-    def ends(i, carry):
-        for out, recvs, k in ((y_out, y_recv, 0), (gt_out, gt_recv, 1)):
-            pltpu.make_async_copy(out.at[i], out.at[i], recvs.at[i]).wait()
-            self_copy = (chip // half == core) & (core * half + i == chip)
-
-            @pl.when(jnp.logical_not(self_copy))
-            def _():
-                pltpu.make_async_copy(out.at[i], out.at[i], tok_send.at[k, i]).wait()
-        return carry
-
-    lax.fori_loop(0, half, ends, 0)
+    sent_blocks(core, chip, gt_out.at[0], tok_send)
+    lax.fori_loop(0, half, lambda i, c: (pltpu.make_async_copy(gt_out.at[i], gt_out.at[i], gt_recv.at[i]).wait(), c)[1], 0)
 
     def sent(dest, carry):
         for m in range(3):
@@ -1227,7 +1294,7 @@
     lax.fori_loop(0, CHIPS, sent, 0)
 
 
-def back_scatter(y_own, dwg, dwu, dwd, dwo, dsmall, x, w, q, k, v, g_att, g_res1, cos, sin, bias_col):
+def back_scatter(dwg, dwu, dwd, dwo, dsmall, x, w, q, k, v, g_att, g_res1, cos, sin, bias_col, att, lse):
     tokens, width = x.shape
     rows = tokens // 2
     span = rows // 8
@@ -1244,7 +1311,7 @@
     scratch = [mem((tokens, width), LOW), mem(w.shape, LOW), mem((rows, width), LOW), mem((tokens, width), LOW), mem((tokens, width), LOW),
                mem((rows, width), LOW), mem((rows, width), F32), mem(cos.shape, F32), mem(sin.shape, F32), mem(bias_col.shape, F32),
                mem((width, tokens), LOW), mem((rows, width), F32), mem((rows, GROUP), F32), mem((tokens, GROUP), F32), mem((tokens, GROUP), F32),
-               mem((2, width, c_qkv), LOW)]
+               mem((2, width, c_qkv), LOW), mem((rows, width), LOW), mem(lse.shape, F32)]
     scratch += [mem((3,) + piece, LOW) for piece in pieces]
     scratch += [mem((CHIPS,) + piece, LOW) for piece in pieces] + [mem((CHIPS, n_gate, c_qkv), LOW)]
     scratch += [mem(pieces[2], F32)]
@@ -1254,17 +1321,17 @@
         scratch += [mem((n, n_gate, third), LOW) for n in landing_slots(order)]
     scratch += [mem((rows, width), LOW), mem((rows, width), LOW), mem(dsmall.shape, F32)]
     dma = pltpu.SemaphoreType.DMA
-    scratch += [dma((10,)), dma((3, CHIPS)), dma((3, 4, CHIPS)), dma((4, CHIPS)), dma((4, CHIPS)), dma((4, 3)), dma((3, CHIPS)), dma((3, 4, CHIPS)),
-                dma((CHIPS,)), dma((CHIPS,)), dma((2,)), dma((2, 8)), dma((8,)), dma((8,)), dma((2 * CHIPS,)), dma((2 * CHIPS,))]
+    scratch += [dma((12,)), dma((3, CHIPS)), dma((3, 4, CHIPS)), dma((4, CHIPS)), dma((4, CHIPS)), dma((4, 3)), dma((3, CHIPS)), dma((3, 4, CHIPS)),
+                dma((CHIPS,)), dma((CHIPS,)), dma((2,)), dma((8,)), dma((8,)), dma((2 * CHIPS,)), dma((2 * CHIPS,))]
     return pl.pallas_call(
         back_scatter_kernel,
-        out_shape=[out8, out8] + finals,
-        in_specs=[anywhere] * 16,
-        out_specs=[anywhere] * 2 + [vmem] * len(finals),
+        out_shape=[out8] + finals,
+        in_specs=[anywhere] * 17,
+        out_specs=[anywhere] + [vmem] * len(finals),
         scratch_shapes=scratch,
         compiler_params=pltpu.CompilerParams(collective_id=1, has_side_effects=True, vmem_limit_bytes=67043328),
         name="back_scatter",
-    )(y_own, dwg, dwu, dwd, dwo, dsmall, x, w, q, k, v, g_att, g_res1, cos, sin, bias_col)
+    )(dwg, dwu, dwd, dwo, dsmall, x, w, q, k, v, g_att, g_res1, cos, sin, bias_col, att, lse)
 
 
 def rotary_turns(tokens, near):
@@ -1282,14 +1349,14 @@
     slots, span, width = tokens.shape
     share = ln_params.shape[1]
     turns_far, turns_near = rotary_turns(span * CHIPS, span)
-    x, cot, ln, w_in, wg, wu, wd, q, k, v, att, cos, sin, bias_col = front(
+    x, cot, ln, w_in, wg, wu, wd, q, k, v, att, cos, sin, bias_col, lse = front(
         tokens, cotangent, w_qkv, w_out, w_gate, w_up, w_down, ln_params, lengths, turns_far, turns_near)
     y, dwg, dwu, dwd, dwo, g_att, g_res1, dln = middle(x, att, w_in, wg, wu, wd, cot, ln, bias_col)
     dsmall = dln[:4].reshape(4, 2 * CHIPS, share).transpose(1, 0, 2)
     dsmall = jnp.pad(dsmall, ((0, 0), (0, 4), (0, LANES - share)))
-    output, grad_tokens, d_gate, d_up, d_down, d_out, d_qkv, d_small = finish(back_scatter(
-        y, dwg, dwu, dwd, dwo, dsmall, x, w_in, q, k, v, g_att, g_res1, cos, sin, bias_col))
-    return (output, grad_tokens, d_qkv, d_out, d_gate, d_up, d_down, d_small[:4, :share])
+    results = back_scatter(dwg, dwu, dwd, dwo, dsmall, x, w_in, q, k, v, g_att, g_res1, cos, sin, bias_col, att, lse)
+    output, grad_tokens, d_gate, d_up, d_down, d_out, d_qkv, d_small = finish([y, *results], share)
+    return (output, grad_tokens, d_qkv, d_out, d_gate, d_up, d_down, d_small)
 
 
 def solution(mesh):

time: 277 us -> 273 us (0.986)
  Pallas kernels: 272 us -> 269 us
    pallas_call x2, Pallas kernels: 118 us -> 115 us  [the longest x1 111 us: back_scatter(): pl.pallas_call(back_scatter_kernel, out_shape=[out8] + finals, in_specs=[...]
where the time goes in v4:
time: 273 us
  Pallas kernels  269 us (99%)
    pallas_call x1, Pallas kernels, front(): pl.pallas_call(front_kernel, out_shape=outs, in_specs=[anywhere] * 7 + [v...  114 us
    pallas_call x1, Pallas kernels, back_scatter(): pl.pallas_call(back_scatter_kernel, out_shape=[out8] + finals, in_specs=[...  111 us
    pallas_call x1, Pallas kernels, middle(): pl.pallas_call(functools.partial(middle_kernel, tiles), grid=(2 * tiles,)...  41 us

profile of v4, /device:TPU:0, one launch (start us, length us, event | category | flops | bytes accessed | tf_op | source)
XLA Modules:
  0.0 273.2 jit_solution(13716760491816966681)
XLA Ops:
  0.7 0.1 multiply_cosine_fusion.1
  0.8 0.6 pad_maximum_fusion.1.turns_far
  1.4 0.2 multiply_cosine_fusion
  1.6 0.6 pad_maximum_fusion.turns_near
  2.2 113.5 %front.1 = (bf16[1024,768]{1,0:T(8,128)(2,1)}, bf16[512,768]{1,0:T(8,128)(2,1)}, f32[8,768]{1,0:T(8,128)}, bf16[2,768,1536]{2,1,0:T(8,128)(2,1)}, bf16[2,768,153...) custom-call(bf16[8,64,768]{2,1,0:T(8,128)(2,1)} %tok.1, ...), custom_call_target="tpu_custom_call" | custom-call | tf_op jit(solution)/shard_map/front/pallas_call | solution.py:919
  115.8 41.0 %middle.1 = (bf16[8,64,768]{2,1,0:T(8,128)(2,1)}, bf16[2,768,1536]{2,1,0:T(8,128)(2,1)}, bf16[2,768,1536]{2,1,0:T(8,128)(2,1)}, bf16[2,3072,384]{2,1,0:T(8,128)(...) custom-call(bf16[1024,768]{1,0:T(8,128)(2,1)} %get-tuple-element.46.x_ref, ...), custom_call_target="tpu_custom_call" | custom-call | flops 24000000000 | bytes 60000000 | tf_op jit(solution)/shard_map/middle/pallas_call | solution.py:587
  156.8 0.7 slice.3
  157.6 0.1 reshape.218
  157.7 0.7 pad.4.dsmall
  158.4 111.2 %back_scatter.1 = (bf16[8,64,768]{2,1,0:T(8,128)(2,1)}, f32[48,1536]{1,0:T(8,128)}, f32[48,1536]{1,0:T(8,128)}, f32[192,384]{1,0:T(8,128)}, f32[48,384]{1,0:T(8,...) custom-call(bf16[2,768,1536]{2,1,0:T(8,128)(2,1)} %get-tuple-element.56.dwg, bf16[2,768,1536]{2,1,0:T(8,128)(2,1)} %get-tuple-element.57.dwu, ...), custom_call_target="tpu_custom_call" | custom-call | tf_op jit(solution)/shard_map/back_scatter/pallas_call | solution.py:1326
  269.6 3.4 %finish.1 = (bf16[8,64,768]{2,1,0:T(8,128)(2,1)}, bf16[8,64,768]{2,1,0:T(8,128)(2,1)}, f32[48,1536]{1,0:T(8,128)}, f32[48,1536]{1,0:T(8,128)}, f32[192,384]{1,0:...) custom-call(bf16[8,64,768]{2,1,0:T(8,128)(2,1)} %get-tuple-element.55.refs_0_, ...), custom_call_target="tpu_custom_call" | custom-call | tf_op jit(solution)/shard_map/finish/pallas_call | solution.py:622
  (4 shorter events, 0.1 us)

commit v5 on v4

--- a/solution.py
+++ b/solution.py
@@ -2,6 +2,7 @@
 
 import jax
 import jax.numpy as jnp
+import numpy as np
 from jax import lax
 from jax.experimental import pallas as pl
 from jax.experimental.pallas import tpu as pltpu
@@ -489,8 +490,8 @@
 
 
 def middle_kernel(tiles, x_ref, att_ref, wo_ref, wg_ref, wu_ref, wd_ref, cot_ref, ln_ref, bias_ref,
-                  y_out, dwg_ref, dwu_ref, dwd_ref, dwo_ref, gatt_ref, gres_ref, dln_ref,
-                  n1_ref, inv1_ref, hid_ref, hidt_ref, gate_ref, up_ref, acc_ref, gb_ref, y_ref, y_send, y_recv):
+                  y_out, dwg_ref, dwu_ref, dwd_ref, dwo_ref, gatt_ref, gres_ref, small_ref,
+                  n1_ref, inv1_ref, hid_ref, hidt_ref, gate_ref, up_ref, acc_ref, gb_ref, y_ref, dln_ref, y_send, y_recv):
     index = pl.program_id(0)
     width = x_ref.shape[1]
     half = width // 2
@@ -568,6 +569,10 @@
         dwo_ref[0] = dwo[:, :half].astype(LOW)
         dwo_ref[1] = dwo[:, half:].astype(LOW)
         gatt_ref[...] = nt(gb1, wide(wo_ref)).astype(LOW)
+        small_ref[...] = jnp.zeros_like(small_ref)
+        share = width // (2 * CHIPS)
+        for device in range(2 * CHIPS):
+            small_ref[device, 0:4, 0:share] = dln_ref[0:4, device * share:device * share + share]
         sent_blocks(core, chip, y_out.at[0], y_send)
         lax.fori_loop(0, eighth, lambda i, carry: (pltpu.make_async_copy(y_out.at[i], y_out.at[i], y_recv.at[i]).wait(), carry)[1], 0)
 
@@ -587,12 +592,12 @@
     return pl.pallas_call(
         functools.partial(middle_kernel, tiles), grid=(2 * tiles,),
         out_shape=[sds((8, rows // 8, width), LOW), sds(wg.shape, LOW), sds(wu.shape, LOW), sds(wd.shape, LOW), sds((2, width, width // 2), LOW),
-                   sds((rows, width), LOW), sds((rows, width), F32), sds((8, width), F32)],
+                   sds((rows, width), LOW), sds((rows, width), F32), sds((2 * CHIPS, 8, LANES), F32)],
         in_specs=[FULL, FULL, pl.BlockSpec((2, width, width // 2), lambda i: (0, 0, 3)), cols(at), cols(at), rowb(at), FULL, FULL, FULL],
         out_specs=[anywhere, cols(late), cols(late), rowb(late), FULL, FULL, FULL, FULL],
         scratch_shapes=[pltpu.VMEM((rows, width), F32), pltpu.VMEM((rows, LANES), F32), pltpu.VMEM((rows, width), LOW),
                         pltpu.VMEM((width, rows), LOW), pltpu.VMEM((rows, hidden), F32), pltpu.VMEM((rows, hidden), F32),
-                        pltpu.VMEM((rows, width), F32), pltpu.VMEM((rows, width), LOW), pltpu.VMEM((rows, width), LOW)]
+                        pltpu.VMEM((rows, width), F32), pltpu.VMEM((rows, width), LOW), pltpu.VMEM((rows, width), LOW), pltpu.VMEM((8, width), F32)]
         + [pltpu.SemaphoreType.DMA((8,))] * 2,
         compiler_params=pltpu.CompilerParams(collective_id=2, has_side_effects=True, vmem_limit_bytes=60 << 20),
         cost_estimate=pl.CostEstimate(flops=24 * 10**9, bytes_accessed=6 * 10**7, transcendentals=3 * 10**6),
@@ -1021,41 +1026,7 @@
         dx, dy, dz = far_first(index)
         return dx, dy, dz, (z + dz >= 0) & (z + dz < ZS), (x + dx) % 2, (y + dy) % 2, jnp.clip(z + dz, 0, ZS - 1)
 
-    meet_all(core, chip)
-
-    def begin(index, carry):
-        dx, dy, dz, valid, tx, ty, tz = dest_of(index)
-
-        @pl.when(valid)
-        def _():
-            for m in range(3):
-                for copy in to_sibling(m, chip_at(tx, ty, tz)):
-                    copy.start()
-        return carry
-
-    lax.fori_loop(0, len(FAR_FIRST), begin, 0)
-
-    def prefetch(index):
-        dx, dy, dz, valid, tx, ty, tz = dest_of(index)
-
-        @pl.when(valid & (index < len(FAR_FIRST)))
-        def _():
-            for m in range(3):
-                for copy in own_load(m, chip_at(tx, ty, tz), index % 3):
-                    copy.start()
-
-    prefetch(jnp.int32(0))
-    prefetch(jnp.int32(1))
-
-    def small_to(step):
-        to = (me + step) % (2 * CHIPS)
-        return pltpu.make_async_remote_copy(
-            src_ref=dsmall.at[to], dst_ref=smalls.at[me], send_sem=small_send.at[step], recv_sem=small_recv.at[me],
-            device_id={"dp": to // CHIPS, "seq": to % CHIPS}, device_id_type=MESH)
-
-    lax.fori_loop(1, 2 * CHIPS, lambda s, c: (small_to(s).start(), c)[1], 0)
-    own_small = pltpu.make_async_copy(dsmall.at[me], smalls.at[me], small_recv.at[me])
-    own_small.start()
+    greet_all(core, chip)
 
     def reduce_piece(order, lands_m, send_at, recv_at, own, acc, offset, target, last, final):
         dx, dy, dz = offset
@@ -1190,13 +1161,51 @@
     def turn_of(index, carry):
         chunk(index)
 
-        @pl.when(index < mixed)
-        def _():
-            early(index)
+        @pl.when(index - ahead < mixed)
+        def _():
+            early(index - ahead)
         return carry
 
-    mixed = min(chunks, len(FAR_FIRST) - 4)
-    lax.fori_loop(0, chunks, turn_of, 0)
+    ahead = 1
+    lax.fori_loop(0, ahead, lambda index, c: (chunk(index), c)[1], 0)
+    all_here()
+
+    def begin(index, carry):
+        dx, dy, dz, valid, tx, ty, tz = dest_of(index)
+
+        @pl.when(valid)
+        def _():
+            for m in range(3):
+                for copy in to_sibling(m, chip_at(tx, ty, tz)):
+                    copy.start()
+        return carry
+
+    lax.fori_loop(0, len(FAR_FIRST), begin, 0)
+
+    def prefetch(index):
+        dx, dy, dz, valid, tx, ty, tz = dest_of(index)
+
+        @pl.when(valid & (index < len(FAR_FIRST)))
+        def _():
+            for m in range(3):
+                for copy in own_load(m, chip_at(tx, ty, tz), index % 3):
+                    copy.start()
+
+    prefetch(jnp.int32(0))
+    prefetch(jnp.int32(1))
+
+    def small_to(step):
+        to = (me + step) % (2 * CHIPS)
+        return pltpu.make_async_remote_copy(
+            src_ref=dsmall.at[to], dst_ref=smalls.at[me], send_sem=small_send.at[step], recv_sem=small_recv.at[me],
+            device_id={"dp": to // CHIPS, "seq": to % CHIPS}, device_id_type=MESH)
+
+    lax.fori_loop(1, 2 * CHIPS, lambda s, c: (small_to(s).start(), c)[1], 0)
+    own_small = pltpu.make_async_copy(dsmall.at[me], smalls.at[me], small_recv.at[me])
+    own_small.start()
+
+    mixed = min(chunks - ahead, len(FAR_FIRST) - 4)
+    lax.fori_loop(ahead, chunks, turn_of, 0)
 
     gt_low[...] = oth_acc[...].astype(LOW)
     third = f_qkv.shape[1] // len(LATE_ORDERS)
@@ -1335,14 +1344,14 @@
 
 
 def rotary_turns(tokens, near):
-    lane = jnp.arange(LANES)
-    inverse = jnp.power(jnp.float32(1000.0), -2.0 * (lane % (HEAD // 2)).astype(F32) / HEAD)
+    pair_index = (np.arange(LANES) % (HEAD // 2)).astype(np.float32)
+    inverse = np.power(np.float32(1000.0), np.float32(-2.0) * pair_index / np.float32(HEAD))
 
     def table(positions):
-        angles = positions.astype(F32)[:, None] * inverse[None, :]
-        return jnp.stack([jnp.cos(angles), jnp.sin(angles)])
-
-    return table(jnp.arange(0, tokens, near)), table(jnp.arange(near))
+        angles = positions.astype(np.float32)[:, None] * inverse[None, :]
+        return jnp.asarray(np.stack([np.cos(angles), np.sin(angles)]), F32)
+
+    return table(np.arange(0, tokens, near)), table(np.arange(near))
 
 
 def local_by_slot(tokens, lengths, w_qkv, w_out, w_gate, w_up, w_down, ln_params, cotangent):
@@ -1351,9 +1360,7 @@
     turns_far, turns_near = rotary_turns(span * CHIPS, span)
     x, cot, ln, w_in, wg, wu, wd, q, k, v, att, cos, sin, bias_col, lse = front(
         tokens, cotangent, w_qkv, w_out, w_gate, w_up, w_down, ln_params, lengths, turns_far, turns_near)
-    y, dwg, dwu, dwd, dwo, g_att, g_res1, dln = middle(x, att, w_in, wg, wu, wd, cot, ln, bias_col)
-    dsmall = dln[:4].reshape(4, 2 * CHIPS, share).transpose(1, 0, 2)
-    dsmall = jnp.pad(dsmall, ((0, 0), (0, 4), (0, LANES - share)))
+    y, dwg, dwu, dwd, dwo, g_att, g_res1, dsmall = middle(x, att, w_in, wg, wu, wd, cot, ln, bias_col)
     results = back_scatter(dwg, dwu, dwd, dwo, dsmall, x, w_in, q, k, v, g_att, g_res1, cos, sin, bias_col, att, lse)
     output, grad_tokens, d_gate, d_up, d_down, d_out, d_qkv, d_small = finish([y, *results], share)
     return (output, grad_tokens, d_qkv, d_out, d_gate, d_up, d_down, d_small)

time: 273 us -> 269 us (0.985)
  no operation moved by 1% of the time
where the time goes in v5:
time: 269 us; the launch traced here: 268 us
  Pallas kernels  268 us (100%)
    pallas_call x1, Pallas kernels, front(): pl.pallas_call(front_kernel, out_shape=outs, in_specs=[anywhere] * 7 + [v...  114 us
    pallas_call x1, Pallas kernels, back_scatter(): pl.pallas_call(back_scatter_kernel, out_shape=[out8] + finals, in_specs=[...  109 us
    pallas_call x1, Pallas kernels, middle(): pl.pallas_call(functools.partial(middle_kernel, tiles), grid=(2 * tiles,)...  41.1 us

profile of v5, /device:TPU:0, one launch (start us, length us, event | category | flops | bytes accessed | tf_op | source)
XLA Modules:
  0.0 268.4 jit_solution(11743339747406389751)
XLA Ops:
  0.6 113.6 %front.1 = (bf16[1024,768]{1,0:T(8,128)(2,1)}, bf16[512,768]{1,0:T(8,128)(2,1)}, f32[8,768]{1,0:T(8,128)}, bf16[2,768,1536]{2,1,0:T(8,128)(2,1)}, bf16[2,768,153...) custom-call(bf16[8,64,768]{2,1,0:T(8,128)(2,1)} %tok.1, ...), custom_call_target="tpu_custom_call" | custom-call | tf_op jit(solution)/shard_map/front/pallas_call | solution.py:924
  114.2 41.1 %middle.1 = (bf16[8,64,768]{2,1,0:T(8,128)(2,1)}, bf16[2,768,1536]{2,1,0:T(8,128)(2,1)}, bf16[2,768,1536]{2,1,0:T(8,128)(2,1)}, bf16[2,3072,384]{2,1,0:T(8,128)(...) custom-call(bf16[1024,768]{1,0:T(8,128)(2,1)} %get-tuple-element.46., ...), custom_call_target="tpu_custom_call" | custom-call | flops 24000000000 | bytes 60000000 | tf_op jit(solution)/shard_map/middle/pallas_call | solution.py:592
  155.4 109.5 %back_scatter.1 = (bf16[8,64,768]{2,1,0:T(8,128)(2,1)}, f32[48,1536]{1,0:T(8,128)}, f32[48,1536]{1,0:T(8,128)}, f32[192,384]{1,0:T(8,128)}, f32[48,384]{1,0:T(8,...) custom-call(bf16[2,768,1536]{2,1,0:T(8,128)(2,1)} %get-tuple-element.56.dwg, bf16[2,768,1536]{2,1,0:T(8,128)(2,1)} %get-tuple-element.57.dwu, ...), custom_call_target="tpu_custom_call" | custom-call | tf_op jit(solution)/shard_map/back_scatter/pallas_call | solution.py:1335
  264.8 3.4 %finish.1 = (bf16[8,64,768]{2,1,0:T(8,128)(2,1)}, bf16[8,64,768]{2,1,0:T(8,128)(2,1)}, f32[48,1536]{1,0:T(8,128)}, f32[48,1536]{1,0:T(8,128)}, f32[192,384]{1,0:...) custom-call(bf16[8,64,768]{2,1,0:T(8,128)(2,1)} %get-tuple-element.55.refs_0_, ...), custom_call_target="tpu_custom_call" | custom-call | tf_op jit(solution)/shard_map/finish/pallas_call | solution.py:627

commit v6 on v5

--- a/solution.py
+++ b/solution.py
@@ -1258,7 +1258,7 @@
                         device_id=neighbours[link], device_id_type=MESH).start()
         when(True if dz == 0 else (z < ZS - dz if dz > 0 else z >= -dz), one)
 
-    early_steps, left = 4, mixed
+    early_steps, left = 8, mixed
     for step_index, offset in enumerate(FAR_FIRST):
         if step_index == early_steps:
             cross.wait()

time: 269 us -> 267 us (level)
  no operation moved by 1% of the time
where the time goes in v6:
time: 267 us
  Pallas kernels  266 us (100%)
    pallas_call x1, Pallas kernels, front(): pl.pallas_call(front_kernel, out_shape=outs, in_specs=[anywhere] * 7 + [v...  114 us
    pallas_call x1, Pallas kernels, back_scatter(): pl.pallas_call(back_scatter_kernel, out_shape=[out8] + finals, in_specs=[...  108 us
    pallas_call x1, Pallas kernels, middle(): pl.pallas_call(functools.partial(middle_kernel, tiles), grid=(2 * tiles,)...  41.1 us

profile of v6, /device:TPU:0, one launch (start us, length us, event | category | flops | bytes accessed | tf_op | source)
XLA Modules:
  0.0 267.2 jit_solution(5514376868588449717)
XLA Ops:
  0.6 113.6 %front.1 = (bf16[1024,768]{1,0:T(8,128)(2,1)}, bf16[512,768]{1,0:T(8,128)(2,1)}, f32[8,768]{1,0:T(8,128)}, bf16[2,768,1536]{2,1,0:T(8,128)(2,1)}, bf16[2,768,153...) custom-call(bf16[8,64,768]{2,1,0:T(8,128)(2,1)} %tok.1, ...), custom_call_target="tpu_custom_call" | custom-call | tf_op jit(solution)/shard_map/front/pallas_call | solution.py:924
  114.2 41.1 %middle.1 = (bf16[8,64,768]{2,1,0:T(8,128)(2,1)}, bf16[2,768,1536]{2,1,0:T(8,128)(2,1)}, bf16[2,768,1536]{2,1,0:T(8,128)(2,1)}, bf16[2,3072,384]{2,1,0:T(8,128)(...) custom-call(bf16[1024,768]{1,0:T(8,128)(2,1)} %get-tuple-element.46., ...), custom_call_target="tpu_custom_call" | custom-call | flops 24000000000 | bytes 60000000 | tf_op jit(solution)/shard_map/middle/pallas_call | solution.py:592
  155.4 108.3 %back_scatter.1 = (bf16[8,64,768]{2,1,0:T(8,128)(2,1)}, f32[48,1536]{1,0:T(8,128)}, f32[48,1536]{1,0:T(8,128)}, f32[192,384]{1,0:T(8,128)}, f32[48,384]{1,0:T(8,...) custom-call(bf16[2,768,1536]{2,1,0:T(8,128)(2,1)} %get-tuple-element.56.dwg, bf16[2,768,1536]{2,1,0:T(8,128)(2,1)} %get-tuple-element.57.dwu, ...), custom_call_target="tpu_custom_call" | custom-call | tf_op jit(solution)/shard_map/back_scatter/pallas_call | solution.py:1335
  263.6 3.4 %finish.1 = (bf16[8,64,768]{2,1,0:T(8,128)(2,1)}, bf16[8,64,768]{2,1,0:T(8,128)(2,1)}, f32[48,1536]{1,0:T(8,128)}, f32[48,1536]{1,0:T(8,128)}, f32[192,384]{1,0:...) custom-call(bf16[8,64,768]{2,1,0:T(8,128)(2,1)} %get-tuple-element.55.refs_0_, ...), custom_call_target="tpu_custom_call" | custom-call | tf_op jit(solution)/shard_map/finish/pallas_call | solution.py:627
